TPU v7x, 128 devices: a whole 4x4x4 slice. The times are simulated.
128 devices in a mesh: ga: 16 (over y, x), band: 4 (over z), pool: 2 (over core).
Axes of the slice: x: 4, y: 4, z: 4, core: 2. Of those that a mesh axis runs over, the one named last changes fastest.
Arguments:
- psi_occ: bfloat16 [512, 64, 64, 128], P(('pool', 'band'), 'ga'), parts along dimension 0, may hold values from -9 to 9
- energies: float32 [32], P(('pool', 'band')), parts along dimension 0, may hold values from -0.8 to 0.6
- k_point: float32 [6], P('pool'), parts along dimension 0, may hold values from -0.5 to 0.5, as said below
- g_mask: int32 [128, 4096], P(('pool', 'ga')), parts along dimension 0, may hold values from 0 to 1, as said below
- v_local: float32 [64, 4096], P(None, 'ga'), may hold values from 1 to 4
- dv: float32 [3, 64, 4096], P(None, None, 'ga'), may hold values from -6 to 6
Outputs:
- response: float32 [32, 3, 64, 64, 128], P(('pool', 'band'), None, 'ga'), parts along dimension 0
- residual: float32 [32, 3, 64, 64, 128], P(('pool', 'band'), None, 'ga'), parts along dimension 0
There are 2 independent parts, one for each index of `pool`. A program takes and returns all parts, laid end to end along the dimension named above; an argument that names none is the same for every part. Nothing has to cross between parts.
Inputs may be any that keep to these rules, and one draw needn't show every extreme that they name: `k_point`: each component is a nonzero multiple of 0.25. `g_mask`: 1 exactly where the distance of (f(g1), f(g2), f(g3)) + k_point from the anchor is below 21, with f the signed frequency; so no 1 stands where |f(g2)| > 21 or |f(g3)| > 21, and in every draw some 1 stands where |f(g2)| = 21.
All inputs are finite; a program needn't handle non-finite values.
Results may differ from a plain program's by a relative error of at most 0.0044.
Values may be sent and summed in bfloat16 or wider, within the bound.
A program may use at most 128 MiB of HBM per device.

v0:
```python
import math

import jax
import jax.numpy as jnp
from jax import lax
from jax.sharding import PartitionSpec as P

BOX = 64
GCUT = 21
NPERT = 3
ITERS = 2
STRIDE = 16


cell_length = 16.5
shift_weight = 8.0


def copy_for_each(shard, axis):
    size = lax.axis_size(axis)
    return lax.all_to_all(
        jnp.broadcast_to(shard[None], (size, *shard.shape)), axis, 0, 0, tiled=True
    )


def of_everyone(shard, axis):
    everything = copy_for_each(shard, axis)
    return jnp.sum(everything, axis=0)


def packed_total(arrays, axis):
    ends = [0]
    for a in arrays:
        ends.append(ends[-1] + a.size)
    total = of_everyone(jnp.concatenate([a.ravel() for a in arrays]), axis)
    return tuple((total[b:e].reshape(a.shape) for a, b, e in zip(arrays, ends, ends[1:])))


def quarter_turn(values):
    halfway = values.shape[-1] // 2
    return jnp.concatenate([-values[..., halfway:], values[..., :halfway]], axis=-1)


def minus_turn(values):
    halfway = values.shape[-1] // 2
    return jnp.concatenate([values[..., halfway:], -values[..., :halfway]], axis=-1)


def phase_tables(length, phase_sign):
    indices = jnp.arange(length, dtype=jnp.int32)
    product = indices[:, None] * indices[None, :] % length
    angle = product.astype(jnp.float32) * (2.0 * math.pi / length)
    return (jnp.cos(angle), phase_sign * jnp.sin(angle))


def transform_rows(values, which, phase_sign):
    cosine_table, sine_table = phase_tables(values.shape[which], phase_sign)
    form = "ab,sbyz->sayz" if which == 1 else "ab,sxbz->sxaz"
    first = jnp.einsum(form, cosine_table, values, precision=lax.Precision.HIGHEST)
    second = jnp.einsum(form, sine_table, values, precision=lax.Precision.HIGHEST)
    return first + quarter_turn(second)


def transform_last(values, phase_sign):
    cosine_table, sine_table = phase_tables(values.shape[-1] // 2, phase_sign)
    upper = jnp.concatenate([cosine_table, sine_table], axis=1)
    lower = jnp.concatenate([-sine_table, cosine_table], axis=1)
    matrix = jnp.concatenate([upper, lower], axis=0)
    return jnp.dot(values, matrix, precision=lax.Precision.HIGHEST)


def keep_rows(values):
    return jnp.concatenate([values[:, :, : GCUT + 1], values[:, :, BOX - GCUT :]], axis=2)


def restore_rows(values):
    filler = jnp.zeros(
        (values.shape[0], values.shape[1], BOX - 2 * GCUT - 1, values.shape[3]), values.dtype
    )
    return jnp.concatenate([values[:, :, : GCUT + 1], filler, values[:, :, GCUT + 1 :]], axis=2)


def local_inner(first, second):
    return jnp.sum(first * second, axis=(1, 2, 3)) / BOX**3


def four_sums(direction, image, residual):
    return packed_total(
        (
            local_inner(direction, image),
            local_inner(residual, image),
            local_inner(image, image),
            local_inner(residual, residual),
        ),
        "ga",
    )


def on_device(psi_occ, energies, k_point, g_mask, v_local, dv):
    slab_rows = psi_occ.shape[1]
    row_count = v_local.shape[1] // BOX
    ga_index = lax.axis_index("ga")
    indices = jnp.arange(BOX, dtype=jnp.int32)
    signed = jnp.where(indices < BOX // 2, indices, indices - BOX).astype(jnp.float32)
    owned = ga_index * slab_rows + jnp.arange(slab_rows, dtype=jnp.int32)
    freq_first = jnp.where(owned < BOX // 2, owned, owned - BOX).astype(jnp.float32)
    factor = 0.5 * (2.0 * math.pi / cell_length) ** 2
    kinetic = factor * (
        (freq_first[:, None, None] + k_point[0]) ** 2
        + (signed[None, :, None] + k_point[1]) ** 2
        + (signed[None, None, :] + k_point[2]) ** 2
    )
    kinetic = jnp.concatenate([kinetic, kinetic], axis=-1)
    sphere = g_mask.reshape(slab_rows, BOX, BOX).astype(jnp.float32)
    sphere = jnp.concatenate([sphere, sphere], axis=-1)
    occupied = psi_occ * sphere.astype(jnp.bfloat16)
    solved = occupied[::STRIDE].astype(jnp.float32)
    energy_shift = jnp.repeat(energies, NPERT)[:, None, None, None]
    potential = v_local.reshape(BOX, row_count, BOX)
    potential = jnp.concatenate([potential, potential], axis=-1)
    changes = dv.reshape(NPERT, BOX, row_count, BOX)
    changes = jnp.concatenate([changes, changes], axis=-1)
    occupied_all = lax.all_gather(keep_rows(occupied), "band", axis=0, tiled=True)
    row_kept = 2 * GCUT + 1
    flat_panel = occupied_all.reshape(occupied_all.shape[0], -1)

    def project_occupied(values):
        count = values.shape[0]
        part = keep_rows(values)
        lowered = part.astype(jnp.bfloat16)
        stacked = jnp.concatenate([lowered, minus_turn(lowered)], axis=0).reshape(2 * count, -1)
        partial_value = lax.dot_general(
            flat_panel, stacked, (((1,), (1,)), ((), ())), preferred_element_type=jnp.float32
        )
        correlation = of_everyone(partial_value, "ga")
        low_correlation = correlation.astype(jnp.bfloat16)
        product = lax.dot_general(
            low_correlation,
            flat_panel,
            (((0,), (0,)), ((), ())),
            preferred_element_type=jnp.float32,
        )
        product = product.reshape(2 * count, slab_rows, row_kept, 2 * BOX)
        result = product[:count] + quarter_turn(product[count:])
        result = restore_rows(result)
        return result / BOX**3

    def through_grid(coeffs, on_grid):
        near = transform_rows(transform_last(coeffs, 1.0), 2, 1.0)
        grid_values = transform_rows(
            lax.all_to_all(near, "ga", split_axis=2, concat_axis=1, tiled=True), 1, 1.0
        )
        result = on_grid(grid_values)
        back = transform_rows(result, 1, -1.0)
        moved = lax.all_to_all(back, "ga", split_axis=1, concat_axis=2, tiled=True)
        far = transform_last(transform_rows(moved, 2, -1.0), -1.0)
        return far * (sphere / BOX**3)

    def with_changes(grid_values):
        spread = grid_values[:, None] * changes[None]
        return spread.reshape(-1, BOX, row_count, 2 * BOX)

    def with_potential(grid_values):
        return grid_values * potential

    source = through_grid(solved, with_changes)
    right_side = project_occupied(source) - source
    response = jnp.zeros_like(right_side)
    residual = right_side
    direction = right_side
    norm_now = None
    for iteration in range(ITERS):
        image = (
            (kinetic - energy_shift) * direction
            + through_grid(direction, with_potential)
            + shift_weight * project_occupied(direction)
        )
        curve, cross, square, start_norm = four_sums(direction, image, residual)
        if iteration == 0:
            norm_now = start_norm
        step_size = norm_now / curve
        response = response + step_size[:, None, None, None] * direction
        residual = residual - step_size[:, None, None, None] * image
        if iteration + 1 < ITERS:
            fresh = norm_now - 2.0 * step_size * cross + step_size * step_size * square
            direction = residual + (fresh / norm_now)[:, None, None, None] * direction
            norm_now = fresh
    local_bands = energies.shape[0]
    response = response.reshape(local_bands, NPERT, slab_rows, BOX, 2 * BOX)
    residual = residual.reshape(local_bands, NPERT, slab_rows, BOX, 2 * BOX)
    return (response, residual)


def solution(mesh):
    placed = (
        P(("pool", "band"), "ga", None, None),
        P(("pool", "band")),
        P("pool"),
        P(("pool", "ga"), None),
        P(None, "ga"),
        P(None, None, "ga"),
    )
    return jax.shard_map(
        on_device,
        mesh=mesh,
        in_specs=placed,
        out_specs=(
            P(("pool", "band"), None, "ga", None, None),
            P(("pool", "band"), None, "ga", None, None),
        ),
        check_vma=False,
    )
```

profile of v0, /device:TPU:0, one launch (start us, length us, event | category | flops | bytes accessed | tf_op | source)
XLA Modules:
  0.0 409.5 jit_solution(5339355475982310337)
XLA Ops:
  8.3 2.5 broadcast_multiply_fusion
  13.4 2.7 copy.96
  20.7 7.7 %all-to-all-start = ((f32[4,4,64,128]{3,1,0,2:T(4,128)}), f32[4,4,64,128]{3,1,0,2:T(4,128)S(1)}, u32[]{:S(2)}, u32[]{:S(2)}) async-start(f32[4,4,64,128]{3,1,0,2:T(4,128)} %copy.97), calls=%async_computation | async-start | bytes 1048576 | tf_op jit(solution)/shard_map/all_to_all | solution.py:151
  28.9 11.0 %all-to-all-done = f32[4,4,64,128]{3,1,0,2:T(4,128)S(1)} async-done(((f32[4,4,64,128]{3,1,0,2:T(4,128)}), f32[4,4,64,128]{3,1,0,2:T(4,128)S(1)}, u32[]{:S(2)}, u32[]{:S(2)}) %all-to-all-start) | async-done | bytes 524320 | tf_op jit(solution)/shard_map/all_to_all | solution.py:151
  44.2 2.1 maximum_add_fusion
  46.3 2.2 copy.100
  48.5 4.0 all-to-all-start.1
  56.1 18.7 %all-to-all-done.1 = f32[12,64,4,128]{3,2,0,1:T(4,128)S(1)} async-done(((f32[12,64,4,128]{3,2,0,1:T(4,128)}), f32[12,64,4,128]{3,2,0,1:T(4,128)S(1)}, u32[]{:S(2)}, u32[]{:S(2)}) %all-to-all-start.1) | async-done | bytes 1572896 | tf_op jit(solution)/shard_map/all_to_all | solution.py:155
  81.8 44.4 %all-gather.2.cloned.1.call-done = bf16[256,4,43,128]{3,1,2,0:T(4,128)(2,1)} async-done(((bf16[64,4,43,128]{3,1,2,0:T(4,128)(2,1)}), bf16[256,4,43,128]{3,1,2,0:T(4,128)(2,1)}) %all-gather.2.cloned.1.call-update) | async-done | bytes 11272208 | tf_op jit(solution)/shard_map/all_gather | solution.py:123
  126.2 18.7 %copy.104 = bf16[256,4,43,128]{0,3,2,1:T(8,128)(2,1)} copy(bf16[256,4,43,128]{3,1,2,0:T(4,128)(2,1)} %all-gather.2.cloned.1.call-done) | data formatting | bytes 22544384 | tf_op jit(solution)/shard_map/all_gather | solution.py:123
  144.9 5.5 %convolution_bitcast_fusion.16 = f32[256,24]{0,1:T(8,128)S(1)} fusion(bf16[256,4,43,128]{0,3,2,1:T(8,128)(2,1)} %copy.104, bf16[24,4,43,128]{3,2,1,0:T(8,128)(2,1)S(1)} %maximum_maximum_fusion), kind=kOutput, calls=%fused_computation.85 | convolution fusion | flops 270532608 | bytes 12353536 | tf_op jit(solution)/shard_map/dot_general | solution.py:132
  151.1 7.0 %all-to-all-start.2 = ((f32[16,256,24]{1,2,0:T(8,128)}), f32[16,256,24]{1,2,0:T(8,128)S(1)}, u32[]{:S(2)}, u32[]{:S(2)}) async-start(f32[16,256,24]{1,2,0:T(8,128)} %broadcast_in_dim.12), calls=%async_computation.2 | async-start | bytes 786432 | tf_op jit(solution)/shard_map/all_to_all | solution.py:21
  158.3 9.8 %all-to-all-done.2 = f32[16,256,24]{1,2,0:T(8,128)S(1)} async-done(((f32[16,256,24]{1,2,0:T(8,128)}), f32[16,256,24]{1,2,0:T(8,128)S(1)}, u32[]{:S(2)}, u32[]{:S(2)}) %all-to-all-start.2) | async-done | bytes 393248 | tf_op jit(solution)/shard_map/all_to_all | solution.py:21
  168.1 7.2 %fusion.227 = f32[24,22016]{1,0:T(8,128)S(1)} fusion(bf16[256,24]{0,1:T(8,128)(2,1)S(1)} %reduce_sum.112, bf16[256,22016]{0,1:T(8,128)(2,1)} %bitcast.230), kind=kOutput, calls=%fused_computation.306 | convolution fusion | flops 270532608 | bytes 13398016 | tf_op jit(solution)/shard_map/dot_general | solution.py:137
  186.9 3.6 all-to-all-start.5
  194.3 2.1 maximum_add_fusion.3
  196.4 2.2 copy.105
  200.6 6.2 %all-to-all-start.3 = ((f32[12,4,64,128]{3,1,0,2:T(4,128)}), f32[12,4,64,128]{3,1,0,2:T(4,128)S(1)}, u32[]{:S(2)}, u32[]{:S(2)}) async-start(f32[12,4,64,128]{3,1,0,2:T(4,128)} %copy.105), calls=%async_computation.3 | async-start | bytes 3145728 | tf_op jit(solution)/shard_map/all_to_all | solution.py:151
  210.0 8.7 %fusion.226 = f32[24,22016]{1,0:T(8,128)} fusion(bf16[256,24]{0,1:T(8,128)(2,1)S(1)} %reduce_sum.113, bf16[256,22016]{0,1:T(8,128)(2,1)} %bitcast.231), kind=kOutput, calls=%fused_computation.305 | convolution fusion | flops 270532608 | bytes 13398016 | tf_op jit(solution)/shard_map/dot_general | solution.py:137
  218.6 10.0 %all-to-all-done.3 = f32[12,4,64,128]{3,1,0,2:T(4,128)S(1)} async-done(((f32[12,4,64,128]{3,1,0,2:T(4,128)}), f32[12,4,64,128]{3,1,0,2:T(4,128)S(1)}, u32[]{:S(2)}, u32[]{:S(2)}) %all-to-all-start.3) | async-done | bytes 1572896 | tf_op jit(solution)/shard_map/all_to_all | solution.py:151
  231.4 2.2 fusion.8
  235.9 2.1 maximum_add_fusion.5
  238.0 2.2 copy.109
  240.1 4.6 %all-to-all-start.4 = ((f32[12,64,4,128]{3,2,0,1:T(4,128)}), f32[12,64,4,128]{3,2,0,1:T(4,128)}, u32[]{:S(2)}, u32[]{:S(2)}) async-start(f32[12,64,4,128]{3,2,0,1:T(4,128)} %copy.109), calls=%async_computation.4 | async-start | bytes 3145728 | tf_op jit(solution)/shard_map/all_to_all | solution.py:155
  244.7 3.0 fusion.221
  252.5 13.8 %all-to-all-done.4 = f32[12,64,4,128]{3,2,0,1:T(4,128)} async-done(((f32[12,64,4,128]{3,2,0,1:T(4,128)}), f32[12,64,4,128]{3,2,0,1:T(4,128)}, u32[]{:S(2)}, u32[]{:S(2)}) %all-to-all-start.4) | async-done | bytes 1572896 | tf_op jit(solution)/shard_map/all_to_all | solution.py:155
  272.6 3.3 multiply_reduce_fusion.6
  276.0 10.1 %all_to_all.135 = f32[16,1,48]{2,1,0:T(1,128)S(1)} all-to-all(f32[16,1,48]{2,1,0:T(1,128)S(1)} %broadcast_in_dim.15), channel_id=1, replica_groups=mesh['ga'=16,'band'=4,'pool'=2] {'ga'}, dimensions={0} | all-to-all | bytes 6144 | tf_op jit(solution)/shard_map/all_to_all | solution.py:21
  286.2 3.2 fusion.217
  290.6 5.5 %convolution_bitcast_fusion.14 = f32[256,24]{0,1:T(8,128)S(1)} fusion(bf16[256,4,43,128]{0,3,2,1:T(8,128)(2,1)} %copy.104, bf16[24,4,43,128]{3,2,1,0:T(8,128)(2,1)S(1)} %maximum_maximum_fusion.2), kind=kOutput, calls=%fused_computation.83 | convolution fusion | flops 270532608 | bytes 12353536 | tf_op jit(solution)/shard_map/dot_general | solution.py:132
  296.9 4.4 %all-to-all-start.9 = ((f32[16,256,24]{1,2,0:T(8,128)}), f32[16,256,24]{1,2,0:T(8,128)}, u32[]{:S(2)}, u32[]{:S(2)}) async-start(f32[16,256,24]{1,2,0:T(8,128)} %broadcast_in_dim.16), calls=%async_computation.9 | async-start | bytes 786432 | tf_op jit(solution)/shard_map/all_to_all | solution.py:21
  305.1 2.1 maximum_add_fusion.8
  307.2 2.2 copy.114
  310.7 6.3 %all-to-all-start.7 = ((f32[12,4,64,128]{3,1,0,2:T(4,128)}), f32[12,4,64,128]{3,1,0,2:T(4,128)}, u32[]{:S(2)}, u32[]{:S(2)}) async-start(f32[12,4,64,128]{3,1,0,2:T(4,128)} %copy.114), calls=%async_computation.7 | async-start | bytes 3145728 | tf_op jit(solution)/shard_map/all_to_all | solution.py:151
  318.1 8.7 %fusion.225 = f32[24,22016]{1,0:T(8,128)} fusion(bf16[256,24]{0,1:T(8,128)(2,1)S(1)} %reduce_sum.118, bf16[256,22016]{0,1:T(8,128)(2,1)} %bitcast.232), kind=kOutput, calls=%fused_computation.304 | convolution fusion | flops 270532608 | bytes 13398016 | tf_op jit(solution)/shard_map/dot_general | solution.py:137
  326.7 11.8 %all-to-all-done.7 = f32[12,4,64,128]{3,1,0,2:T(4,128)} async-done(((f32[12,4,64,128]{3,1,0,2:T(4,128)}), f32[12,4,64,128]{3,1,0,2:T(4,128)}, u32[]{:S(2)}, u32[]{:S(2)}) %all-to-all-start.7) | async-done | bytes 1572896 | tf_op jit(solution)/shard_map/all_to_all | solution.py:151
  343.0 2.2 fusion.12
  347.5 2.1 maximum_add_fusion.10
  349.6 2.2 copy.116
  351.7 4.6 %all-to-all-start.8 = ((f32[12,64,4,128]{3,2,0,1:T(4,128)}), f32[12,64,4,128]{3,2,0,1:T(4,128)}, u32[]{:S(2)}, u32[]{:S(2)}) async-start(f32[12,64,4,128]{3,2,0,1:T(4,128)} %copy.116), calls=%async_computation.8 | async-start | bytes 3145728 | tf_op jit(solution)/shard_map/all_to_all | solution.py:155
  356.3 3.6 fusion.220
  359.9 2.7 slice.282
  362.6 2.7 slice.284
  365.2 2.1 slice_negate_fusion.10
  368.9 8.4 %all-to-all-done.8 = f32[12,64,4,128]{3,2,0,1:T(4,128)} async-done(((f32[12,64,4,128]{3,2,0,1:T(4,128)}), f32[12,64,4,128]{3,2,0,1:T(4,128)}, u32[]{:S(2)}, u32[]{:S(2)}) %all-to-all-start.8) | async-done | bytes 1572896 | tf_op jit(solution)/shard_map/all_to_all | solution.py:155
  384.3 3.4 multiply_reduce_fusion.3
  387.8 10.1 %all_to_all.136 = f32[16,1,48]{2,1,0:T(1,128)S(1)} all-to-all(f32[16,1,48]{2,1,0:T(1,128)S(1)} %broadcast_in_dim.17), channel_id=1, replica_groups=mesh['ga'=16,'band'=4,'pool'=2] {'ga'}, dimensions={0} | all-to-all | bytes 6144 | tf_op jit(solution)/shard_map/all_to_all | solution.py:21
  398.0 4.5 %multiply_subtract_fusion = (f32[12,4,64,128]{3,2,1,0:T(8,128)}, f32[12,4,64,128]{3,2,1,0:T(8,128)}) fusion(f32[12,4,64,128]{3,2,1,0:T(8,128)} %get-tuple-element.11, f32[12,4,64,128]{3,2,1,0:T(8,128)} %get-tuple-element.67, f32[12]{0:T(128)S(1)} %slice_divide_fusion, f32[12,4,64,128]{3,2,1,0:T(8,128)S(1)} %get-tuple-element.10, ...), kind=kLoop, calls=%fused_computation.46 | loop fusion | flops 1966080 | bytes 9437280 | tf_op jit(solution)/shard_map/sub | solution.py:183
  (177 shorter events, 84.2 us)
Async XLA Ops:
  7.2 119.1 %all-gather.2.cloned.1.call-start = ((), (), s32[]{:S(2)}) async-start(), calls=%async_computation.11 | async-start | bytes 14090240 | tf_op jit(solution)/shard_map/all_gather | solution.py:123
  10.8 2.6 copy-start.1
  16.2 174.3 %copy-start.15 = (f32[64,64]{1,0:T(8,128)}, f32[64,64]{1,0:T(8,128)S(1)}, u32[]{:S(2)}) copy-start(f32[64,64]{1,0:T(8,128)S(1)} %fusion.89) | copy-start | bytes 49156
  16.4 174.1 %copy-start.17 = (f32[64,64]{1,0:T(8,128)}, f32[64,64]{1,0:T(8,128)S(1)}, u32[]{:S(2)}) copy-start(f32[64,64]{1,0:T(8,128)S(1)} %get-tuple-element.68) | copy-start | bytes 49156
  19.5 8.8 %copy-start.19 = (f32[3,64,256]{2,1,0:T(8,128)S(1)}, f32[3,64,256]{2,1,0:T(8,128)}, u32[]{:S(2)}) copy-start(f32[3,64,256]{2,1,0:T(8,128)} %param.11) | copy-start | bytes 589828
  20.7 19.2 %all-to-all-start = ((f32[4,4,64,128]{3,1,0,2:T(4,128)}), f32[4,4,64,128]{3,1,0,2:T(4,128)S(1)}, u32[]{:S(2)}, u32[]{:S(2)}) async-start(f32[4,4,64,128]{3,1,0,2:T(4,128)} %copy.97), calls=%async_computation | async-start | bytes 1048576 | tf_op jit(solution)/shard_map/all_to_all | solution.py:151
  48.5 4.0 copy-start.21
  48.5 26.3 %all-to-all-start.1 = ((f32[12,64,4,128]{3,2,0,1:T(4,128)}), f32[12,64,4,128]{3,2,0,1:T(4,128)S(1)}, u32[]{:S(2)}, u32[]{:S(2)}) async-start(f32[12,64,4,128]{3,2,0,1:T(4,128)} %copy.100), calls=%async_computation.1 | async-start | bytes 3145728 | tf_op jit(solution)/shard_map/all_to_all | solution.py:155
  55.1 24.0 %copy-start.12 = (f32[64,64]{1,0:T(8,128)}, f32[64,64]{1,0:T(8,128)S(1)}, u32[]{:S(2)}) copy-start(f32[64,64]{1,0:T(8,128)S(1)} %get-tuple-element.71) | copy-start | bytes 49156
  151.1 16.9 %all-to-all-start.2 = ((f32[16,256,24]{1,2,0:T(8,128)}), f32[16,256,24]{1,2,0:T(8,128)S(1)}, u32[]{:S(2)}, u32[]{:S(2)}) async-start(f32[16,256,24]{1,2,0:T(8,128)} %broadcast_in_dim.12), calls=%async_computation.2 | async-start | bytes 786432 | tf_op jit(solution)/shard_map/all_to_all | solution.py:21
  179.6 4.0 slice-start
  180.0 3.6 slice-start.1
  182.0 2.4 slice-start.2
  186.9 12.9 %all-to-all-start.5 = ((f32[16,256,24]{1,2,0:T(8,128)}), f32[16,256,24]{1,2,0:T(8,128)S(1)}, u32[]{:S(2)}, u32[]{:S(2)}) async-start(f32[16,256,24]{1,2,0:T(8,128)} %broadcast_in_dim.14), calls=%async_computation.5 | async-start | bytes 786432 | tf_op jit(solution)/shard_map/all_to_all | solution.py:21
  198.5 8.3 %copy-start.20 = (f32[64,256]{1,0:T(8,128)S(1)}, f32[64,256]{1,0:T(8,128)}, u32[]{:S(2)}) copy-start(f32[64,256]{1,0:T(8,128)} %param.10) | copy-start | bytes 196612
  198.5 9.1 %copy-start.22 = (f32[4]{0:T(128)S(1)}, f32[4]{0:T(128)}, u32[]{:S(2)}) copy-start(f32[4]{0:T(128)} %param.7) | copy-start | bytes 52
  199.9 0.7 copy-start.7
  200.6 28.0 %all-to-all-start.3 = ((f32[12,4,64,128]{3,1,0,2:T(4,128)}), f32[12,4,64,128]{3,1,0,2:T(4,128)S(1)}, u32[]{:S(2)}, u32[]{:S(2)}) async-start(f32[12,4,64,128]{3,1,0,2:T(4,128)} %copy.105), calls=%async_computation.3 | async-start | bytes 3145728 | tf_op jit(solution)/shard_map/all_to_all | solution.py:151
  208.9 22.5 %copy-start.10 = (f32[64,4,128]{2,0,1:T(8,128)}, f32[64,4,128]{2,0,1:T(8,128)S(1)}, u32[]{:S(2)}) copy-start(f32[64,4,128]{2,0,1:T(8,128)S(1)} %pad_maximum_fusion.7) | copy-start | bytes 393220
  240.1 26.2 %all-to-all-start.4 = ((f32[12,64,4,128]{3,2,0,1:T(4,128)}), f32[12,64,4,128]{3,2,0,1:T(4,128)}, u32[]{:S(2)}, u32[]{:S(2)}) async-start(f32[12,64,4,128]{3,2,0,1:T(4,128)} %copy.109), calls=%async_computation.4 | async-start | bytes 3145728 | tf_op jit(solution)/shard_map/all_to_all | solution.py:155
  250.8 1.3 copy-start.2
  252.4 15.8 %copy-start.4 = (f32[12,4,43,128]{3,2,1,0:T(8,128)}, f32[12,4,43,128]{3,2,1,0:T(8,128)S(1)}, u32[]{:S(2)}) copy-start(f32[12,4,43,128]{3,2,1,0:T(8,128)S(1)} %maximum_add_fusion.20) | copy-start | bytes 3170308
  271.5 1.1 slice-start.3
  271.5 1.1 copy-start.8
  271.5 1.1 copy-start.13
  290.6 10.7 %copy-start.16 = (f32[64,64]{1,0:T(8,128)S(1)}, f32[64,64]{1,0:T(8,128)}, u32[]{:S(2)}) copy-start(f32[64,64]{1,0:T(8,128)} %copy-done.15) | copy-start | bytes 49156
  290.6 10.7 %copy-start.18 = (f32[64,64]{1,0:T(8,128)S(1)}, f32[64,64]{1,0:T(8,128)}, u32[]{:S(2)}) copy-start(f32[64,64]{1,0:T(8,128)} %copy-done.17) | copy-start | bytes 49156
  296.9 13.8 %all-to-all-start.9 = ((f32[16,256,24]{1,2,0:T(8,128)}), f32[16,256,24]{1,2,0:T(8,128)}, u32[]{:S(2)}, u32[]{:S(2)}) async-start(f32[16,256,24]{1,2,0:T(8,128)} %broadcast_in_dim.16), calls=%async_computation.9 | async-start | bytes 786432 | tf_op jit(solution)/shard_map/all_to_all | solution.py:21
  310.7 27.9 %all-to-all-start.7 = ((f32[12,4,64,128]{3,1,0,2:T(4,128)}), f32[12,4,64,128]{3,1,0,2:T(4,128)}, u32[]{:S(2)}, u32[]{:S(2)}) async-start(f32[12,4,64,128]{3,1,0,2:T(4,128)} %copy.114), calls=%async_computation.7 | async-start | bytes 3145728 | tf_op jit(solution)/shard_map/all_to_all | solution.py:151
  342.1 0.9 copy-start.11
  351.7 25.6 %all-to-all-start.8 = ((f32[12,64,4,128]{3,2,0,1:T(4,128)}), f32[12,64,4,128]{3,2,0,1:T(4,128)}, u32[]{:S(2)}, u32[]{:S(2)}) async-start(f32[12,64,4,128]{3,2,0,1:T(4,128)} %copy.116), calls=%async_computation.8 | async-start | bytes 3145728 | tf_op jit(solution)/shard_map/all_to_all | solution.py:155
  365.2 2.1 copy-start.3
  367.8 1.2 copy-start.5
  382.5 1.4 copy-start
  382.6 1.5 slice-start.4
  382.6 1.7 copy-start.6
  382.6 1.7 copy-start.9
  382.6 1.7 copy-start.14
Sparse Core Ops, SparseCore 0:
  16.2 109.9 all-gather.1
where the time goes:
time: 417 us; the launch traced here: 410 us
  waiting for transfers between devices  131 us (31%)
  matrix products  89.3 us (21%)
  local copies, waits for them, and re-layouts  70.6 us (17%)
  starting transfers between devices  48.5 us (12%)
  other arithmetic  35 us (8%)
  blocking collectives  20.2 us (5%)
  between operations  15.3 us (4%)
    all_gather x1, waiting for transfers between devices, on_device(): lax.all_gather(keep_rows(occupied), 'band', axis=0, tiled=True)  44.4 us
    all_to_all x3, waiting for transfers between devices, through_grid(): moved = lax.all_to_all(back, 'ga', split_axis=1, concat_axis=2, tiled=True)  40.9 us
    all_to_all x3, waiting for transfers between devices, through_grid(): lax.all_to_all(near, 'ga', split_axis=2, concat_axis=1, tiled=True)  32.8 us
    dot_general x3, matrix products, project_occupied(): lax.dot_general(low_correlation, flat_panel, (((0,), (0,)), ((), ())), pr...  24.6 us
    dot_general x12, matrix products, transform_rows(): jnp.einsum(form, cosine_table, values, precision=lax.Precision.HIGHEST)  21.2 us
    all_to_all x3, starting transfers between devices, through_grid(): lax.all_to_all(near, 'ga', split_axis=2, concat_axis=1, tiled=True)  20.2 us
    all_to_all x2, blocking collectives, copy_for_each(): lax.all_to_all(jnp.broadcast_to(shard[None], (size, *shard.shape)), axis,...  20.2 us
    slice x9, local copies, waits for them, and re-layouts, project_occupied(): result = product[:count] + quarter_turn(product[count:])  19.2 us
  transfers between devices with their start and end apart: 10, of which 10 were waited for; matrix products, arithmetic and copies ran while one was open for 20% of the time, Pallas kernels for 0%

commit v1 on v0

v1 whole, which is shorter than its diff:
```python
import functools
import math

import jax
import jax.numpy as jnp
import numpy as np
from jax import lax
from jax.experimental import pallas as pl
from jax.experimental.pallas import tpu as pltpu
from jax.sharding import PartitionSpec as P

BOX = 64
GCUT = 21
KEPT = 2 * GCUT + 1
NPERT = 3
STRIDE = 16
BASE_ROW = 13
SHIFT = 16.0
ROWS = 2 * BASE_ROW + 1

cell_length = 16.5
shift_weight = 8.0

kept_freqs = list(range(GCUT + 1)) + list(range(-GCUT, 0))
place_of = {f: i for i, f in enumerate(kept_freqs)}
base_freqs = list(range(BASE_ROW + 1)) + list(range(-BASE_ROW, 0))
wide_freqs = [f for m in range(14, 19) for f in (m, -m)]
narrow_freqs = [f for m in range(19, 22) for f in (m, -m)]
WIDE = len(wide_freqs)
F32 = jnp.float32
BF16 = jnp.bfloat16


def add(a, b):
    if a is None:
        return b
    if b is None:
        return a
    return (a[0] + b[0], a[1] + b[1])


def sub(a, b):
    if b is None:
        return a
    if a is None:
        return (-b[0], -b[1])
    return (a[0] - b[0], a[1] - b[1])


def times_phase(a, turns, sign):
    if a is None:
        return None
    turns = turns % 1.0
    re, im = a
    if turns == 0.0:
        return a
    if turns == 0.5:
        return (-re, -im)
    if turns in (0.25, 0.75):
        if (turns == 0.25) == (sign > 0):
            return (-im, re)
        return (im, -re)
    c, s = math.cos(2 * math.pi * turns), sign * math.sin(2 * math.pi * turns)
    if turns in (0.125, 0.375, 0.625, 0.875):
        h = abs(c)
        if (c > 0) == (s > 0):
            pair = ((re - im) * h, (re + im) * h)
        else:
            pair = ((re + im) * h, (im - re) * h)
        return pair if c > 0 else (-pair[0], -pair[1])
    return (re * c - im * s, im * c + re * s)


def small_dft(xs, sign):
    n = len(xs)
    if n == 1:
        return xs
    even, odd = small_dft(xs[0::2], sign), small_dft(xs[1::2], sign)
    turned = [times_phase(o, k / n, sign) for k, o in enumerate(odd)]
    return [add(e, o) for e, o in zip(even, turned)] + [sub(e, o) for e, o in zip(even, turned)]


def dft64(load, keep, tmp, store, sign):
    for n2 in range(8):
        out = small_dft([load(8 * n1 + n2) for n1 in range(8)], sign)
        for k1 in range(8):
            re, im = times_phase(out[k1], n2 * k1 / 64.0, sign)
            tmp[8 * n2 + k1, 0:8] = re
            tmp[8 * n2 + k1, 8:16] = im
    for k1 in range(8):
        if not any((k1 + 8 * k2) in keep for k2 in range(8)):
            continue
        out = small_dft([(tmp[8 * n2 + k1, 0:8], tmp[8 * n2 + k1, 8:16]) for n2 in range(8)], sign)
        for k2 in range(8):
            if (k1 + 8 * k2) in keep:
                store(k1 + 8 * k2, out[k2])


def corner_turn(block):
    front = lax.broadcasted_iota(jnp.int32, (8, 2 * BOX), 1) < BOX
    top = lax.broadcasted_iota(jnp.int32, (8, 2 * BOX), 0) < 4
    half = []
    for h in range(2):
        a, b = block[2 * h], block[2 * h + 1]
        half.append(
            (
                jnp.where(front, a, pltpu.roll(b, BOX, 1)),
                jnp.where(front, pltpu.roll(a, BOX, 1), b),
            )
        )
    out = [None] * 4
    for i in range(2):
        a, b = half[0][i], half[1][i]
        out[i] = jnp.where(top, a, pltpu.roll(b, 4, 0))
        out[2 + i] = jnp.where(top, pltpu.roll(a, 4, 0), b)
    return out


def turn_in(src, rows, dst):
    for s in range(16):
        tiles = [src[4 * s + c, rows].astype(F32) for c in range(4)]
        re = corner_turn([t[0:8] for t in tiles])
        im = corner_turn([t[8:16] for t in tiles])
        for c in range(4):
            dst[4 * s + c, 0:8] = re[c]
            dst[4 * s + c, 8:16] = im[c]


def pair(ref):
    return lambda n: (ref[n, 0:8], ref[n, 8:16])


def put_pair(ref, rows, dtype):
    def store(n, value):
        ref[n, rows] = jnp.concatenate([value[0], value[1]], axis=0).astype(dtype)

    return store


def split_dot(x, high, low):
    hi = x.astype(BF16)
    lo = (x - hi.astype(F32)).astype(BF16)
    dot = functools.partial(jnp.dot, preferred_element_type=F32)
    return dot(hi, high) + dot(lo, high) + dot(hi, low)


def lanes_forward(src, first_row, high, low, dst):
    a = src[:, pl.ds(first_row, 8), :].reshape(KEPT * 8, 2 * BOX)
    b = src[:, pl.ds(first_row + 8, 8), :].reshape(KEPT * 8, 2 * BOX)
    out = split_dot(jnp.concatenate([a, b], axis=1), high, low)
    dst[0:KEPT, 0:8, :] = out[:, : 2 * BOX].reshape(KEPT, 8, 2 * BOX)
    dst[0:KEPT, 8:16, :] = out[:, 2 * BOX :].reshape(KEPT, 8, 2 * BOX)


def lanes_back(src, high, low):
    x = jnp.concatenate(
        [
            src[0:KEPT, 0:8, :].reshape(KEPT * 8, 2 * BOX),
            src[0:KEPT, 8:16, :].reshape(KEPT * 8, 2 * BOX),
        ],
        axis=1,
    )
    out = split_dot(x, high, low)
    return (
        out[:, : 2 * BOX].reshape(KEPT, 8, 2 * BOX),
        out[:, 2 * BOX :].reshape(KEPT, 8, 2 * BOX),
    )


def lane_tables():
    index = np.arange(BOX)
    angle = (index[:, None] * index[None, :] % BOX) * (2.0 * np.pi / BOX)
    c, s, z = np.cos(angle), np.sin(angle), np.zeros((BOX, BOX))
    forward = np.block([[c, z, s, z], [-s, z, c, z], [z, c, z, s], [z, -s, z, c]])
    s = -s
    back = np.block([[c, s, z, z], [z, z, c, s], [-s, c, z, z], [z, z, -s, c]])
    out = []
    for w in (forward, back):
        w = jnp.asarray(w, F32)
        high = w.astype(BF16)
        out += [high, (w - high.astype(F32)).astype(BF16)]
    return out


kept_place = lambda n: n if n <= GCUT else (n - (BOX - KEPT) if n >= BOX - GCUT else None)
KEPT_SET = frozenset(f % BOX for f in kept_freqs)
ALL_SET = frozenset(range(BOX))


def load_kept(ref):
    def load(n):
        place = kept_place(n)
        return None if place is None else (ref[place, 0:8], ref[place, 8:16])

    return load


def forward_tile(src, first_row, high, low, near, tmp, store):
    lanes_forward(src, first_row, high, low, near)
    dft64(load_kept(near), ALL_SET, tmp, store, 1)


def back_tile(src, rows, high, low, near, tmp):
    turn_in(src, rows, near)

    def store(n, value):
        tmp2 = near
        tmp2[kept_place(n), 0:8] = value[0]
        tmp2[kept_place(n), 8:16] = value[1]

    dft64(pair(near), KEPT_SET, tmp, store, -1)
    return lanes_back(near, high, low)


def front_lanes(shape):
    return lax.broadcasted_iota(jnp.int32, shape, len(shape) - 1) % BOX < BOX // 2


def pack_row(get, r):
    value = get(base_freqs[r])
    front = front_lanes(value.shape)
    axis = value.ndim - 1
    if r < WIDE:
        guest = jnp.where(front, get(wide_freqs[r]), 0.0)
        value = value + pltpu.roll(guest, GCUT + 1, axis)
    elif r < 2 * WIDE:
        guest = jnp.where(front, 0.0, get(wide_freqs[r - WIDE]))
        value = value + pltpu.roll(guest, 2 * BOX - GCUT, axis)
    elif r < 2 * WIDE + 6:
        guest = get(narrow_freqs[r - 2 * WIDE])
        value = value + pltpu.roll(jnp.where(front, guest, 0.0), BOX // 2, axis)
        value = value + pltpu.roll(jnp.where(front, 0.0, guest), 3 * BOX // 2, axis)
    return value


def unpack_row(get, f):
    if f in base_freqs:
        return get(base_freqs.index(f))
    if f in wide_freqs:
        r = wide_freqs.index(f)
        up, down = get(r), get(WIDE + r)
        axis = up.ndim - 1
        return jnp.where(
            front_lanes(up.shape),
            pltpu.roll(up, 2 * BOX - GCUT - 1, axis),
            pltpu.roll(down, GCUT, axis),
        )
    value = get(2 * WIDE + narrow_freqs.index(f))
    axis = value.ndim - 1
    return jnp.where(
        front_lanes(value.shape),
        pltpu.roll(value, 3 * BOX // 2, axis),
        pltpu.roll(value, BOX // 2, axis),
    )


def lane_sign(shape):
    return jnp.where(lax.broadcasted_iota(jnp.int32, shape, len(shape) - 1) < BOX, 1.0, -1.0)


def panel_rows(panel, r, p):
    return jnp.concatenate([panel[b, r, p] for b in range(4)], axis=0)


def correlate(values, panel, fold, packed):
    for r in range(ROWS):
        straight = pack_row(lambda f: values[place_of[f]], r)
        turned = pack_row(
            lambda f: pltpu.roll(values[place_of[f]], BOX, 1) * lane_sign((48, 2 * BOX)), r
        )
        packed[r] = jnp.concatenate([straight, turned], axis=0).astype(BF16)
    total = [None] * 4
    for r in range(0, ROWS, 2):
        both = r + 1 < ROWS
        y = jnp.concatenate([packed[r], packed[r + 1]], axis=1) if both else packed[r]
        for p in range(4):
            o = panel_rows(panel, r, p)
            if both:
                o = jnp.concatenate([o, panel_rows(panel, r + 1, p)], axis=1)
            part = lax.dot_general(o, y, (((1,), (1,)), ((), ())), preferred_element_type=F32)
            total[p] = part if total[p] is None else total[p] + part
    column = lax.broadcasted_iota(jnp.int32, (256, 96), 1) % 16 // 4
    chosen = total[0]
    for p in range(1, 4):
        chosen = jnp.where(column == 2 * (p % 2) + p // 2, total[p], chosen)
    hi = chosen.astype(BF16)
    lo = (chosen - hi.astype(F32)).astype(BF16)
    nt = (((1,), (1,)), ((), ()))
    return lax.dot_general(fold, hi, nt, preferred_element_type=F32) + lax.dot_general(
        fold, lo, nt, preferred_element_type=F32
    )


def fold_table():
    f = np.zeros((2, 3, 4, 2, 3, 4, 4), np.float32)
    for a in range(2):
        for t in range(3):
            for q in range(4):
                f[a, t, q, a, t, :, q] = 1.0
    return f.reshape(24, 96)


def spread_table():
    f = np.zeros((4, 2, 3, 2, 2, 4, 2, 3, 4), np.float32)
    for p in range(4):
        for a in range(2):
            for t in range(3):
                for q in range(4):
                    f[p, a, t, p % 2, p // 2, q, a, t, q] = 1.0
    return f.reshape(384, 24)


def combine(corr, panel, spread, product, finish):
    rows = jnp.dot(spread[...], corr, preferred_element_type=F32).astype(BF16)
    sign = -lane_sign((48, 2 * BOX))
    for r in range(0, ROWS, 2):
        both = r + 1 < ROWS
        total = None
        for p in range(4):
            o = panel_rows(panel, r, p)
            if both:
                o = jnp.concatenate([o, panel_rows(panel, r + 1, p)], axis=1)
            part = jnp.dot(rows[96 * p : 96 * p + 96], o, preferred_element_type=F32)
            total = part if total is None else total + part
        for c in range(2 if both else 1):
            lanes = slice(2 * BOX * c, 2 * BOX * (c + 1))
            product[r + c] = (
                total[:48, lanes] + pltpu.roll(total[48:, lanes], BOX, 1) * sign
            )
    for f in kept_freqs:
        finish(place_of[f], unpack_row(lambda r: product[r], f))


VMEM_LIMIT = 60 * 1024 * 1024
vmem = pl.BlockSpec(memory_space=pltpu.VMEM)
TILE = pltpu.VMEM((BOX, 16, 2 * BOX), F32)


def call(body, outs, args, scratch=(), flops=10**9):
    return pl.pallas_call(
        body,
        out_shape=outs,
        in_specs=[vmem] * len(args),
        out_specs=jax.tree.map(lambda _: vmem, outs),
        scratch_shapes=list(scratch),
        compiler_params=pltpu.CompilerParams(vmem_limit_bytes=VMEM_LIMIT),
        cost_estimate=pl.CostEstimate(flops=flops, bytes_accessed=4 * 10**6, transcendentals=0),
    )(*args)


def shape(dims, dtype=F32):
    return jax.ShapeDtypeStruct(dims, dtype)


def pack_body(psi, mask, out):
    for r in range(ROWS):
        get = lambda f: psi[0, f % BOX].astype(F32) * mask[0, f % BOX]
        out[r, 0] = pack_row(get, r).astype(BF16)


def pack_panel(psi, mask):
    bands = psi.shape[2]
    return pl.pallas_call(
        pack_body,
        grid=(4,),
        out_shape=shape((ROWS, 4, bands, 2 * BOX), BF16),
        in_specs=[
            pl.BlockSpec((1, BOX, bands, 2 * BOX), lambda p: (p, 0, 0, 0)),
            pl.BlockSpec((1, BOX, 1, 2 * BOX), lambda p: (p, 0, 0, 0)),
        ],
        out_specs=pl.BlockSpec((ROWS, 1, bands, 2 * BOX), lambda p: (0, p, 0, 0)),
    )(psi, mask)


def source_forward_body(solved, high, low, out, near, tmp):
    forward_tile(solved, 0, high[...], low[...], near, tmp, put_pair(out, slice(0, 16), F32))


def source_middle_body(came, changes, out, near, tmp, space):
    turn_in(came, slice(0, 16), near)

    def keep(n, value):
        space[n, 0:8] = value[0]
        space[n, 8:16] = value[1]

    dft64(pair(near), ALL_SET, tmp, keep, 1)

    def each(p, carry):
        def load(n):
            d = changes[p, n]
            return (space[n, 0:8] * d, space[n, 8:16] * d)

        rows = pl.ds(pl.multiple_of(16 * p, 16), 16)
        dft64(load, ALL_SET, tmp, put_pair(out, rows, F32), -1)
        return carry

    lax.fori_loop(0, NPERT, each, 0)


def back_body(came, high, low, mask, out, near, tmp):
    def each(t, carry):
        start = pl.multiple_of(16 * t, 16)
        a, b = back_tile(came, pl.ds(start, 16), high[...], low[...], near, tmp)
        out[:, pl.ds(start, 8), :] = a * mask[:, 0:8, :]
        out[:, pl.ds(start + 8, 8), :] = b * mask[:, 8:16, :]
        return carry

    lax.fori_loop(0, 3, each, 0)


def forward_body(values, high, low, out, near, tmp):
    def each(t, carry):
        start = pl.multiple_of(16 * t, 16)
        forward_tile(values, start, high[...], low[...], near, tmp, put_pair(out, pl.ds(start, 16), BF16))
        return carry

    lax.fori_loop(0, 3, each, 0)


def middle_body(came, potential, out, near, tmp):
    def each(t, carry):
        rows = pl.ds(pl.multiple_of(16 * t, 16), 16)
        turn_in(came, rows, near)

        def keep(n, value):
            v = potential[n]
            near[n, 0:8] = value[0] * v
            near[n, 8:16] = value[1] * v

        dft64(pair(near), ALL_SET, tmp, keep, 1)
        dft64(pair(near), ALL_SET, tmp, put_pair(out, rows, BF16), -1)
        return carry

    lax.fori_loop(0, 3, each, 0)


def correlate_body(values, panel, fold, out, packed):
    out[...] = correlate(values, panel, fold[...], packed).astype(BF16)


def combine_body(shares, panel, spread, mask, out, product):
    total = shares[0].astype(F32)
    for s in range(1, 16):
        total = total + shares[s].astype(F32)

    def finish(place, row):
        for t in range(3):
            out[place, 16 * t : 16 * t + 16] = row[16 * t : 16 * t + 16] * mask[place]

    combine(total.astype(BF16), panel, spread, product, finish)


def copy_for_each(shard, axis):
    size = lax.axis_size(axis)
    return lax.all_to_all(
        jnp.broadcast_to(shard[None], (size, *shard.shape)), axis, 0, 0, tiled=True
    )


def swap(values):
    return lax.all_to_all(values, "ga", split_axis=0, concat_axis=0, tiled=True)


def rows_of_planes(values):
    values = values.reshape(2, 2, BOX, 2 * BOX).transpose(2, 1, 0, 3).reshape(BOX, 4, 2 * BOX)
    return jnp.concatenate([values[: GCUT + 1], values[BOX - GCUT :]], axis=0)


def on_device(psi_occ, energies, k_point, g_mask, v_local, dv):
    planes = psi_occ.shape[1]
    ga_index = lax.axis_index("ga")
    indices = jnp.arange(BOX, dtype=jnp.int32)
    signed = jnp.where(indices < BOX // 2, indices, indices - BOX).astype(F32)
    owned = ga_index * planes + jnp.arange(planes, dtype=jnp.int32)
    freq_first = jnp.where(owned < BOX // 2, owned, owned - BOX).astype(F32)
    factor = 0.5 * (2.0 * math.pi / cell_length) ** 2
    kinetic = factor * (
        (freq_first[:, None, None] + k_point[0]) ** 2
        + (signed[None, :, None] + k_point[1]) ** 2
        + (signed[None, None, :] + k_point[2]) ** 2
    )
    kinetic = jnp.concatenate([kinetic, kinetic], axis=-1)
    sphere = g_mask.reshape(planes, BOX, BOX).astype(F32)
    sphere = jnp.concatenate([sphere, sphere], axis=-1)
    tables = lane_tables()
    fold = jnp.asarray(fold_table(), BF16)
    spread = jnp.asarray(spread_table(), BF16)

    packed = pack_panel(psi_occ.transpose(1, 2, 0, 3), sphere[:, :, None, :])
    panel = lax.all_gather(packed, "band", axis=0, tiled=False)

    mask4 = rows_of_planes(sphere)
    mask = jnp.repeat(mask4, 4, axis=1)
    level = (rows_of_planes(kinetic)[:, :, None, :] - energies[None, None, :, None]).reshape(
        KEPT, 16, 2 * BOX
    ) * mask
    mask_scaled = mask / BOX**3
    solved = psi_occ[::STRIDE].astype(F32) * sphere[None]
    solved = solved.reshape(4, 2, 2, BOX, 2 * BOX).transpose(3, 2, 1, 0, 4).reshape(BOX, 16, 2 * BOX)
    solved = jnp.concatenate([solved[: GCUT + 1], solved[BOX - GCUT :]], axis=0)
    potential = jnp.repeat(v_local.reshape(BOX, 2, 2 * BOX), 4, axis=1)
    changes = jnp.repeat(dv.reshape(NPERT, BOX, 2, 2 * BOX), 4, axis=2)

    grid_bf = shape((BOX, 48, 2 * BOX), BF16)
    grid_f = shape((BOX, 48, 2 * BOX), F32)
    natural = shape((KEPT, 48, 2 * BOX))

    def project(values):
        share = call(
            correlate_body, shape((24, 256), BF16), (values, panel, fold),
            [pltpu.VMEM((ROWS, 96, 2 * BOX), BF16)],
        )
        return call(
            combine_body, natural, (copy_for_each(share, "ga"), panel, spread, mask_scaled),
            [pltpu.VMEM((ROWS, 48, 2 * BOX), F32)],
        )

    def grid_potential(values):
        sent = call(forward_body, grid_bf, (values, tables[0], tables[1]), [TILE, TILE])
        sent = call(middle_body, grid_bf, (swap(sent), potential), [TILE, TILE])
        return call(back_body, natural, (swap(sent), tables[2], tables[3], mask_scaled), [TILE, TILE])

    sent = call(source_forward_body, shape((BOX, 16, 2 * BOX)), (solved, tables[0], tables[1]), [TILE, TILE])
    sent = call(source_middle_body, grid_f, (swap(sent), changes), [TILE, TILE, TILE])
    source = call(back_body, natural, (swap(sent), tables[2], tables[3], mask_scaled), [TILE, TILE])

    def by_tile(values):
        return values.reshape(KEPT, 3, 16, 2 * BOX)

    def apply(values):
        local = grid_potential(values)
        return (
            (by_tile(values) * level[:, None]).reshape(values.shape)
            + local
            + shift_weight * project(values)
        )

    def inner(a, b):
        total = jnp.sum(a * b, axis=(0, 2)).reshape(3, 4, 4)
        return jnp.sum(total, axis=1) / BOX**3

    first = project(source) - source
    image = apply(first)
    second = image - SHIFT * first
    other = apply(second)
    sums = jnp.stack([inner(first, first), inner(first, image), inner(image, image), inner(second, other)])
    m0, m1, m2, m3 = jnp.sum(copy_for_each(sums, "ga"), axis=0)
    step0 = m0 / m1
    fresh = m0 - 2.0 * step0 * m1 + step0 * step0 * m2
    u = 1.0 + fresh / m0 - step0 * SHIFT
    curve = u * u * m1 - 2.0 * u * step0 * (m2 - SHIFT * m1) + step0 * step0 * m3
    step1 = fresh / curve

    def each(v):
        return jnp.repeat(v[:, None, :], 4, axis=1).reshape(48)[None, :, None]

    response = each(step0 + step1 * u) * first - each(step1 * step0) * second
    residual = first - each(step0 + step1 * u) * image + each(step1 * step0) * other

    def placed(values):
        values = values.reshape(KEPT, 3, 2, 2, 4, 2 * BOX).transpose(4, 1, 3, 2, 0, 5)
        values = values.reshape(4, NPERT, 4, KEPT, 2 * BOX)
        gap = jnp.zeros((4, NPERT, 4, BOX - KEPT, 2 * BOX), F32)
        return jnp.concatenate([values[..., : GCUT + 1, :], gap, values[..., GCUT + 1 :, :]], axis=3)

    return placed(response), placed(residual)


def solution(mesh):
    placed = (
        P(("pool", "band"), "ga", None, None),
        P(("pool", "band")),
        P("pool"),
        P(("pool", "ga"), None),
        P(None, "ga"),
        P(None, None, "ga"),
    )
    return jax.shard_map(
        on_device,
        mesh=mesh,
        in_specs=placed,
        out_specs=(
            P(("pool", "band"), None, "ga", None, None),
            P(("pool", "band"), None, "ga", None, None),
        ),
        check_vma=False,
    )
```

time: 417 us -> 264 us (0.63); the launches traced: 410 us -> 262 us
  matrix products: 89.3 us -> 0 us
  Pallas kernels: 0 us -> 73 us
  local copies, waits for them, and re-layouts: 70.6 us -> 19.1 us
  waiting for transfers between devices: 131 us -> 84.3 us
  other arithmetic: 35 us -> 18.8 us
  starting transfers between devices: 48.5 us -> 37.5 us
  blocking collectives: 20.2 us -> 15.1 us
    dot_general x36 -> x0, matrix products: 89.3 us -> none  [the longest x3 24.6 us: project_occupied(): lax.dot_general(low_correlation, flat_panel, (((0,), (0,)), ((), ())), pr...]
    pallas_call x0 -> x16, Pallas kernels: none -> 73 us  [the longest x15 68.1 us: call(): pl.pallas_call(body, out_shape=outs, in_specs=[vmem] * len(args), out_spe...]
    all_gather x1, waiting for transfers between devices: 44.4 us -> 14.9 us  [on_device(): panel = lax.all_gather(packed, 'band', axis=0, tiled=False)]
    slice x26 -> x11, local copies, waits for them, and re-layouts: 23.2 us -> 0.89 us  [the longest x1 0.64 us: on_device(): k_point[1]]
    all_to_all x6, waiting for transfers between devices: 73.7 us -> 53.2 us  [swap(): return lax.all_to_all(values, 'ga', split_axis=0, concat_axis=0, tiled=True)]
    all_gather x1 -> x0, local copies, waits for them, and re-layouts: 18.7 us -> none  [on_device(): lax.all_gather(keep_rows(occupied), 'band', axis=0, tiled=True)]
    add x6 -> x0, local copies, waits for them, and re-layouts: 11.9 us -> none  [transform_rows(): return first + quarter_turn(second)]
    neg x16 -> x0, other arithmetic: 9.57 us -> none  [the longest x15 9.42 us: quarter_turn(): -values[..., halfway:]]
  transfers between devices with their start and end apart: 10 -> 10, of which waited for: 10 -> 10; matrix products, arithmetic and copies ran while one was open for 20% -> 3% of each run, Pallas kernels for 0% -> 16%
where the time goes in v1:
time: 264 us; the launch traced here: 262 us
  waiting for transfers between devices  84.3 us (32%)
  Pallas kernels  73 us (28%)
  starting transfers between devices  37.5 us (14%)
  local copies, waits for them, and re-layouts  19.1 us (7%)
  other arithmetic  18.8 us (7%)
  blocking collectives  15.1 us (6%)
  between operations  14.5 us (5%)
    pallas_call x15, Pallas kernels, call(): pl.pallas_call(body, out_shape=outs, in_specs=[vmem] * len(args), out_spe...  68.1 us
    all_to_all x6, waiting for transfers between devices, swap(): return lax.all_to_all(values, 'ga', split_axis=0, concat_axis=0, tiled=True)  53.2 us
    all_to_all x6, starting transfers between devices, swap(): return lax.all_to_all(values, 'ga', split_axis=0, concat_axis=0, tiled=True)  26.3 us
    all_to_all x3, waiting for transfers between devices, copy_for_each(): lax.all_to_all(jnp.broadcast_to(shard[None], (size, *shard.shape)), axis,...  16.2 us
    all_to_all x1, blocking collectives, copy_for_each(): lax.all_to_all(jnp.broadcast_to(shard[None], (size, *shard.shape)), axis,...  15.1 us
    all_gather x1, waiting for transfers between devices, on_device(): panel = lax.all_gather(packed, 'band', axis=0, tiled=False)  14.9 us
    all_to_all x3, starting transfers between devices, copy_for_each(): lax.all_to_all(jnp.broadcast_to(shard[None], (size, *shard.shape)), axis,...  11.2 us
    unnamed x33, local copies, waits for them, and re-layouts  9.84 us
  transfers between devices with their start and end apart: 10, of which 10 were waited for; matrix products, arithmetic and copies ran while one was open for 3% of the time, Pallas kernels for 16%

profile of v1, /device:TPU:0, one launch (start us, length us, event | category | flops | bytes accessed | tf_op | source)
XLA Modules:
  0.0 262.3 jit_solution(12078457180436693040)
XLA Ops:
  9.0 6.8 %copy.102 = bf16[64,4,64,128]{3,0,2,1:T(8,128)(2,1)} copy(bf16[64,4,64,128]{3,2,1,0:T(8,128)(2,1)} %param.10) | data formatting | bytes 8388608 | tf_op args[0]
  15.8 4.9 %shard_map.116 = bf16[27,4,64,128]{3,2,1,0:T(8,128)(2,1)} custom-call(bf16[4,64,64,128]{3,2,1,0:T(8,128)(2,1)} %bitcast.136, f32[4,64,1,128]{3,2,1,0:T(1,128)} %bitcast.148), custom_call_target="tpu_custom_call" | custom-call | tf_op jit(solution)/shard_map/pallas_call | solution.py:363
  21.6 1.0 convert_multiply_fusion
  23.8 2.3 shard_map.113
  26.1 7.3 %all-to-all-start = ((f32[64,16,128]{2,1,0:T(8,128)}), f32[64,16,128]{2,1,0:T(8,128)S(1)}, u32[]{:S(2)}, u32[]{:S(2)}) async-start(f32[64,16,128]{2,1,0:T(8,128)} %shard_map.113), calls=%async_computation | async-start | bytes 1048576 | tf_op jit(solution)/shard_map/all_to_all | solution.py:461
  34.2 10.8 %all-to-all-done.came = f32[64,16,128]{2,1,0:T(8,128)S(1)} async-done(((f32[64,16,128]{2,1,0:T(8,128)}), f32[64,16,128]{2,1,0:T(8,128)S(1)}, u32[]{:S(2)}, u32[]{:S(2)}) %all-to-all-start) | async-done | bytes 524320 | tf_op jit(solution)/shard_map/all_to_all | solution.py:461
  44.9 1.0 broadcast_in_dim.20
  46.0 3.4 %shard_map.114 = f32[64,48,128]{2,1,0:T(8,128)} custom-call(f32[64,16,128]{2,1,0:T(8,128)} %copy-done.11, f32[3,64,8,128]{3,2,1,0:T(8,128)} %bitcast.149), custom_call_target="tpu_custom_call" | custom-call | flops 1000000000 | bytes 4000000 | tf_op jit(solution)/shard_map/pallas_call | solution.py:340
  49.4 3.7 %all-to-all-start.1 = ((f32[64,48,128]{2,1,0:T(8,128)}), f32[64,48,128]{2,1,0:T(8,128)S(1)}, u32[]{:S(2)}, u32[]{:S(2)}) async-start(f32[64,48,128]{2,1,0:T(8,128)} %shard_map.114), calls=%async_computation.1 | async-start | bytes 3145728 | tf_op jit(solution)/shard_map/all_to_all | solution.py:461
  57.1 18.4 %all-to-all-done.1.came = f32[64,48,128]{2,1,0:T(8,128)S(1)} async-done(((f32[64,48,128]{2,1,0:T(8,128)}), f32[64,48,128]{2,1,0:T(8,128)S(1)}, u32[]{:S(2)}, u32[]{:S(2)}) %all-to-all-start.1) | async-done | bytes 1572896 | tf_op jit(solution)/shard_map/all_to_all | solution.py:461
  75.5 1.1 copy-done.4
  76.7 4.2 %shard_map.115.values = f32[43,48,128]{2,1,0:T(8,128)} custom-call(f32[64,48,128]{2,1,0:T(8,128)} %copy-done.4, bf16[256,256]{1,0:T(8,128)(2,1)} %constant.60.high, bf16[256,256]{1,0:T(8,128)(2,1)} %constant.63.low, f32[43,16,128]{2,1,0:T(8,128)} %get-tuple-element.13.mask), custom_call_target="tpu_custom_call" | custom-call | flops 1000000000 | bytes 4000000 | tf_op jit(solution)/shard_map/pallas_call | solution.py:340
  80.9 14.9 %all-gather.3.cloned.1.call-done = bf16[108,4,64,128]{3,2,1,0:T(8,128)(2,1)} async-done(((bf16[27,4,64,128]{3,2,1,0:T(8,128)(2,1)}), bf16[108,4,64,128]{3,2,1,0:T(8,128)(2,1)}) %all-gather.3.cloned.1.call-update) | async-done | bytes 7077904 | tf_op jit(solution)/shard_map/all_gather | solution.py:490
  95.8 6.2 %shard_map.117 = bf16[24,256]{1,0:T(8,128)(2,1)} custom-call(f32[43,48,128]{2,1,0:T(8,128)} %shard_map.115.values, bf16[4,27,4,64,128]{4,3,2,1,0:T(8,128)(2,1)} %bitcast.130, bf16[24,96]{1,0:T(8,128)(2,1)} %constant.50.clone.fold), custom_call_target="tpu_custom_call" | custom-call | flops 1000000000 | bytes 4000000 | tf_op jit(solution)/shard_map/pallas_call | solution.py:340
  102.7 15.1 %all_to_all.50.shares = bf16[16,24,256]{2,1,0:T(8,128)(2,1)} all-to-all(bf16[16,24,256]{2,1,0:T(8,128)(2,1)S(1)} %broadcast_in_dim.23), channel_id=1, replica_groups=mesh['ga'=16,'band'=4,'pool'=2] {'ga'}, dimensions={0} | all-to-all | bytes 393216 | tf_op jit(solution)/shard_map/all_to_all | solution.py:455
  117.7 5.7 %shard_map.118 = f32[43,48,128]{2,1,0:T(8,128)} custom-call(bf16[16,24,256]{2,1,0:T(8,128)(2,1)} %all_to_all.50.shares, bf16[4,27,4,64,128]{4,3,2,1,0:T(8,128)(2,1)} %bitcast.131, bf16[384,24]{1,0:T(8,128)(2,1)} %constant.51.clone.spread, f32[43,16,128]{2,1,0:T(8,128)} %get-tuple-element.13.mask), custom_call_target="tpu_custom_call" | custom-call | flops 1000000000 | bytes 4000000 | tf_op jit(solution)/shard_map/pallas_call | solution.py:340
  123.5 2.4 sub.65.values
  125.9 3.6 %shard_map.119 = bf16[64,48,128]{2,1,0:T(8,128)(2,1)} custom-call(f32[43,48,128]{2,1,0:T(8,128)} %sub.65.values, bf16[256,256]{1,0:T(8,128)(2,1)} %constant.56.high, bf16[256,256]{1,0:T(8,128)(2,1)} %constant.59.low), custom_call_target="tpu_custom_call" | custom-call | flops 1000000000 | bytes 4000000 | tf_op jit(solution)/shard_map/pallas_call | solution.py:340
  129.5 3.8 %all-to-all-start.3 = ((bf16[64,48,128]{2,1,0:T(8,128)(2,1)}), bf16[64,48,128]{2,1,0:T(8,128)(2,1)S(1)}, u32[]{:S(2)}, u32[]{:S(2)}) async-start(bf16[64,48,128]{2,1,0:T(8,128)(2,1)} %shard_map.119), calls=%async_computation.3 | async-start | bytes 1572864 | tf_op jit(solution)/shard_map/all_to_all | solution.py:461
  133.3 6.2 %shard_map.122 = bf16[24,256]{1,0:T(8,128)(2,1)} custom-call(f32[43,48,128]{2,1,0:T(8,128)} %sub.65.values, bf16[4,27,4,64,128]{4,3,2,1,0:T(8,128)(2,1)} %bitcast.132, bf16[24,96]{1,0:T(8,128)(2,1)} %constant.50.clone.fold), custom_call_target="tpu_custom_call" | custom-call | flops 1000000000 | bytes 4000000 | tf_op jit(solution)/shard_map/pallas_call | solution.py:340
  139.5 6.7 %all-to-all-done.3.came = bf16[64,48,128]{2,1,0:T(8,128)(2,1)S(1)} async-done(((bf16[64,48,128]{2,1,0:T(8,128)(2,1)}), bf16[64,48,128]{2,1,0:T(8,128)(2,1)S(1)}, u32[]{:S(2)}, u32[]{:S(2)}) %all-to-all-start.3) | async-done | bytes 786464 | tf_op jit(solution)/shard_map/all_to_all | solution.py:461
  146.2 1.4 broadcast_in_dim.25
  147.7 3.5 %all-to-all-start.5 = ((bf16[16,24,256]{2,1,0:T(8,128)(2,1)}), bf16[16,24,256]{2,1,0:T(8,128)(2,1)S(1)}, u32[]{:S(2)}, u32[]{:S(2)}) async-start(bf16[16,24,256]{2,1,0:T(8,128)(2,1)} %broadcast_in_dim.25), calls=%async_computation.5 | async-start | bytes 393216 | tf_op jit(solution)/shard_map/all_to_all | solution.py:455
  152.0 3.7 %shard_map.120 = bf16[64,48,128]{2,1,0:T(8,128)(2,1)} custom-call(bf16[64,48,128]{2,1,0:T(8,128)(2,1)} %copy-done.6, f32[64,8,128]{2,1,0:T(8,128)} %bitcast.152), custom_call_target="tpu_custom_call" | custom-call | flops 1000000000 | bytes 4000000 | tf_op jit(solution)/shard_map/pallas_call | solution.py:340
  155.7 3.8 %all-to-all-done.5.shares = bf16[16,24,256]{2,1,0:T(8,128)(2,1)S(1)} async-done(((bf16[16,24,256]{2,1,0:T(8,128)(2,1)}), bf16[16,24,256]{2,1,0:T(8,128)(2,1)S(1)}, u32[]{:S(2)}, u32[]{:S(2)}) %all-to-all-start.5) | async-done | bytes 196640 | tf_op jit(solution)/shard_map/all_to_all | solution.py:455
  159.5 3.6 %all-to-all-start.4 = ((bf16[64,48,128]{2,1,0:T(8,128)(2,1)}), bf16[64,48,128]{2,1,0:T(8,128)(2,1)S(1)}, u32[]{:S(2)}, u32[]{:S(2)}) async-start(bf16[64,48,128]{2,1,0:T(8,128)(2,1)} %shard_map.120), calls=%async_computation.4 | async-start | bytes 1572864 | tf_op jit(solution)/shard_map/all_to_all | solution.py:461
  163.1 5.7 %shard_map.123 = f32[43,48,128]{2,1,0:T(8,128)} custom-call(bf16[16,24,256]{2,1,0:T(8,128)(2,1)} %copy-done.9, bf16[4,27,4,64,128]{4,3,2,1,0:T(8,128)(2,1)} %bitcast.133, bf16[384,24]{1,0:T(8,128)(2,1)} %constant.51.clone.spread, f32[43,16,128]{2,1,0:T(8,128)} %get-tuple-element.13.mask), custom_call_target="tpu_custom_call" | custom-call | flops 1000000000 | bytes 4000000 | tf_op jit(solution)/shard_map/pallas_call | solution.py:340
  168.8 5.9 %all-to-all-done.4.came = bf16[64,48,128]{2,1,0:T(8,128)(2,1)S(1)} async-done(((bf16[64,48,128]{2,1,0:T(8,128)(2,1)}), bf16[64,48,128]{2,1,0:T(8,128)(2,1)S(1)}, u32[]{:S(2)}, u32[]{:S(2)}) %all-to-all-start.4) | async-done | bytes 786464 | tf_op jit(solution)/shard_map/all_to_all | solution.py:461
  175.7 4.0 %shard_map.121 = f32[43,48,128]{2,1,0:T(8,128)} custom-call(bf16[64,48,128]{2,1,0:T(8,128)(2,1)} %copy-done.8, bf16[256,256]{1,0:T(8,128)(2,1)} %constant.60.high, bf16[256,256]{1,0:T(8,128)(2,1)} %constant.63.low, f32[43,16,128]{2,1,0:T(8,128)} %get-tuple-element.13.mask), custom_call_target="tpu_custom_call" | custom-call | flops 1000000000 | bytes 4000000 | tf_op jit(solution)/shard_map/pallas_call | solution.py:340
  179.7 2.6 multiply_subtract_fusion.1
  182.3 3.6 %shard_map.124 = bf16[64,48,128]{2,1,0:T(8,128)(2,1)} custom-call(f32[43,48,128]{2,1,0:T(8,128)} %get-tuple-element.8.values, bf16[256,256]{1,0:T(8,128)(2,1)} %constant.56.high, bf16[256,256]{1,0:T(8,128)(2,1)} %constant.59.low), custom_call_target="tpu_custom_call" | custom-call | flops 1000000000 | bytes 4000000 | tf_op jit(solution)/shard_map/pallas_call | solution.py:340
  185.9 3.6 %all-to-all-start.6 = ((bf16[64,48,128]{2,1,0:T(8,128)(2,1)}), bf16[64,48,128]{2,1,0:T(8,128)(2,1)S(1)}, u32[]{:S(2)}, u32[]{:S(2)}) async-start(bf16[64,48,128]{2,1,0:T(8,128)(2,1)} %shard_map.124), calls=%async_computation.6 | async-start | bytes 1572864 | tf_op jit(solution)/shard_map/all_to_all | solution.py:461
  189.5 6.2 %shard_map.127 = bf16[24,256]{1,0:T(8,128)(2,1)} custom-call(f32[43,48,128]{2,1,0:T(8,128)} %get-tuple-element.8.values, bf16[4,27,4,64,128]{4,3,2,1,0:T(8,128)(2,1)} %bitcast.134, bf16[24,96]{1,0:T(8,128)(2,1)} %constant.50.clone.fold), custom_call_target="tpu_custom_call" | custom-call | flops 1000000000 | bytes 4000000 | tf_op jit(solution)/shard_map/pallas_call | solution.py:340
  195.7 5.4 %all-to-all-done.6.came = bf16[64,48,128]{2,1,0:T(8,128)(2,1)S(1)} async-done(((bf16[64,48,128]{2,1,0:T(8,128)(2,1)}), bf16[64,48,128]{2,1,0:T(8,128)(2,1)S(1)}, u32[]{:S(2)}, u32[]{:S(2)}) %all-to-all-start.6) | async-done | bytes 786464 | tf_op jit(solution)/shard_map/all_to_all | solution.py:461
  201.0 1.4 broadcast_in_dim.26
  202.4 3.5 %all-to-all-start.8 = ((bf16[16,24,256]{2,1,0:T(8,128)(2,1)}), bf16[16,24,256]{2,1,0:T(8,128)(2,1)S(1)}, u32[]{:S(2)}, u32[]{:S(2)}) async-start(bf16[16,24,256]{2,1,0:T(8,128)(2,1)} %broadcast_in_dim.26), calls=%async_computation.8 | async-start | bytes 393216 | tf_op jit(solution)/shard_map/all_to_all | solution.py:455
  206.0 3.7 %shard_map.125 = bf16[64,48,128]{2,1,0:T(8,128)(2,1)} custom-call(bf16[64,48,128]{2,1,0:T(8,128)(2,1)} %copy-done.7, f32[64,8,128]{2,1,0:T(8,128)} %bitcast.153), custom_call_target="tpu_custom_call" | custom-call | flops 1000000000 | bytes 4000000 | tf_op jit(solution)/shard_map/pallas_call | solution.py:340
  209.6 4.6 %all-to-all-done.8.shares = bf16[16,24,256]{2,1,0:T(8,128)(2,1)S(1)} async-done(((bf16[16,24,256]{2,1,0:T(8,128)(2,1)}), bf16[16,24,256]{2,1,0:T(8,128)(2,1)S(1)}, u32[]{:S(2)}, u32[]{:S(2)}) %all-to-all-start.8) | async-done | bytes 196640 | tf_op jit(solution)/shard_map/all_to_all | solution.py:455
  214.3 4.3 %all-to-all-start.7 = ((bf16[64,48,128]{2,1,0:T(8,128)(2,1)}), bf16[64,48,128]{2,1,0:T(8,128)(2,1)}, u32[]{:S(2)}, u32[]{:S(2)}) async-start(bf16[64,48,128]{2,1,0:T(8,128)(2,1)} %shard_map.125), calls=%async_computation.7 | async-start | bytes 1572864 | tf_op jit(solution)/shard_map/all_to_all | solution.py:461
  218.6 5.7 %shard_map.128 = f32[43,48,128]{2,1,0:T(8,128)} custom-call(bf16[16,24,256]{2,1,0:T(8,128)(2,1)} %copy-done.10, bf16[4,27,4,64,128]{4,3,2,1,0:T(8,128)(2,1)} %bitcast.135, bf16[384,24]{1,0:T(8,128)(2,1)} %constant.51.clone.spread, f32[43,16,128]{2,1,0:T(8,128)} %get-tuple-element.13.mask), custom_call_target="tpu_custom_call" | custom-call | flops 1000000000 | bytes 4000000 | tf_op jit(solution)/shard_map/pallas_call | solution.py:340
  224.2 5.9 %all-to-all-done.7.came = bf16[64,48,128]{2,1,0:T(8,128)(2,1)} async-done(((bf16[64,48,128]{2,1,0:T(8,128)(2,1)}), bf16[64,48,128]{2,1,0:T(8,128)(2,1)}, u32[]{:S(2)}, u32[]{:S(2)}) %all-to-all-start.7) | async-done | bytes 786464 | tf_op jit(solution)/shard_map/all_to_all | solution.py:461
  230.2 4.0 %shard_map.126 = f32[43,48,128]{2,1,0:T(8,128)} custom-call(bf16[64,48,128]{2,1,0:T(8,128)(2,1)} %all-to-all-done.7.came, bf16[256,256]{1,0:T(8,128)(2,1)} %constant.60.high, bf16[256,256]{1,0:T(8,128)(2,1)} %constant.63.low, f32[43,16,128]{2,1,0:T(8,128)} %get-tuple-element.13.mask), custom_call_target="tpu_custom_call" | custom-call | flops 1000000000 | bytes 4000000 | tf_op jit(solution)/shard_map/pallas_call | solution.py:340
  234.2 2.0 multiply_reduce_fusion.2
  237.3 4.2 %all-to-all-start.9 = ((f32[16,4,3,4]{3,1,2,0:T(4,128)}), f32[16,4,3,4]{3,1,2,0:T(4,128)}, u32[]{:S(2)}, u32[]{:S(2)}) async-start(f32[16,4,3,4]{3,1,2,0:T(4,128)} %broadcast_in_dim.27), calls=%async_computation.9 | async-start | bytes 196608 | tf_op jit(solution)/shard_map/all_to_all | solution.py:455
  241.6 7.7 %all-to-all-done.9 = f32[16,4,3,4]{3,1,2,0:T(4,128)} async-done(((f32[16,4,3,4]{3,1,2,0:T(4,128)}), f32[16,4,3,4]{3,1,2,0:T(4,128)}, u32[]{:S(2)}, u32[]{:S(2)}) %all-to-all-start.9) | async-done | bytes 3104 | tf_op jit(solution)/shard_map/all_to_all | solution.py:455
  249.3 0.9 reduce_sum.89
  250.5 1.9 multiply_add_fusion
  253.3 2.2 pad_maximum_fusion.1
  (93 shorter events, 13.2 us)
Async XLA Ops:
  7.2 88.6 %all-gather.3.cloned.1.call-start = ((), (), s32[]{:S(2)}) async-start(), calls=%async_computation.10 | async-start | bytes 8847360 | tf_op jit(solution)/shard_map/all_gather | solution.py:490
  20.7 0.9 copy-start.5
  26.1 7.3 %copy-start.12 = (f32[3,64,256]{2,1,0:T(8,128)S(1)}, f32[3,64,256]{2,1,0:T(8,128)}, u32[]{:S(2)}) copy-start(f32[3,64,256]{2,1,0:T(8,128)} %param.15) | copy-start | bytes 589828
  26.1 7.4 %copy-start.14 = (f32[3]{0:T(128)S(1)}, f32[3]{0:T(128)}, u32[]{:S(2)}) copy-start(f32[3]{0:T(128)} %param.12) | copy-start | bytes 40
  26.1 18.8 %all-to-all-start = ((f32[64,16,128]{2,1,0:T(8,128)}), f32[64,16,128]{2,1,0:T(8,128)S(1)}, u32[]{:S(2)}, u32[]{:S(2)}) async-start(f32[64,16,128]{2,1,0:T(8,128)} %shard_map.113), calls=%async_computation | async-start | bytes 1048576 | tf_op jit(solution)/shard_map/all_to_all | solution.py:461
  44.9 1.1 copy-start.11
  49.4 26.1 %all-to-all-start.1 = ((f32[64,48,128]{2,1,0:T(8,128)}), f32[64,48,128]{2,1,0:T(8,128)S(1)}, u32[]{:S(2)}, u32[]{:S(2)}) async-start(f32[64,48,128]{2,1,0:T(8,128)} %shard_map.114), calls=%async_computation.1 | async-start | bytes 3145728 | tf_op jit(solution)/shard_map/all_to_all | solution.py:461
  53.1 2.9 %copy-start.15 = (f32[4]{0:T(128)S(1)}, f32[4]{0:T(128)}, u32[]{:S(2)}) copy-start(f32[4]{0:T(128)} %param.11) | copy-start | bytes 52
  75.5 1.1 copy-start.4
  117.7 5.7 %copy-start.2 = (f32[43,48,128]{2,1,0:T(8,128)S(1)}, f32[43,48,128]{2,1,0:T(8,128)}, u32[]{:S(2)}) copy-start(f32[43,48,128]{2,1,0:T(8,128)} %shard_map.115.values) | copy-start | bytes 3170308
  129.5 16.8 %all-to-all-start.3 = ((bf16[64,48,128]{2,1,0:T(8,128)(2,1)}), bf16[64,48,128]{2,1,0:T(8,128)(2,1)S(1)}, u32[]{:S(2)}, u32[]{:S(2)}) async-start(bf16[64,48,128]{2,1,0:T(8,128)(2,1)} %shard_map.119), calls=%async_computation.3 | async-start | bytes 1572864 | tf_op jit(solution)/shard_map/all_to_all | solution.py:461
  133.3 17.9 %copy-start.13 = (f32[64,256]{1,0:T(8,128)S(1)}, f32[64,256]{1,0:T(8,128)}, u32[]{:S(2)}) copy-start(f32[64,256]{1,0:T(8,128)} %param.14) | copy-start | bytes 196612
  146.2 5.8 %copy-start.6 = (bf16[64,48,128]{2,1,0:T(8,128)(2,1)}, bf16[64,48,128]{2,1,0:T(8,128)(2,1)S(1)}, u32[]{:S(2)}) copy-start(bf16[64,48,128]{2,1,0:T(8,128)(2,1)S(1)} %all-to-all-done.3.came) | copy-start | bytes 2359300
  147.7 11.8 %all-to-all-start.5 = ((bf16[16,24,256]{2,1,0:T(8,128)(2,1)}), bf16[16,24,256]{2,1,0:T(8,128)(2,1)S(1)}, u32[]{:S(2)}, u32[]{:S(2)}) async-start(bf16[16,24,256]{2,1,0:T(8,128)(2,1)} %broadcast_in_dim.25), calls=%async_computation.5 | async-start | bytes 393216 | tf_op jit(solution)/shard_map/all_to_all | solution.py:455
  159.5 3.6 %copy-start.9 = (bf16[16,24,256]{2,1,0:T(8,128)(2,1)}, bf16[16,24,256]{2,1,0:T(8,128)(2,1)S(1)}, u32[]{:S(2)}) copy-start(bf16[16,24,256]{2,1,0:T(8,128)(2,1)S(1)} %all-to-all-done.5.shares) | copy-start | bytes 589828
  159.5 15.2 %all-to-all-start.4 = ((bf16[64,48,128]{2,1,0:T(8,128)(2,1)}), bf16[64,48,128]{2,1,0:T(8,128)(2,1)S(1)}, u32[]{:S(2)}, u32[]{:S(2)}) async-start(bf16[64,48,128]{2,1,0:T(8,128)(2,1)} %shard_map.120), calls=%async_computation.4 | async-start | bytes 1572864 | tf_op jit(solution)/shard_map/all_to_all | solution.py:461
  168.8 10.9 %copy-start = (f32[43,48,128]{2,1,0:T(8,128)S(1)}, f32[43,48,128]{2,1,0:T(8,128)}, u32[]{:S(2)}) copy-start(f32[43,48,128]{2,1,0:T(8,128)} %sub.65.values) | copy-start | bytes 3170308
  168.8 10.9 %copy-start.3 = (f32[43,48,128]{2,1,0:T(8,128)S(1)}, f32[43,48,128]{2,1,0:T(8,128)}, u32[]{:S(2)}) copy-start(f32[43,48,128]{2,1,0:T(8,128)} %shard_map.123) | copy-start | bytes 3170308
  174.7 0.9 copy-start.8
  185.9 15.2 %all-to-all-start.6 = ((bf16[64,48,128]{2,1,0:T(8,128)(2,1)}), bf16[64,48,128]{2,1,0:T(8,128)(2,1)S(1)}, u32[]{:S(2)}, u32[]{:S(2)}) async-start(bf16[64,48,128]{2,1,0:T(8,128)(2,1)} %shard_map.124), calls=%async_computation.6 | async-start | bytes 1572864 | tf_op jit(solution)/shard_map/all_to_all | solution.py:461
  201.0 4.9 %copy-start.7 = (bf16[64,48,128]{2,1,0:T(8,128)(2,1)}, bf16[64,48,128]{2,1,0:T(8,128)(2,1)S(1)}, u32[]{:S(2)}) copy-start(bf16[64,48,128]{2,1,0:T(8,128)(2,1)S(1)} %all-to-all-done.6.came) | copy-start | bytes 2359300
  202.4 11.8 %all-to-all-start.8 = ((bf16[16,24,256]{2,1,0:T(8,128)(2,1)}), bf16[16,24,256]{2,1,0:T(8,128)(2,1)S(1)}, u32[]{:S(2)}, u32[]{:S(2)}) async-start(bf16[16,24,256]{2,1,0:T(8,128)(2,1)} %broadcast_in_dim.26), calls=%async_computation.8 | async-start | bytes 393216 | tf_op jit(solution)/shard_map/all_to_all | solution.py:455
  214.3 4.3 %copy-start.10 = (bf16[16,24,256]{2,1,0:T(8,128)(2,1)}, bf16[16,24,256]{2,1,0:T(8,128)(2,1)S(1)}, u32[]{:S(2)}) copy-start(bf16[16,24,256]{2,1,0:T(8,128)(2,1)S(1)} %all-to-all-done.8.shares) | copy-start | bytes 589828
  214.3 15.9 %all-to-all-start.7 = ((bf16[64,48,128]{2,1,0:T(8,128)(2,1)}), bf16[64,48,128]{2,1,0:T(8,128)(2,1)}, u32[]{:S(2)}, u32[]{:S(2)}) async-start(bf16[64,48,128]{2,1,0:T(8,128)(2,1)} %shard_map.125), calls=%async_computation.7 | async-start | bytes 1572864 | tf_op jit(solution)/shard_map/all_to_all | solution.py:461
  224.2 9.9 %copy-start.1 = (f32[43,48,128]{2,1,0:T(8,128)S(1)}, f32[43,48,128]{2,1,0:T(8,128)}, u32[]{:S(2)}) copy-start(f32[43,48,128]{2,1,0:T(8,128)} %shard_map.128) | copy-start | bytes 3170308
  237.3 12.0 %all-to-all-start.9 = ((f32[16,4,3,4]{3,1,2,0:T(4,128)}), f32[16,4,3,4]{3,1,2,0:T(4,128)}, u32[]{:S(2)}, u32[]{:S(2)}) async-start(f32[16,4,3,4]{3,1,2,0:T(4,128)} %broadcast_in_dim.27), calls=%async_computation.9 | async-start | bytes 196608 | tf_op jit(solution)/shard_map/all_to_all | solution.py:455
Sparse Core Ops, SparseCore 0:
  20.9 74.8 all-gather.2

commit v2 on v1

--- a/solution.py
+++ b/solution.py
@@ -116,9 +116,9 @@
     return out
 
 
-def turn_in(src, rows, dst):
+def turn_in(src, dst):
     for s in range(16):
-        tiles = [src[4 * s + c, rows].astype(F32) for c in range(4)]
+        tiles = [src[4 * s + c].astype(F32) for c in range(4)]
         re = corner_turn([t[0:8] for t in tiles])
         im = corner_turn([t[8:16] for t in tiles])
         for c in range(4):
@@ -200,8 +200,8 @@
     dft64(load_kept(near), ALL_SET, tmp, store, 1)
 
 
-def back_tile(src, rows, high, low, near, tmp):
-    turn_in(src, rows, near)
+def back_tile(src, high, low, near, tmp):
+    turn_in(src, near)
 
     def store(n, value):
         tmp2 = near
@@ -258,34 +258,38 @@
     return jnp.where(lax.broadcasted_iota(jnp.int32, shape, len(shape) - 1) < BOX, 1.0, -1.0)
 
 
-def panel_rows(panel, r, p):
-    return jnp.concatenate([panel[b, r, p] for b in range(4)], axis=0)
-
-
-def correlate(values, panel, fold, packed):
+def panel_rows(panel, slots, r, p, both):
+    rows = [jnp.concatenate([panel[d, p, r] for d in slots], axis=0)]
+    if both:
+        rows.append(jnp.concatenate([panel[d, p, r + 1] for d in slots], axis=0))
+    return jnp.concatenate(rows, axis=1)
+
+
+def pack_values(values, packed):
+    sign = lane_sign((48, 2 * BOX))
     for r in range(ROWS):
         straight = pack_row(lambda f: values[place_of[f]], r)
-        turned = pack_row(
-            lambda f: pltpu.roll(values[place_of[f]], BOX, 1) * lane_sign((48, 2 * BOX)), r
-        )
+        turned = pack_row(lambda f: pltpu.roll(values[place_of[f]], BOX, 1) * sign, r)
         packed[r] = jnp.concatenate([straight, turned], axis=0).astype(BF16)
+
+
+def correlate(packed, panel, fold, slots):
+    count = 64 * len(slots)
+    nt = (((1,), (1,)), ((), ()))
     total = [None] * 4
     for r in range(0, ROWS, 2):
         both = r + 1 < ROWS
         y = jnp.concatenate([packed[r], packed[r + 1]], axis=1) if both else packed[r]
         for p in range(4):
-            o = panel_rows(panel, r, p)
-            if both:
-                o = jnp.concatenate([o, panel_rows(panel, r + 1, p)], axis=1)
-            part = lax.dot_general(o, y, (((1,), (1,)), ((), ())), preferred_element_type=F32)
+            o = panel_rows(panel, slots, r, p, both)
+            part = lax.dot_general(o, y, nt, preferred_element_type=F32)
             total[p] = part if total[p] is None else total[p] + part
-    column = lax.broadcasted_iota(jnp.int32, (256, 96), 1) % 16 // 4
+    column = lax.broadcasted_iota(jnp.int32, (count, 96), 1) % 16 // 4
     chosen = total[0]
     for p in range(1, 4):
         chosen = jnp.where(column == 2 * (p % 2) + p // 2, total[p], chosen)
     hi = chosen.astype(BF16)
     lo = (chosen - hi.astype(F32)).astype(BF16)
-    nt = (((1,), (1,)), ((), ()))
     return lax.dot_general(fold, hi, nt, preferred_element_type=F32) + lax.dot_general(
         fold, lo, nt, preferred_element_type=F32
     )
@@ -317,9 +321,7 @@
         both = r + 1 < ROWS
         total = None
         for p in range(4):
-            o = panel_rows(panel, r, p)
-            if both:
-                o = jnp.concatenate([o, panel_rows(panel, r + 1, p)], axis=1)
+            o = panel_rows(panel, SLOTS, r, p, both)
             part = jnp.dot(rows[96 * p : 96 * p + 96], o, preferred_element_type=F32)
             total = part if total is None else total + part
         for c in range(2 if both else 1):
@@ -331,53 +333,121 @@
         finish(place_of[f], unpack_row(lambda r: product[r], f))
 
 
-VMEM_LIMIT = 60 * 1024 * 1024
+VMEM_LIMIT = 62 * 1024 * 1024
+MESH = pl.DeviceIdType.MESH
 vmem = pl.BlockSpec(memory_space=pltpu.VMEM)
-TILE = pltpu.VMEM((BOX, 16, 2 * BOX), F32)
-
-
-def call(body, outs, args, scratch=(), flops=10**9):
-    return pl.pallas_call(
-        body,
-        out_shape=outs,
-        in_specs=[vmem] * len(args),
-        out_specs=jax.tree.map(lambda _: vmem, outs),
-        scratch_shapes=list(scratch),
-        compiler_params=pltpu.CompilerParams(vmem_limit_bytes=VMEM_LIMIT),
-        cost_estimate=pl.CostEstimate(flops=flops, bytes_accessed=4 * 10**6, transcendentals=0),
-    )(*args)
+STEP = 72
+SLOTS = (0, 1, 3, 2)
 
 
 def shape(dims, dtype=F32):
     return jax.ShapeDtypeStruct(dims, dtype)
 
 
-def pack_body(psi, mask, out):
-    for r in range(ROWS):
-        get = lambda f: psi[0, f % BOX].astype(F32) * mask[0, f % BOX]
-        out[r, 0] = pack_row(get, r).astype(BF16)
-
-
-def pack_panel(psi, mask):
-    bands = psi.shape[2]
-    return pl.pallas_call(
-        pack_body,
-        grid=(4,),
-        out_shape=shape((ROWS, 4, bands, 2 * BOX), BF16),
-        in_specs=[
-            pl.BlockSpec((1, BOX, bands, 2 * BOX), lambda p: (p, 0, 0, 0)),
-            pl.BlockSpec((1, BOX, 1, 2 * BOX), lambda p: (p, 0, 0, 0)),
-        ],
-        out_specs=pl.BlockSpec((ROWS, 1, bands, 2 * BOX), lambda p: (0, p, 0, 0)),
-    )(psi, mask)
-
-
-def source_forward_body(solved, high, low, out, near, tmp):
-    forward_tile(solved, 0, high[...], low[...], near, tmp, put_pair(out, slice(0, 16), F32))
-
-
-def source_middle_body(came, changes, out, near, tmp, space):
-    turn_in(came, slice(0, 16), near)
+def remote(src, dst, send, recv, where):
+    return pltpu.make_async_remote_copy(
+        src_ref=src, dst_ref=dst, send_sem=send, recv_sem=recv, device_id=where, device_id_type=MESH
+    )
+
+
+def to_peers(me, src_of, dst, send, recv):
+    def one(k, carry):
+        g = lax.rem(me + k, 16)
+        remote(src_of(g), dst, send, recv, {"ga": g}).start()
+        return carry
+
+    lax.fori_loop(1, 16, one, 0)
+
+
+def kernel(
+    psi, mask_rows, solved, fwd_hi, fwd_lo, back_hi, back_lo, changes, potential, mask, level,
+    fold, spread,
+    response, residual,
+    raw, wide_rows, panel, near, tmp, space, send_a, came_a, send_b, came_b, send_1, send_2,
+    came_1, came_2, packed, product, share, shares, source, vec, image, sums, all_sums,
+    raw_sem, ring_send, ring_recv, a_sem, b_send, b_recv, s1, r1, s2, r2, c_send, c_recv, m_sem,
+):
+    me = lax.axis_index("ga")
+    z = lax.axis_index("band")
+    up, down = lax.rem(z + 1, 4), lax.rem(z + 3, 4)
+
+    barrier = pltpu.get_barrier_semaphore()
+
+    def greet(k, carry):
+        pl.semaphore_signal(
+            barrier, inc=1, device_id={"ga": lax.rem(me + k, 16)}, device_id_type=MESH
+        )
+        return carry
+
+    lax.fori_loop(1, 16, greet, 0)
+    for other in (up, down):
+        pl.semaphore_signal(barrier, inc=1, device_id={"band": other}, device_id_type=MESH)
+
+    def raw_copy(p):
+        return pltpu.make_async_copy(psi.at[:, p], raw.at[p], raw_sem.at[p])
+
+    for p in range(4):
+        raw_copy(p).start()
+
+    forward_tile(solved, 0, fwd_hi[...], fwd_lo[...], near, tmp, put_pair(send_a, slice(0, 16), F32))
+    pl.semaphore_wait(barrier, 17)
+
+    mine = pl.ds(4 * me, 4)
+    to_peers(me, lambda g: send_a.at[pl.ds(4 * g, 4)], came_a.at[mine], a_sem.at[0], a_sem.at[1])
+    came_a[mine] = send_a[mine]
+
+    def ring(src_slot, dst_slot, p, where, n):
+        return remote(
+            panel.at[src_slot, p], panel.at[dst_slot, p], ring_send.at[n], ring_recv.at[dst_slot, p],
+            {"band": where},
+        )
+
+    def ring_up(p):
+        return ring(0, 3, p, up, p)
+
+    def ring_down(p):
+        return ring(0, 1, p, down, 4 + p)
+
+    def pack_plane(u, carry):
+        p = 2 * lax.rem(u, 2) + u // 2
+        raw_copy(p).wait()
+
+        def widen(m, c):
+            wide_rows[pl.ds(pl.multiple_of(STEP * m, 8), BOX), :] = raw[p, m].astype(F32)
+            return c
+
+        lax.fori_loop(0, 64, widen, 0)
+
+        def get(f):
+            n = f % BOX
+            return wide_rows[pl.ds(n, 64, stride=STEP), :] * mask_rows[p, n : n + 1]
+
+        for r in range(ROWS):
+            panel[0, p, r] = pack_row(get, r).astype(BF16)
+
+        @pl.when(lax.rem(u, 2) == 0)
+        def _():
+            ring_up(p).start()
+
+        @pl.when(lax.rem(u, 2) == 1)
+        def _():
+            ring_down(p).start()
+
+        return carry
+
+    lax.fori_loop(0, 4, pack_plane, 0)
+    ring_up(2).start()
+    ring_down(0).start()
+    ring_up(3).start()
+    ring_down(1).start()
+
+    def wait_all(src, dst, send, recv):
+        return remote(src, dst, send, recv, {"ga": lax.rem(me + 1, 16)})
+
+    every = pl.ds(0, 60)
+    wait_all(send_a.at[every], came_a.at[every], a_sem.at[0], a_sem.at[1]).wait()
+
+    turn_in(came_a, near)
 
     def keep(n, value):
         space[n, 0:8] = value[0]
@@ -385,80 +455,228 @@
 
     dft64(pair(near), ALL_SET, tmp, keep, 1)
 
-    def each(p, carry):
+    def each_change(p, carry):
         def load(n):
             d = changes[p, n]
             return (space[n, 0:8] * d, space[n, 8:16] * d)
 
-        rows = pl.ds(pl.multiple_of(16 * p, 16), 16)
-        dft64(load, ALL_SET, tmp, put_pair(out, rows, F32), -1)
+        dft64(load, ALL_SET, tmp, put_pair(send_b.at[p], slice(0, 16), F32), -1)
+        to_peers(
+            me, lambda g: send_b.at[p, pl.ds(4 * g, 4)], came_b.at[p, mine], b_send.at[p], b_recv.at[p]
+        )
+        came_b[p, mine] = send_b[p, mine]
         return carry
 
-    lax.fori_loop(0, NPERT, each, 0)
-
-
-def back_body(came, high, low, mask, out, near, tmp):
-    def each(t, carry):
+    lax.fori_loop(0, NPERT, each_change, 0)
+
+    def pass_on(p_up, p_down):
+        ring(0, 3, p_up, up, p_up).wait_recv()
+        first = ring(3, 2, p_up, up, 8 + p_up)
+        first.start()
+        ring(0, 1, p_down, down, 4 + p_down).wait_recv()
+        second = ring(1, 2, p_down, down, 8 + p_down)
+        second.start()
+
+    pass_on(0, 2)
+    pass_on(1, 3)
+
+    def back(came, dst_add):
+        def each(t, carry):
+            dst_add(t)
+            return carry
+
+        lax.fori_loop(0, 3, each, 0)
+
+    def source_tile(t):
+        wait_all(send_b.at[t, every], came_b.at[t, every], b_send.at[t], b_recv.at[t]).wait()
         start = pl.multiple_of(16 * t, 16)
-        a, b = back_tile(came, pl.ds(start, 16), high[...], low[...], near, tmp)
-        out[:, pl.ds(start, 8), :] = a * mask[:, 0:8, :]
-        out[:, pl.ds(start + 8, 8), :] = b * mask[:, 8:16, :]
+        a, b = back_tile(came_b.at[t], back_hi[...], back_lo[...], near, tmp)
+        source[:, pl.ds(start, 8), :] = a * mask[:, 0:8, :]
+        source[:, pl.ds(start + 8, 8), :] = b * mask[:, 8:16, :]
+
+    back(came_b, source_tile)
+
+    def send_share(n, src):
+        to_peers(me, lambda g: src, shares.at[n, me], c_send.at[n], c_recv.at[n])
+
+    def total_share(n):
+        first = pl.ds(0, 15)
+        wait_all(shares.at[n, first], shares.at[n, first], c_send.at[n], c_recv.at[n]).wait()
+        total = shares[n, 0].astype(F32)
+        for g in range(1, 16):
+            total = total + shares[n, g].astype(F32)
+        return total.astype(BF16)
+
+    pack_values(source, packed)
+    for p in range(2, 4):
+        ring(0, 3, p, up, p).wait_recv()
+    for p in range(2):
+        ring(0, 1, p, down, 4 + p).wait_recv()
+    early = correlate(packed, panel, fold[...], SLOTS[:3])
+    for p in range(2):
+        ring(3, 2, p, up, 8 + p).wait_recv()
+    for p in range(2, 4):
+        ring(1, 2, p, down, 8 + p).wait_recv()
+    late = correlate(packed, panel, fold[...], SLOTS[3:])
+    share[0] = jnp.concatenate([early, late], axis=1).astype(BF16)
+    shares[0, me] = share[0]
+    send_share(0, share.at[0])
+
+    def first_row(place, row):
+        for t in range(3):
+            rows = slice(16 * t, 16 * t + 16)
+            vec[0, place, rows] = row[rows] * mask[place] - source[place, rows]
+
+    combine(total_share(0), panel, spread, product, first_row)
+
+    def apply(it, carry):
+        def near_tile(t, c):
+            start = pl.multiple_of(16 * t, 16)
+            forward_tile(
+                vec.at[it], start, fwd_hi[...], fwd_lo[...], near, tmp,
+                put_pair(send_1.at[it, t], slice(0, 16), BF16),
+            )
+            to_peers(
+                me, lambda g: send_1.at[it, t, pl.ds(4 * g, 4)], came_1.at[it, t, mine],
+                s1.at[it, t], r1.at[it, t],
+            )
+            came_1[it, t, mine] = send_1[it, t, mine]
+            return c
+
+        lax.fori_loop(0, 3, near_tile, 0)
+
+        pack_values(vec.at[it], packed)
+        n = it + 1
+        share[n] = correlate(packed, panel, fold[...], SLOTS).astype(BF16)
+        shares[n, me] = share[n]
+        send_share(n, share.at[n])
+
+        def space_tile(t, c):
+            wait_all(send_1.at[it, t, every], came_1.at[it, t, every], s1.at[it, t], r1.at[it, t]).wait()
+            turn_in(came_1.at[it, t], near)
+
+            def with_potential(k, value):
+                v = potential[k]
+                near[k, 0:8] = value[0] * v
+                near[k, 8:16] = value[1] * v
+
+            dft64(pair(near), ALL_SET, tmp, with_potential, 1)
+            dft64(pair(near), ALL_SET, tmp, put_pair(send_2.at[it, t], slice(0, 16), BF16), -1)
+            to_peers(
+                me, lambda g: send_2.at[it, t, pl.ds(4 * g, 4)], came_2.at[it, t, mine],
+                s2.at[it, t], r2.at[it, t],
+            )
+            came_2[it, t, mine] = send_2[it, t, mine]
+            return c
+
+        lax.fori_loop(0, 3, space_tile, 0)
+
+        def with_level(place, row):
+            for t in range(3):
+                rows = slice(16 * t, 16 * t + 16)
+                image[it, place, rows] = (
+                    row[rows] * (shift_weight * mask[place])
+                    + level[place] * vec[it, place, rows]
+                )
+
+        combine(total_share(n), panel, spread, product, with_level)
+
+        def far_tile(t, c):
+            wait_all(send_2.at[it, t, every], came_2.at[it, t, every], s2.at[it, t], r2.at[it, t]).wait()
+            start = pl.multiple_of(16 * t, 16)
+            a, b = back_tile(came_2.at[it, t], back_hi[...], back_lo[...], near, tmp)
+            for half, value in ((0, a), (8, b)):
+                rows = pl.ds(start + half, 8)
+                total = image[it, :, rows, :] + value * mask[:, half : half + 8, :]
+                image[it, :, rows, :] = total
+                vec[it + 1, :, rows, :] = total - SHIFT * vec[it, :, rows, :]
+            return c
+
+        lax.fori_loop(0, 3, far_tile, 0)
         return carry
 
-    lax.fori_loop(0, 3, each, 0)
-
-
-def forward_body(values, high, low, out, near, tmp):
-    def each(t, carry):
-        start = pl.multiple_of(16 * t, 16)
-        forward_tile(values, start, high[...], low[...], near, tmp, put_pair(out, pl.ds(start, 16), BF16))
-        return carry
-
-    lax.fori_loop(0, 3, each, 0)
-
-
-def middle_body(came, potential, out, near, tmp):
-    def each(t, carry):
-        rows = pl.ds(pl.multiple_of(16 * t, 16), 16)
-        turn_in(came, rows, near)
-
-        def keep(n, value):
-            v = potential[n]
-            near[n, 0:8] = value[0] * v
-            near[n, 8:16] = value[1] * v
-
-        dft64(pair(near), ALL_SET, tmp, keep, 1)
-        dft64(pair(near), ALL_SET, tmp, put_pair(out, rows, BF16), -1)
-        return carry
-
-    lax.fori_loop(0, 3, each, 0)
-
-
-def correlate_body(values, panel, fold, out, packed):
-    out[...] = correlate(values, panel, fold[...], packed).astype(BF16)
-
-
-def combine_body(shares, panel, spread, mask, out, product):
-    total = shares[0].astype(F32)
-    for s in range(1, 16):
-        total = total + shares[s].astype(F32)
-
-    def finish(place, row):
+    lax.fori_loop(0, 2, apply, 0)
+
+    def moments(place, totals):
+        b, ab, w, aw = vec[0, place], image[0, place], vec[1, place], image[1, place]
+        return tuple(x + y for x, y in zip(totals, (b * b, b * ab, ab * ab, w * aw)))
+
+    zero = jnp.zeros((48, 2 * BOX), F32)
+    totals = lax.fori_loop(0, KEPT, moments, (zero,) * 4)
+    lane = lax.broadcasted_iota(jnp.int32, (8, 2 * BOX), 1)
+    own = jnp.zeros((8, 2 * BOX), F32)
+    for m, total in enumerate(totals):
+        line = jnp.sum(total, axis=1, keepdims=True) / BOX**3
         for t in range(3):
-            out[place, 16 * t : 16 * t + 16] = row[16 * t : 16 * t + 16] * mask[place]
-
-    combine(total.astype(BF16), panel, spread, product, finish)
-
-
-def copy_for_each(shard, axis):
-    size = lax.axis_size(axis)
-    return lax.all_to_all(
-        jnp.broadcast_to(shard[None], (size, *shard.shape)), axis, 0, 0, tiled=True
-    )
-
-
-def swap(values):
-    return lax.all_to_all(values, "ga", split_axis=0, concat_axis=0, tiled=True)
+            both = line[16 * t : 16 * t + 8] + line[16 * t + 8 : 16 * t + 16]
+            own = jnp.where(lane == 4 * t + m, jnp.broadcast_to(both, own.shape), own)
+    own = own + pltpu.roll(own, 4, 0)
+    sums[...] = own
+    all_sums[me] = own
+    to_peers(me, lambda g: sums, all_sums.at[me], m_sem.at[0], m_sem.at[1])
+    first = pl.ds(0, 15)
+    wait_all(all_sums.at[first], all_sums.at[first], m_sem.at[0], m_sem.at[1]).wait()
+    m0 = all_sums[0]
+    for g in range(1, 16):
+        m0 = m0 + all_sums[g]
+    m1, m2, m3 = (pltpu.roll(m0, 2 * BOX - n, 1) for n in (1, 2, 3))
+    step0 = m0 / m1
+    fresh = m0 - 2.0 * step0 * m1 + step0 * step0 * m2
+    u = 1.0 + fresh / m0 - step0 * SHIFT
+    curve = u * u * m1 - 2.0 * u * step0 * (m2 - SHIFT * m1) + step0 * step0 * m3
+    step1 = fresh / curve
+    low_part, high_part = step0 + step1 * u, step1 * step0
+    for t in range(3):
+        a = jnp.broadcast_to(low_part[:, 4 * t : 4 * t + 1], (8, 2 * BOX))
+        e = jnp.broadcast_to(high_part[:, 4 * t : 4 * t + 1], (8, 2 * BOX))
+        for half in (0, 8):
+            rows = slice(16 * t + half, 16 * t + half + 8)
+            b, ab = vec[0, :, rows, :], image[0, :, rows, :]
+            response[:, rows, :] = a * b - e * vec[1, :, rows, :]
+            residual[:, rows, :] = b - a * ab + e * image[1, :, rows, :]
+
+    for p in range(4):
+        ring_up(p).wait_send()
+        ring_down(p).wait_send()
+    for p in range(2):
+        ring(3, 2, p, up, 8 + p).wait_send()
+    for p in range(2, 4):
+        ring(1, 2, p, down, 8 + p).wait_send()
+
+
+def run(*args):
+    grid_f = pltpu.VMEM((BOX, 16, 2 * BOX), F32)
+    three_f = pltpu.VMEM((3, BOX, 16, 2 * BOX), F32)
+    six_b = pltpu.VMEM((2, 3, BOX, 16, 2 * BOX), BF16)
+    natural = (KEPT, 48, 2 * BOX)
+    dma = pltpu.SemaphoreType.DMA
+    return pl.pallas_call(
+        kernel,
+        out_shape=(shape(natural), shape(natural)),
+        in_specs=[pl.BlockSpec(memory_space=pl.ANY)] + [vmem] * (len(args) - 1),
+        out_specs=(vmem, vmem),
+        scratch_shapes=[
+            pltpu.VMEM((4, 64, BOX, 2 * BOX), BF16),
+            pltpu.VMEM((64 * STEP, 2 * BOX), F32),
+            pltpu.VMEM((4, 4, ROWS, 64, 2 * BOX), BF16),
+            grid_f, grid_f, grid_f,
+            grid_f, grid_f, three_f, three_f, six_b, six_b, six_b, six_b,
+            pltpu.VMEM((ROWS, 96, 2 * BOX), BF16),
+            pltpu.VMEM((ROWS, 48, 2 * BOX), F32),
+            pltpu.VMEM((3, 24, 256), BF16),
+            pltpu.VMEM((3, 16, 24, 256), BF16),
+            pltpu.VMEM(natural, F32),
+            pltpu.VMEM((3, *natural), F32),
+            pltpu.VMEM((2, *natural), F32),
+            pltpu.VMEM((8, 2 * BOX), F32),
+            pltpu.VMEM((16, 8, 2 * BOX), F32),
+            dma((4,)), dma((12,)), dma((4, 4)), dma((2,)), dma((3,)), dma((3,)),
+            dma((2, 3)), dma((2, 3)), dma((2, 3)), dma((2, 3)), dma((3,)), dma((3,)), dma((2,)),
+        ],
+        compiler_params=pltpu.CompilerParams(
+            vmem_limit_bytes=VMEM_LIMIT, collective_id=0, has_side_effects=True
+        ),
+    )(*args)
 
 
 def rows_of_planes(values):
@@ -482,80 +700,20 @@
     kinetic = jnp.concatenate([kinetic, kinetic], axis=-1)
     sphere = g_mask.reshape(planes, BOX, BOX).astype(F32)
     sphere = jnp.concatenate([sphere, sphere], axis=-1)
-    tables = lane_tables()
-    fold = jnp.asarray(fold_table(), BF16)
-    spread = jnp.asarray(spread_table(), BF16)
-
-    packed = pack_panel(psi_occ.transpose(1, 2, 0, 3), sphere[:, :, None, :])
-    panel = lax.all_gather(packed, "band", axis=0, tiled=False)
-
-    mask4 = rows_of_planes(sphere)
-    mask = jnp.repeat(mask4, 4, axis=1)
+    mask = jnp.repeat(rows_of_planes(sphere), 4, axis=1)
     level = (rows_of_planes(kinetic)[:, :, None, :] - energies[None, None, :, None]).reshape(
         KEPT, 16, 2 * BOX
     ) * mask
-    mask_scaled = mask / BOX**3
     solved = psi_occ[::STRIDE].astype(F32) * sphere[None]
     solved = solved.reshape(4, 2, 2, BOX, 2 * BOX).transpose(3, 2, 1, 0, 4).reshape(BOX, 16, 2 * BOX)
     solved = jnp.concatenate([solved[: GCUT + 1], solved[BOX - GCUT :]], axis=0)
     potential = jnp.repeat(v_local.reshape(BOX, 2, 2 * BOX), 4, axis=1)
     changes = jnp.repeat(dv.reshape(NPERT, BOX, 2, 2 * BOX), 4, axis=2)
 
-    grid_bf = shape((BOX, 48, 2 * BOX), BF16)
-    grid_f = shape((BOX, 48, 2 * BOX), F32)
-    natural = shape((KEPT, 48, 2 * BOX))
-
-    def project(values):
-        share = call(
-            correlate_body, shape((24, 256), BF16), (values, panel, fold),
-            [pltpu.VMEM((ROWS, 96, 2 * BOX), BF16)],
-        )
-        return call(
-            combine_body, natural, (copy_for_each(share, "ga"), panel, spread, mask_scaled),
-            [pltpu.VMEM((ROWS, 48, 2 * BOX), F32)],
-        )
-
-    def grid_potential(values):
-        sent = call(forward_body, grid_bf, (values, tables[0], tables[1]), [TILE, TILE])
-        sent = call(middle_body, grid_bf, (swap(sent), potential), [TILE, TILE])
-        return call(back_body, natural, (swap(sent), tables[2], tables[3], mask_scaled), [TILE, TILE])
-
-    sent = call(source_forward_body, shape((BOX, 16, 2 * BOX)), (solved, tables[0], tables[1]), [TILE, TILE])
-    sent = call(source_middle_body, grid_f, (swap(sent), changes), [TILE, TILE, TILE])
-    source = call(back_body, natural, (swap(sent), tables[2], tables[3], mask_scaled), [TILE, TILE])
-
-    def by_tile(values):
-        return values.reshape(KEPT, 3, 16, 2 * BOX)
-
-    def apply(values):
-        local = grid_potential(values)
-        return (
-            (by_tile(values) * level[:, None]).reshape(values.shape)
-            + local
-            + shift_weight * project(values)
-        )
-
-    def inner(a, b):
-        total = jnp.sum(a * b, axis=(0, 2)).reshape(3, 4, 4)
-        return jnp.sum(total, axis=1) / BOX**3
-
-    first = project(source) - source
-    image = apply(first)
-    second = image - SHIFT * first
-    other = apply(second)
-    sums = jnp.stack([inner(first, first), inner(first, image), inner(image, image), inner(second, other)])
-    m0, m1, m2, m3 = jnp.sum(copy_for_each(sums, "ga"), axis=0)
-    step0 = m0 / m1
-    fresh = m0 - 2.0 * step0 * m1 + step0 * step0 * m2
-    u = 1.0 + fresh / m0 - step0 * SHIFT
-    curve = u * u * m1 - 2.0 * u * step0 * (m2 - SHIFT * m1) + step0 * step0 * m3
-    step1 = fresh / curve
-
-    def each(v):
-        return jnp.repeat(v[:, None, :], 4, axis=1).reshape(48)[None, :, None]
-
-    response = each(step0 + step1 * u) * first - each(step1 * step0) * second
-    residual = first - each(step0 + step1 * u) * image + each(step1 * step0) * other
+    response, residual = run(
+        psi_occ, sphere, solved, *lane_tables(), changes, potential, mask / BOX**3, level,
+        jnp.asarray(fold_table(), BF16), jnp.asarray(spread_table(), BF16),
+    )
 
     def placed(values):
         values = values.reshape(KEPT, 3, 2, 2, 4, 2 * BOX).transpose(4, 1, 3, 2, 0, 5)

time: 264 us -> 145 us (0.55)
  waiting for transfers between devices: 84.3 us -> 0 us
  Pallas kernels: 73 us -> 128 us
  starting transfers between devices: 37.5 us -> 0 us
  blocking collectives: 15.1 us -> 0 us
  between operations: 14.5 us -> 0.89 us
  local copies, waits for them, and re-layouts: 19.1 us -> 8.12 us
  other arithmetic: 18.8 us -> 7.89 us
    all_to_all x9 -> x0, waiting for transfers between devices: 69.4 us -> none  [the longest x6 53.2 us: swap(): return lax.all_to_all(values, 'ga', split_axis=0, concat_axis=0, tiled=True)]
    pallas_call x16 -> x1, Pallas kernels: 73 us -> 128 us  [run(): pl.pallas_call(kernel, out_shape=(shape(natural), shape(natural)), in_spe...]
    all_to_all x9 -> x0, starting transfers between devices: 37.5 us -> none  [the longest x6 26.3 us: swap(): return lax.all_to_all(values, 'ga', split_axis=0, concat_axis=0, tiled=True)]
    all_to_all x1 -> x0, blocking collectives: 15.1 us -> none  [copy_for_each(): lax.all_to_all(jnp.broadcast_to(shard[None], (size, *shard.shape)), axis,...]
    all_gather x1 -> x0, waiting for transfers between devices: 14.9 us -> none  [on_device(): panel = lax.all_gather(packed, 'band', axis=0, tiled=False)]
    unnamed x33 -> x6, local copies, waits for them, and re-layouts: 9.84 us -> 0.01 us
    sub x2 -> x0, other arithmetic: 5.01 us -> none  [the longest x1 2.6 us: on_device(): second = image - SHIFT * first]
    broadcast_in_dim x7 -> x1, local copies, waits for them, and re-layouts: 4.26 us -> 0.06 us  [on_device(): mask = jnp.repeat(rows_of_planes(sphere), 4, axis=1)]
  transfers between devices with their start and end apart: 10 -> 0, of which waited for: 10 -> 0; matrix products, arithmetic and copies ran while one was open for 3% -> 0% of each run, Pallas kernels for 16% -> 0%
where the time goes in v2:
time: 145 us
  Pallas kernels  128 us (88%)
  local copies, waits for them, and re-layouts  8.12 us (6%)
  other arithmetic  7.89 us (5%)
    pallas_call x1, Pallas kernels, run(): pl.pallas_call(kernel, out_shape=(shape(natural), shape(natural)), in_spe...  128 us

profile of v2, /device:TPU:0, one launch (start us, length us, event | category | flops | bytes accessed | tf_op | source)
XLA Modules:
  0.0 145.0 jit_solution(1521593454785686029)
XLA Ops:
  0.6 0.0 copy-start.2
  0.7 0.1 pad.4.clone
  0.7 1.4 fusion.4
  2.2 0.7 add_multiply_fusion.2
  2.8 0.7 fusion.2
  3.5 0.7 add_multiply_fusion.1
  4.2 0.7 sub.41
  4.8 0.1 sub.42
  4.9 0.1 broadcast_add_fusion
  5.1 0.2 add_multiply_fusion
  5.3 0.2 maximum_bitcast_fusion.1
  5.5 0.9 convert_element_type.53
  6.4 0.9 reshape.140
  7.3 0.1 convert_element_type.62
  7.4 0.1 copy.16
  7.5 0.2 maximum_bitcast_fusion
  7.8 0.1 convert_element_type.54
  7.9 0.1 pad_maximum_fusion.3.mask_rows
  8.0 0.0 copy-start
  8.0 0.8 broadcast_in_dim.7
  8.8 0.0 copy-done.2
  8.8 0.1 reshape.138
  8.9 0.1 broadcast_in_dim.8
  9.0 0.1 sub.39
  9.0 1.0 convert_multiply_fusion
  10.0 0.3 copy.21
  10.4 0.0 copy-done
  10.4 1.0 subtract_multiply_fusion
  11.4 1.0 broadcast_in_dim.6
  12.4 128.1 %shard_map.113 = (f32[43,48,128]{2,1,0:T(8,128)}, f32[43,48,128]{2,1,0:T(8,128)}) custom-call(bf16[64,4,64,128]{3,2,1,0:T(8,128)(2,1)} %psi.1, f32[4,64,128]{2,1,0:T(8,128)} %copy-done, f32[43,16,128]{2,1,0:T(8,128)} %get-tuple-element.13.solved, bf16[256,256]{1,0:T(8,128)(2,1)} %constant.41.fwd_hi, bf16[256,256]{1,0:T(8,128)(2,1)} %constant.44.fwd_lo, ...), custom_call_target="tpu_custom_call" | custom-call | tf_op jit(solution)/shard_map/pallas_call | solution.py:653
  140.5 0.0 copy-start.1
  140.5 1.7 %copy.19 = f32[4,3,2,2,43,128]{5,4,3,2,1,0:T(8,128)S(1)} copy(f32[4,3,2,2,43,128]{5,0,2,3,1,4:T(4,128)} %bitcast.40) | data formatting | bytes 2113536 | tf_op jit(solution)/shard_map/transpose | solution.py:719
  142.2 0.0 copy-done.1
  142.2 0.4 copy.18
  142.6 0.1 slice.87
  142.7 0.1 slice.89
  142.8 2.2 %pad_maximum_fusion.1 = (f32[4,3,4,64,128]{4,3,2,1,0:T(8,128)}, f32[4,3,4,64,128]{4,3,2,1,0:T(8,128)}) fusion(f32[4,3,4,21,128]{4,3,2,1,0:T(8,128)S(1)} %slice.89, f32[4,3,4,22,128]{4,3,2,1,0:T(8,128)S(1)} %slice.88, f32[64]{0:T(128)S(1)} %pad.4.clone, f32[4,3,4,21,128]{4,3,2,1,0:T(8,128)S(1)} %slice.87, f32[4,3,4,22,128]{4,3,2,1,0:T(8,128)S(1)} %slice.86), kind=kLoop, calls=%fused_computation.1 | loop fusion | flops 1572864 | bytes 5259520 | tf_op jit(solution)/shard_map/concatenate | solution.py:722
  (11 shorter events, 0.2 us)
Async XLA Ops:
  0.6 8.2 %copy-start.2 = (f32[3,64,256]{2,1,0:T(8,128)S(1)}, f32[3,64,256]{2,1,0:T(8,128)}, u32[]{:S(2)}) copy-start(f32[3,64,256]{2,1,0:T(8,128)} %param.15) | copy-start | bytes 589828
  8.0 2.4 %copy-start = (f32[4,64,128]{2,1,0:T(8,128)}, f32[4,64,128]{2,1,0:T(8,128)S(1)}, u32[]{:S(2)}) copy-start(f32[4,64,128]{2,1,0:T(8,128)S(1)} %pad_maximum_fusion.3.mask_rows) | copy-start | bytes 393220
  140.5 1.7 %copy-start.1 = (f32[43,48,128]{2,1,0:T(8,128)S(1)}, f32[43,48,128]{2,1,0:T(8,128)}, u32[]{:S(2)}) copy-start(f32[43,48,128]{2,1,0:T(8,128)} %get-tuple-element.4) | copy-start | bytes 3170308

commit v3 on v2

--- a/solution.py
+++ b/solution.py
@@ -336,6 +336,7 @@
 VMEM_LIMIT = 62 * 1024 * 1024
 MESH = pl.DeviceIdType.MESH
 vmem = pl.BlockSpec(memory_space=pltpu.VMEM)
+smem = pl.BlockSpec(memory_space=pltpu.SMEM)
 STEP = 72
 SLOTS = (0, 1, 3, 2)
 
@@ -360,11 +361,10 @@
 
 
 def kernel(
-    psi, mask_rows, solved, fwd_hi, fwd_lo, back_hi, back_lo, changes, potential, mask, level,
-    fold, spread,
+    psi, g_mask, v_local, dv, energies, k_point, fwd_hi, fwd_lo, back_hi, back_lo, fold, spread,
     response, residual,
-    raw, wide_rows, panel, near, tmp, space, send_a, came_a, send_b, came_b, send_1, send_2,
-    came_1, came_2, packed, product, share, shares, source, vec, image, sums, all_sums,
+    raw, mask_rows, mask, level, solved, changes, potential, solved_rows, weights, wide_rows, panel, near, tmp, space, send_a, came_a, send_b, came_b, send_1, send_2,
+    came_1, came_2, packed, product, share, shares, source, vec, image, sums, sums_here, all_sums,
     raw_sem, ring_send, ring_recv, a_sem, b_send, b_recv, s1, r1, s2, r2, c_send, c_recv, m_sem,
 ):
     me = lax.axis_index("ga")
@@ -389,12 +389,38 @@
     for p in range(4):
         raw_copy(p).start()
 
-    forward_tile(solved, 0, fwd_hi[...], fwd_lo[...], near, tmp, put_pair(send_a, slice(0, 16), F32))
+    front = lax.broadcasted_iota(jnp.int32, (4, 2 * BOX), 1) < BOX
+    top = lax.broadcasted_iota(jnp.int32, (8, 2 * BOX), 0) < 4
+    for c in range(BOX // 2):
+        both = g_mask[:, 2 * BOX * c : 2 * BOX * (c + 1)].astype(F32)
+        turned = pltpu.roll(both, BOX, 1)
+        for n, rows in ((2 * c, jnp.where(front, both, turned)), (2 * c + 1, jnp.where(front, turned, both))):
+            for p in range(4):
+                mask_rows[p, n : n + 1] = rows[p : p + 1]
+
+    def spread_rows(first, second):
+        return jnp.where(top, jnp.broadcast_to(first, (8, 2 * BOX)), jnp.broadcast_to(second, (8, 2 * BOX)))
+
+    def pack_plane(u, carry):
+        p = 2 * lax.rem(u, 2) + u // 2
+        raw_copy(p).wait()
+
+        def widen(m, c):
+            wide_rows[pl.ds(pl.multiple_of(STEP * m, 8), BOX), :] = raw[p, m].astype(F32)
+            return c
+
+        lax.fori_loop(0, 64, widen, 0)
+
+        def get(f):
+            n = f % BOX
+            return wide_rows[pl.ds(n, 64, stride=STEP), :] * mask_rows[p, n : n + 1]
+
+        for r in range(ROWS):
+            panel[0, p, r] = pack_row(get, r).astype(BF16)
+        return carry
+
+    lax.fori_loop(0, 2, pack_plane, 0)
     pl.semaphore_wait(barrier, 17)
-
-    mine = pl.ds(4 * me, 4)
-    to_peers(me, lambda g: send_a.at[pl.ds(4 * g, 4)], came_a.at[mine], a_sem.at[0], a_sem.at[1])
-    came_a[mine] = send_a[mine]
 
     def ring(src_slot, dst_slot, p, where, n):
         return remote(
@@ -408,38 +434,57 @@
     def ring_down(p):
         return ring(0, 1, p, down, 4 + p)
 
-    def pack_plane(u, carry):
-        p = 2 * lax.rem(u, 2) + u // 2
-        raw_copy(p).wait()
-
-        def widen(m, c):
-            wide_rows[pl.ds(pl.multiple_of(STEP * m, 8), BOX), :] = raw[p, m].astype(F32)
-            return c
-
-        lax.fori_loop(0, 64, widen, 0)
-
-        def get(f):
-            n = f % BOX
-            return wide_rows[pl.ds(n, 64, stride=STEP), :] * mask_rows[p, n : n + 1]
-
-        for r in range(ROWS):
-            panel[0, p, r] = pack_row(get, r).astype(BF16)
-
-        @pl.when(lax.rem(u, 2) == 0)
-        def _():
-            ring_up(p).start()
-
-        @pl.when(lax.rem(u, 2) == 1)
-        def _():
-            ring_down(p).start()
-
-        return carry
-
-    lax.fori_loop(0, 4, pack_plane, 0)
+    ring_up(0).start()
+    ring_down(2).start()
+    lax.fori_loop(2, 4, pack_plane, 0)
+    ring_up(1).start()
+    ring_down(3).start()
     ring_up(2).start()
     ring_down(0).start()
     ring_up(3).start()
     ring_down(1).start()
+
+    for i in range(2):
+        for k in range(2):
+            for q in range(4):
+                solved_rows[pl.ds(STEP * (8 * i + 4 * k + q), BOX), :] = raw[2 * k + i, STRIDE * q].astype(F32)
+    for f in kept_freqs:
+        n = f % BOX
+        for i in range(2):
+            rows = mask_rows[i, n : n + 1], mask_rows[2 + i, n : n + 1]
+            mask[place_of[f], 8 * i : 8 * i + 8] = spread_rows(*rows)
+        solved[place_of[f]] = solved_rows[pl.ds(n, 16, stride=STEP), :] * mask[place_of[f]]
+    forward_tile(solved, 0, fwd_hi[...], fwd_lo[...], near, tmp, put_pair(send_a, slice(0, 16), F32))
+
+    mine = pl.ds(4 * me, 4)
+    to_peers(me, lambda g: send_a.at[pl.ds(4 * g, 4)], came_a.at[mine], a_sem.at[0], a_sem.at[1])
+    came_a[mine] = send_a[mine]
+
+    def spread_field(n, carry):
+        line = v_local[pl.ds(n, 1), :]
+        potential[n] = spread_rows(line[:, : 2 * BOX], line[:, 2 * BOX :])
+        for p in range(NPERT):
+            line = dv[p, pl.ds(n, 1), :]
+            changes[p, n] = spread_rows(line[:, : 2 * BOX], line[:, 2 * BOX :])
+        return carry
+
+    lax.fori_loop(0, BOX, spread_field, 0)
+
+    factor = 0.5 * (2.0 * math.pi / cell_length) ** 2
+    row = lax.broadcasted_iota(jnp.int32, (8, 2 * BOX), 0)
+    third = lax.broadcasted_iota(jnp.int32, (8, 2 * BOX), 1) % BOX
+    third = jnp.where(third < BOX // 2, third, third - BOX).astype(F32)
+    for i in range(2):
+        first = 4 * me + 2 * (row // 4) + i
+        first = jnp.where(first < BOX // 2, first, first - BOX).astype(F32)
+        still = factor * ((first + k_point[0]) ** 2 + (third + k_point[2]) ** 2)
+        for q in range(4):
+            still = jnp.where(row % 4 == q, still - energies[q], still)
+        for f in kept_freqs:
+            here = mask[place_of[f], 8 * i : 8 * i + 8]
+            rise = factor * (float(f) + k_point[1]) * (float(f) + k_point[1])
+            level[place_of[f], 8 * i : 8 * i + 8] = (still + rise) * here
+            mask[place_of[f], 8 * i : 8 * i + 8] = here * (1.0 / BOX**3)
 
     def wait_all(src, dst, send, recv):
         return remote(src, dst, send, recv, {"ga": lax.rem(me + 1, 16)})
@@ -529,6 +574,8 @@
 
     combine(total_share(0), panel, spread, product, first_row)
 
+    lane = lax.broadcasted_iota(jnp.int32, (8, 2 * BOX), 1)
+
     def apply(it, carry):
         def near_tile(t, c):
             start = pl.multiple_of(16 * t, 16)
@@ -555,12 +602,17 @@
             wait_all(send_1.at[it, t, every], came_1.at[it, t, every], s1.at[it, t], r1.at[it, t]).wait()
             turn_in(came_1.at[it, t], near)
 
+            weight = [jnp.zeros((8, 2 * BOX), F32)]
+
             def with_potential(k, value):
                 v = potential[k]
-                near[k, 0:8] = value[0] * v
-                near[k, 8:16] = value[1] * v
+                re, im = value[0] * v, value[1] * v
+                near[k, 0:8] = re
+                near[k, 8:16] = im
+                weight[0] = weight[0] + (value[0] * re + value[1] * im)
 
             dft64(pair(near), ALL_SET, tmp, with_potential, 1)
+            weights[t] = weight[0]
             dft64(pair(near), ALL_SET, tmp, put_pair(send_2.at[it, t], slice(0, 16), BF16), -1)
             to_peers(
                 me, lambda g: send_2.at[it, t, pl.ds(4 * g, 4)], came_2.at[it, t, mine],
@@ -579,7 +631,39 @@
                     + level[place] * vec[it, place, rows]
                 )
 
-        combine(total_share(n), panel, spread, product, with_level)
+        corr = total_share(n)
+
+        @pl.when(it == 1)
+        def _():
+            def moments(place, totals):
+                b, ab, w = vec[0, place], image[0, place], vec[1, place]
+                lift = jnp.concatenate([level[place]] * 3, axis=0)
+                return tuple(x + y for x, y in zip(totals, (b * b, b * ab, ab * ab, lift * w * w)))
+
+            zero = jnp.zeros((48, 2 * BOX), F32)
+            totals = lax.fori_loop(0, KEPT, moments, (zero,) * 4)
+            own = jnp.zeros((8, 2 * BOX), F32)
+            for m, total in enumerate(totals):
+                line = jnp.sum(total, axis=1, keepdims=True) * (1.0 / BOX**3)
+                for t in range(3):
+                    both = line[16 * t : 16 * t + 8] + line[16 * t + 8 : 16 * t + 16]
+                    if m == 3:
+                        both = both + jnp.sum(weights[t], axis=1, keepdims=True) * (1.0 / BOX**6)
+                    own = jnp.where(lane == 4 * t + m, jnp.broadcast_to(both, own.shape), own)
+            own = own + pltpu.roll(own, 4, 0)
+            sums[...] = own
+            all_sums[me] = own
+            to_peers(me, lambda g: sums, all_sums.at[me], m_sem.at[0], m_sem.at[1])
+            square = corr.astype(F32)
+            square = jnp.sum(square * square, axis=1, keepdims=True) * (shift_weight / BOX**6)
+            rest = jnp.zeros((8, 2 * BOX), F32)
+            for t in range(3):
+                four = square[4 * t : 4 * t + 4] + square[12 + 4 * t : 16 + 4 * t]
+                eight = jnp.concatenate([four, four], axis=0)
+                rest = jnp.where(lane == 4 * t + 3, jnp.broadcast_to(eight, rest.shape), rest)
+            sums_here[...] = rest
+
+        combine(corr, panel, spread, product, with_level)
 
         def far_tile(t, c):
             wait_all(send_2.at[it, t, every], came_2.at[it, t, every], s2.at[it, t], r2.at[it, t]).wait()
@@ -597,26 +681,9 @@
 
     lax.fori_loop(0, 2, apply, 0)
 
-    def moments(place, totals):
-        b, ab, w, aw = vec[0, place], image[0, place], vec[1, place], image[1, place]
-        return tuple(x + y for x, y in zip(totals, (b * b, b * ab, ab * ab, w * aw)))
-
-    zero = jnp.zeros((48, 2 * BOX), F32)
-    totals = lax.fori_loop(0, KEPT, moments, (zero,) * 4)
-    lane = lax.broadcasted_iota(jnp.int32, (8, 2 * BOX), 1)
-    own = jnp.zeros((8, 2 * BOX), F32)
-    for m, total in enumerate(totals):
-        line = jnp.sum(total, axis=1, keepdims=True) / BOX**3
-        for t in range(3):
-            both = line[16 * t : 16 * t + 8] + line[16 * t + 8 : 16 * t + 16]
-            own = jnp.where(lane == 4 * t + m, jnp.broadcast_to(both, own.shape), own)
-    own = own + pltpu.roll(own, 4, 0)
-    sums[...] = own
-    all_sums[me] = own
-    to_peers(me, lambda g: sums, all_sums.at[me], m_sem.at[0], m_sem.at[1])
     first = pl.ds(0, 15)
     wait_all(all_sums.at[first], all_sums.at[first], m_sem.at[0], m_sem.at[1]).wait()
-    m0 = all_sums[0]
+    m0 = sums_here[...] + all_sums[0]
     for g in range(1, 16):
         m0 = m0 + all_sums[g]
     m1, m2, m3 = (pltpu.roll(m0, 2 * BOX - n, 1) for n in (1, 2, 3))
@@ -653,10 +720,18 @@
     return pl.pallas_call(
         kernel,
         out_shape=(shape(natural), shape(natural)),
-        in_specs=[pl.BlockSpec(memory_space=pl.ANY)] + [vmem] * (len(args) - 1),
+        in_specs=[pl.BlockSpec(memory_space=pl.ANY)] + [vmem] * 3 + [smem] * 2 + [vmem] * 6,
         out_specs=(vmem, vmem),
         scratch_shapes=[
             pltpu.VMEM((4, 64, BOX, 2 * BOX), BF16),
+            pltpu.VMEM((4, BOX, 2 * BOX), F32),
+            pltpu.VMEM((KEPT, 16, 2 * BOX), F32),
+            pltpu.VMEM((KEPT, 16, 2 * BOX), F32),
+            pltpu.VMEM((KEPT, 16, 2 * BOX), F32),
+            pltpu.VMEM((NPERT, BOX, 8, 2 * BOX), F32),
+            pltpu.VMEM((BOX, 8, 2 * BOX), F32),
+            pltpu.VMEM((16 * STEP, 2 * BOX), F32),
+            pltpu.VMEM((3, 8, 2 * BOX), F32),
             pltpu.VMEM((64 * STEP, 2 * BOX), F32),
             pltpu.VMEM((4, 4, ROWS, 64, 2 * BOX), BF16),
             grid_f, grid_f, grid_f,
@@ -669,6 +744,7 @@
             pltpu.VMEM((3, *natural), F32),
             pltpu.VMEM((2, *natural), F32),
             pltpu.VMEM((8, 2 * BOX), F32),
+            pltpu.VMEM((8, 2 * BOX), F32),
             pltpu.VMEM((16, 8, 2 * BOX), F32),
             dma((4,)), dma((12,)), dma((4, 4)), dma((2,)), dma((3,)), dma((3,)),
             dma((2, 3)), dma((2, 3)), dma((2, 3)), dma((2, 3)), dma((3,)), dma((3,)), dma((2,)),
@@ -679,39 +755,9 @@
     )(*args)
 
 
-def rows_of_planes(values):
-    values = values.reshape(2, 2, BOX, 2 * BOX).transpose(2, 1, 0, 3).reshape(BOX, 4, 2 * BOX)
-    return jnp.concatenate([values[: GCUT + 1], values[BOX - GCUT :]], axis=0)
-
-
 def on_device(psi_occ, energies, k_point, g_mask, v_local, dv):
-    planes = psi_occ.shape[1]
-    ga_index = lax.axis_index("ga")
-    indices = jnp.arange(BOX, dtype=jnp.int32)
-    signed = jnp.where(indices < BOX // 2, indices, indices - BOX).astype(F32)
-    owned = ga_index * planes + jnp.arange(planes, dtype=jnp.int32)
-    freq_first = jnp.where(owned < BOX // 2, owned, owned - BOX).astype(F32)
-    factor = 0.5 * (2.0 * math.pi / cell_length) ** 2
-    kinetic = factor * (
-        (freq_first[:, None, None] + k_point[0]) ** 2
-        + (signed[None, :, None] + k_point[1]) ** 2
-        + (signed[None, None, :] + k_point[2]) ** 2
-    )
-    kinetic = jnp.concatenate([kinetic, kinetic], axis=-1)
-    sphere = g_mask.reshape(planes, BOX, BOX).astype(F32)
-    sphere = jnp.concatenate([sphere, sphere], axis=-1)
-    mask = jnp.repeat(rows_of_planes(sphere), 4, axis=1)
-    level = (rows_of_planes(kinetic)[:, :, None, :] - energies[None, None, :, None]).reshape(
-        KEPT, 16, 2 * BOX
-    ) * mask
-    solved = psi_occ[::STRIDE].astype(F32) * sphere[None]
-    solved = solved.reshape(4, 2, 2, BOX, 2 * BOX).transpose(3, 2, 1, 0, 4).reshape(BOX, 16, 2 * BOX)
-    solved = jnp.concatenate([solved[: GCUT + 1], solved[BOX - GCUT :]], axis=0)
-    potential = jnp.repeat(v_local.reshape(BOX, 2, 2 * BOX), 4, axis=1)
-    changes = jnp.repeat(dv.reshape(NPERT, BOX, 2, 2 * BOX), 4, axis=2)
-
     response, residual = run(
-        psi_occ, sphere, solved, *lane_tables(), changes, potential, mask / BOX**3, level,
+        psi_occ, g_mask, v_local, dv, energies, k_point, *lane_tables(),
         jnp.asarray(fold_table(), BF16), jnp.asarray(spread_table(), BF16),
     )
 

time: 145 us -> 128 us (0.88)
  local copies, waits for them, and re-layouts: 8.12 us -> 2.31 us
  other arithmetic: 7.89 us -> 2.17 us
  Pallas kernels: 128 us -> 123 us
    pallas_call x1, Pallas kernels: 128 us -> 123 us  [run(): pl.pallas_call(kernel, out_shape=(shape(natural), shape(natural)), in_spe...]
    mul x3 -> x0, other arithmetic: 2.19 us -> none  [the longest x1 1 us: on_device(): solved = psi_occ[::STRIDE].astype(F32) * sphere[None]]
    integer_pow x3 -> x0, other arithmetic: 2 us -> none  [the longest x1 0.7 us: on_device(): (signed[None, None, :] + k_point[2]) ** 2]
    broadcast_in_dim x3 -> x0, local copies, waits for them, and re-layouts: 1.85 us -> none  [the longest x1 1.01 us: on_device(): changes = jnp.repeat(dv.reshape(NPERT, BOX, 2, 2 * BOX), 4, axis=2)]
    slice x7 -> x0, local copies, waits for them, and re-layouts: 1.48 us -> none  [the longest x1 1.43 us: on_device(): k_point[1]]
where the time goes in v3:
time: 128 us
  Pallas kernels  123 us (96%)
  local copies, waits for them, and re-layouts  2.31 us (2%)
  other arithmetic  2.17 us (2%)
    pallas_call x1, Pallas kernels, run(): pl.pallas_call(kernel, out_shape=(shape(natural), shape(natural)), in_spe...  123 us

profile of v3, /device:TPU:0, one launch (start us, length us, event | category | flops | bytes accessed | tf_op | source)
XLA Modules:
  0.0 128.1 jit_solution(3080681050277432191)
XLA Ops:
  0.6 0.1 pad.4.clone
  0.7 122.9 %shard_map.113 = (f32[43,48,128]{2,1,0:T(8,128)}, f32[43,48,128]{2,1,0:T(8,128)}) custom-call(bf16[64,4,64,128]{3,2,1,0:T(8,128)(2,1)} %psi.1, s32[4,4096]{1,0:T(4,128)} %g_mask.1, f32[64,256]{1,0:T(8,128)} %v_local.1, f32[3,64,256]{2,1,0:T(8,128)} %dv.1, f32[4]{0:T(128)} %energies.1, f32[3]{0:T(128)} %k_point.1, bf16[256,256]{1,0:T(8,128)(2,1)} %constant.18.fwd_hi, ...), custom_call_target="tpu_custom_call" | custom-call | tf_op jit(solution)/shard_map/pallas_call | solution.py:720
  123.7 0.0 copy-start
  123.7 1.7 %copy.13 = f32[4,3,2,2,43,128]{5,4,3,2,1,0:T(8,128)S(1)} copy(f32[4,3,2,2,43,128]{5,0,2,3,1,4:T(4,128)} %bitcast.13) | data formatting | bytes 2113536 | tf_op jit(solution)/shard_map/transpose | solution.py:765
  125.3 0.0 copy-done
  125.4 0.4 copy.12
  125.7 0.1 slice.17
  125.8 0.1 slice.19
  126.0 2.2 %pad_maximum_fusion.1 = (f32[4,3,4,64,128]{4,3,2,1,0:T(8,128)}, f32[4,3,4,64,128]{4,3,2,1,0:T(8,128)}) fusion(f32[4,3,4,21,128]{4,3,2,1,0:T(8,128)S(1)} %slice.19, f32[4,3,4,22,128]{4,3,2,1,0:T(8,128)S(1)} %slice.18, f32[64]{0:T(128)S(1)} %pad.4.clone, f32[4,3,4,21,128]{4,3,2,1,0:T(8,128)S(1)} %slice.17, f32[4,3,4,22,128]{4,3,2,1,0:T(8,128)S(1)} %slice.16), kind=kLoop, calls=%fused_computation.1 | loop fusion | flops 1572864 | bytes 5259520 | tf_op jit(solution)/shard_map/concatenate | solution.py:768
  (3 shorter events, 0.1 us)
Async XLA Ops:
  123.7 1.7 %copy-start = (f32[43,48,128]{2,1,0:T(8,128)S(1)}, f32[43,48,128]{2,1,0:T(8,128)}, u32[]{:S(2)}) copy-start(f32[43,48,128]{2,1,0:T(8,128)} %get-tuple-element.4) | copy-start | bytes 3170308

commit v4 on v3

--- a/solution.py
+++ b/solution.py
@@ -14,19 +14,14 @@
 KEPT = 2 * GCUT + 1
 NPERT = 3
 STRIDE = 16
-BASE_ROW = 13
 SHIFT = 16.0
-ROWS = 2 * BASE_ROW + 1
+ROWS = 24
 
 cell_length = 16.5
 shift_weight = 8.0
 
 kept_freqs = list(range(GCUT + 1)) + list(range(-GCUT, 0))
 place_of = {f: i for i, f in enumerate(kept_freqs)}
-base_freqs = list(range(BASE_ROW + 1)) + list(range(-BASE_ROW, 0))
-wide_freqs = [f for m in range(14, 19) for f in (m, -m)]
-narrow_freqs = [f for m in range(19, 22) for f in (m, -m)]
-WIDE = len(wide_freqs)
 F32 = jnp.float32
 BF16 = jnp.bfloat16
 
@@ -216,41 +211,53 @@
     return lax.broadcasted_iota(jnp.int32, shape, len(shape) - 1) % BOX < BOX // 2
 
 
+def widest(f):
+    return int(math.sqrt(GCUT**2 - max(abs(f) - 0.5, 0.0) ** 2) + 0.5)
+
+
+def lay_rows():
+    order = sorted(kept_freqs, key=lambda f: (abs(f), -f))
+    hosts, others = order[:ROWS], order[ROWS:]
+    room = [[widest(f) + 1, BOX - 1 - widest(f)] for f in hosts]
+    pieces = sorted(
+        [(widest(f) + 1, f, True) for f in others] + [(widest(f), f, False) for f in others],
+        key=lambda piece: -piece[0],
+    )
+    guests, where = [[] for _ in hosts], {}
+    for size, f, ahead in pieces:
+        fits = [r for r in range(ROWS) if room[r][1] - room[r][0] + 1 >= size]
+        r = min(fits, key=lambda n: (room[n][1] - room[n][0] + 1 - size, n))
+        start = room[r][0]
+        shift = start if ahead else start - (BOX - size)
+        room[r][0] = start + size
+        guests[r].append((f, ahead, shift % (2 * BOX)))
+        where[f, ahead] = (r, shift % (2 * BOX))
+    return hosts, guests, where
+
+
+hosts, guests, where_laid = lay_rows()
+
+
 def pack_row(get, r):
-    value = get(base_freqs[r])
+    value = get(hosts[r])
     front = front_lanes(value.shape)
-    axis = value.ndim - 1
-    if r < WIDE:
-        guest = jnp.where(front, get(wide_freqs[r]), 0.0)
-        value = value + pltpu.roll(guest, GCUT + 1, axis)
-    elif r < 2 * WIDE:
-        guest = jnp.where(front, 0.0, get(wide_freqs[r - WIDE]))
-        value = value + pltpu.roll(guest, 2 * BOX - GCUT, axis)
-    elif r < 2 * WIDE + 6:
-        guest = get(narrow_freqs[r - 2 * WIDE])
-        value = value + pltpu.roll(jnp.where(front, guest, 0.0), BOX // 2, axis)
-        value = value + pltpu.roll(jnp.where(front, 0.0, guest), 3 * BOX // 2, axis)
+    for f, ahead, shift in guests[r]:
+        row = get(f)
+        piece = jnp.where(front, row, 0.0) if ahead else jnp.where(front, 0.0, row)
+        value = value + pltpu.roll(piece, shift, value.ndim - 1)
     return value
 
 
 def unpack_row(get, f):
-    if f in base_freqs:
-        return get(base_freqs.index(f))
-    if f in wide_freqs:
-        r = wide_freqs.index(f)
-        up, down = get(r), get(WIDE + r)
-        axis = up.ndim - 1
-        return jnp.where(
-            front_lanes(up.shape),
-            pltpu.roll(up, 2 * BOX - GCUT - 1, axis),
-            pltpu.roll(down, GCUT, axis),
-        )
-    value = get(2 * WIDE + narrow_freqs.index(f))
-    axis = value.ndim - 1
+    if f in hosts:
+        return get(hosts.index(f))
+    (r, up), (n, down) = where_laid[f, True], where_laid[f, False]
+    first, second = get(r), get(n)
+    axis = first.ndim - 1
     return jnp.where(
-        front_lanes(value.shape),
-        pltpu.roll(value, 3 * BOX // 2, axis),
-        pltpu.roll(value, BOX // 2, axis),
+        front_lanes(first.shape),
+        pltpu.roll(first, (2 * BOX - up) % (2 * BOX), axis),
+        pltpu.roll(second, (2 * BOX - down) % (2 * BOX), axis),
     )
 
 
@@ -755,19 +762,36 @@
     )(*args)
 
 
+def place_body(response, residual, *outs):
+    for src, out in zip((response, residual), outs):
+        flat = src.reshape(KEPT * 16, 2 * BOX)
+        for i in range(2):
+            for k in range(2):
+                for q in range(4):
+                    line = flat[pl.ds(8 * i + 4 * k + q, KEPT, stride=16), :]
+                    out[q, 0, 2 * k + i, 0 : GCUT + 1] = line[: GCUT + 1]
+                    out[q, 0, 2 * k + i, GCUT + 1 : BOX - GCUT] = jnp.zeros((BOX - KEPT, 2 * BOX), F32)
+                    out[q, 0, 2 * k + i, BOX - GCUT :] = line[GCUT + 1 :]
+
+
+def place(*values):
+    out = shape((4, NPERT, 4, BOX, 2 * BOX))
+    return pl.pallas_call(
+        place_body,
+        grid=(NPERT,),
+        out_shape=(out, out),
+        in_specs=[pl.BlockSpec((KEPT, 16, 2 * BOX), lambda t: (0, t, 0))] * 2,
+        out_specs=(pl.BlockSpec((4, 1, 4, BOX, 2 * BOX), lambda t: (0, t, 0, 0, 0)),) * 2,
+    )(*values)
+
+
 def on_device(psi_occ, energies, k_point, g_mask, v_local, dv):
     response, residual = run(
         psi_occ, g_mask, v_local, dv, energies, k_point, *lane_tables(),
         jnp.asarray(fold_table(), BF16), jnp.asarray(spread_table(), BF16),
     )
 
-    def placed(values):
-        values = values.reshape(KEPT, 3, 2, 2, 4, 2 * BOX).transpose(4, 1, 3, 2, 0, 5)
-        values = values.reshape(4, NPERT, 4, KEPT, 2 * BOX)
-        gap = jnp.zeros((4, NPERT, 4, BOX - KEPT, 2 * BOX), F32)
-        return jnp.concatenate([values[..., : GCUT + 1, :], gap, values[..., GCUT + 1 :, :]], axis=3)
-
-    return placed(response), placed(residual)
+    return place(response, residual)
 
 
 def solution(mesh):

time: 128 us -> 122 us (0.953)
  local copies, waits for them, and re-layouts: 2.31 us -> 0 us
  other arithmetic: 2.17 us -> 0 us
  Pallas kernels: 123 us -> 121 us
    pallas_call x1, Pallas kernels: 123 us -> 117 us  [run(): pl.pallas_call(kernel, out_shape=(shape(natural), shape(natural)), in_spe...]
    pallas_call x0 -> x1, Pallas kernels: none -> 4.23 us  [place(): pl.pallas_call(place_body, grid=(NPERT,), out_shape=(out, out), in_specs=...]
    concatenate x1 -> x0, other arithmetic: 2.17 us -> none  [placed(): jnp.concatenate([values[..., :GCUT + 1, :], gap, values[..., GCUT + 1:, :...]
    transpose x2 -> x0, local copies, waits for them, and re-layouts: 2.03 us -> none  [placed(): values.reshape(KEPT, 3, 2, 2, 4, 2 * BOX).transpose(4, 1, 3, 2, 0, 5)]
where the time goes in v4:
time: 122 us
  Pallas kernels  121 us (99%)
    pallas_call x1, Pallas kernels, run(): pl.pallas_call(kernel, out_shape=(shape(natural), shape(natural)), in_spe...  117 us
    pallas_call x1, Pallas kernels, place(): pl.pallas_call(place_body, grid=(NPERT,), out_shape=(out, out), in_specs=...  4.23 us

profile of v4, /device:TPU:0, one launch (start us, length us, event | category | flops | bytes accessed | tf_op | source)
XLA Modules:
  0.0 121.6 jit_solution(1849352211701278090)
XLA Ops:
  0.6 116.8 %shard_map.113 = (f32[43,48,128]{2,1,0:T(8,128)}, f32[43,48,128]{2,1,0:T(8,128)}) custom-call(bf16[64,4,64,128]{3,2,1,0:T(8,128)(2,1)} %psi.1, s32[4,4096]{1,0:T(4,128)} %g_mask.1, f32[64,256]{1,0:T(8,128)} %v_local.1, f32[3,64,256]{2,1,0:T(8,128)} %dv.1, f32[4]{0:T(128)} %energies.1, f32[3]{0:T(128)} %k_point.1, bf16[256,256]{1,0:T(8,128)(2,1)} %constant.16.fwd_hi, ...), custom_call_target="tpu_custom_call" | custom-call | tf_op jit(solution)/shard_map/pallas_call | solution.py:727
  117.4 4.2 %shard_map.114 = (f32[4,3,4,64,128]{4,3,2,1,0:T(8,128)}, f32[4,3,4,64,128]{4,3,2,1,0:T(8,128)}) custom-call(f32[43,48,128]{2,1,0:T(8,128)} %get-tuple-element.4.response, f32[43,48,128]{2,1,0:T(8,128)} %get-tuple-element.5.residual), custom_call_target="tpu_custom_call" | custom-call | tf_op jit(solution)/shard_map/pallas_call | solution.py:779

commit v5 on v4

--- a/solution.py
+++ b/solution.py
@@ -265,10 +265,8 @@
     return jnp.where(lax.broadcasted_iota(jnp.int32, shape, len(shape) - 1) < BOX, 1.0, -1.0)
 
 
-def panel_rows(panel, slots, r, p, both):
-    rows = [jnp.concatenate([panel[d, p, r] for d in slots], axis=0)]
-    if both:
-        rows.append(jnp.concatenate([panel[d, p, r + 1] for d in slots], axis=0))
+def panel_rows(panel, slots, r, p):
+    rows = [jnp.concatenate([panel[d, p, n] for d in slots], axis=0) for n in (r, r + 1)]
     return jnp.concatenate(rows, axis=1)
 
 
@@ -280,20 +278,20 @@
         packed[r] = jnp.concatenate([straight, turned], axis=0).astype(BF16)
 
 
-def correlate(packed, panel, fold, slots):
+def correlate(packed, panel, fold, slots, planes=(0, 1, 2, 3)):
     count = 64 * len(slots)
     nt = (((1,), (1,)), ((), ()))
-    total = [None] * 4
+    total = {p: None for p in planes}
     for r in range(0, ROWS, 2):
-        both = r + 1 < ROWS
-        y = jnp.concatenate([packed[r], packed[r + 1]], axis=1) if both else packed[r]
-        for p in range(4):
-            o = panel_rows(panel, slots, r, p, both)
-            part = lax.dot_general(o, y, nt, preferred_element_type=F32)
+        y = jnp.concatenate([packed[r], packed[r + 1]], axis=1)
+        for p in planes:
+            part = lax.dot_general(
+                panel_rows(panel, slots, r, p), y, nt, preferred_element_type=F32
+            )
             total[p] = part if total[p] is None else total[p] + part
     column = lax.broadcasted_iota(jnp.int32, (count, 96), 1) % 16 // 4
-    chosen = total[0]
-    for p in range(1, 4):
+    chosen = jnp.zeros((count, 96), F32)
+    for p in planes:
         chosen = jnp.where(column == 2 * (p % 2) + p // 2, total[p], chosen)
     hi = chosen.astype(BF16)
     lo = (chosen - hi.astype(F32)).astype(BF16)
@@ -321,21 +319,23 @@
     return f.reshape(384, 24)
 
 
-def combine(corr, panel, spread, product, finish):
+def multiply(corr, panel, spread, product, slots, more=False):
     rows = jnp.dot(spread[...], corr, preferred_element_type=F32).astype(BF16)
     sign = -lane_sign((48, 2 * BOX))
     for r in range(0, ROWS, 2):
-        both = r + 1 < ROWS
         total = None
         for p in range(4):
-            o = panel_rows(panel, SLOTS, r, p, both)
-            part = jnp.dot(rows[96 * p : 96 * p + 96], o, preferred_element_type=F32)
+            part = jnp.dot(
+                rows[96 * p : 96 * p + 96], panel_rows(panel, slots, r, p), preferred_element_type=F32
+            )
             total = part if total is None else total + part
-        for c in range(2 if both else 1):
+        for c in range(2):
             lanes = slice(2 * BOX * c, 2 * BOX * (c + 1))
-            product[r + c] = (
-                total[:48, lanes] + pltpu.roll(total[48:, lanes], BOX, 1) * sign
-            )
+            value = total[:48, lanes] + pltpu.roll(total[48:, lanes], BOX, 1) * sign
+            product[r + c] = product[r + c] + value if more else value
+
+
+def lay_out(product, finish):
     for f in kept_freqs:
         finish(place_of[f], unpack_row(lambda r: product[r], f))
 
@@ -358,20 +358,28 @@
     )
 
 
+def away(step):
+    return min(step[0], 4 - step[0]) + min(step[1], 4 - step[1])
+
+
+STEPS = sorted([(y, x) for y in range(4) for x in range(4) if (y, x) != (0, 0)], key=lambda s: -away(s))
+
+
+def peers(me):
+    for dy, dx in STEPS:
+        yield 4 * lax.rem(me // 4 + dy, 4) + lax.rem(lax.rem(me, 4) + dx, 4)
+
+
 def to_peers(me, src_of, dst, send, recv):
-    def one(k, carry):
-        g = lax.rem(me + k, 16)
+    for g in peers(me):
         remote(src_of(g), dst, send, recv, {"ga": g}).start()
-        return carry
-
-    lax.fori_loop(1, 16, one, 0)
 
 
 def kernel(
     psi, g_mask, v_local, dv, energies, k_point, fwd_hi, fwd_lo, back_hi, back_lo, fold, spread,
     response, residual,
     raw, mask_rows, mask, level, solved, changes, potential, solved_rows, weights, wide_rows, panel, near, tmp, space, send_a, came_a, send_b, came_b, send_1, send_2,
-    came_1, came_2, packed, product, share, shares, source, vec, image, sums, sums_here, all_sums,
+    came_1, came_2, packed, product, share, shares, far_share, far_shares, source, vec, image, sums, sums_here, all_sums,
     raw_sem, ring_send, ring_recv, a_sem, b_send, b_recv, s1, r1, s2, r2, c_send, c_recv, m_sem,
 ):
     me = lax.axis_index("ga")
@@ -380,13 +388,8 @@
 
     barrier = pltpu.get_barrier_semaphore()
 
-    def greet(k, carry):
-        pl.semaphore_signal(
-            barrier, inc=1, device_id={"ga": lax.rem(me + k, 16)}, device_id_type=MESH
-        )
-        return carry
-
-    lax.fori_loop(1, 16, greet, 0)
+    for g in peers(me):
+        pl.semaphore_signal(barrier, inc=1, device_id={"ga": g}, device_id_type=MESH)
     for other in (up, down):
         pl.semaphore_signal(barrier, inc=1, device_id={"band": other}, device_id_type=MESH)
 
@@ -564,22 +567,33 @@
         ring(0, 3, p, up, p).wait_recv()
     for p in range(2):
         ring(0, 1, p, down, 4 + p).wait_recv()
-    early = correlate(packed, panel, fold[...], SLOTS[:3])
-    for p in range(2):
-        ring(3, 2, p, up, 8 + p).wait_recv()
-    for p in range(2, 4):
-        ring(1, 2, p, down, 8 + p).wait_recv()
-    late = correlate(packed, panel, fold[...], SLOTS[3:])
-    share[0] = jnp.concatenate([early, late], axis=1).astype(BF16)
+    early = correlate(packed, panel, fold[...], SLOTS[:3]).astype(BF16)
+    share[0] = jnp.concatenate([early, jnp.zeros((24, 64), BF16)], axis=1)
     shares[0, me] = share[0]
     send_share(0, share.at[0])
+    ring(3, 2, 0, up, 8).wait_recv()
+    ring(1, 2, 2, down, 10).wait_recv()
+    late = correlate(packed, panel, fold[...], SLOTS[3:], (0, 2))
+    multiply(total_share(0)[:, :192], panel, spread, product, SLOTS[:3])
+    ring(3, 2, 1, up, 9).wait_recv()
+    ring(1, 2, 3, down, 11).wait_recv()
+    late = late + correlate(packed, panel, fold[...], SLOTS[3:], (1, 3))
+    far_share[...] = jnp.concatenate([late.astype(BF16), jnp.zeros((24, 64), BF16)], axis=1)
+    far_shares[me] = far_share[...]
+    to_peers(me, lambda g: far_share, far_shares.at[me], c_send.at[3], c_recv.at[3])
 
     def first_row(place, row):
         for t in range(3):
             rows = slice(16 * t, 16 * t + 16)
             vec[0, place, rows] = row[rows] * mask[place] - source[place, rows]
 
-    combine(total_share(0), panel, spread, product, first_row)
+    first = pl.ds(0, 15)
+    wait_all(far_shares.at[first], far_shares.at[first], c_send.at[3], c_recv.at[3]).wait()
+    total = far_shares[0].astype(F32)
+    for g in range(1, 16):
+        total = total + far_shares[g].astype(F32)
+    multiply(total.astype(BF16)[:, :64], panel, spread, product, SLOTS[3:], True)
+    lay_out(product, first_row)
 
     lane = lax.broadcasted_iota(jnp.int32, (8, 2 * BOX), 1)
 
@@ -670,7 +684,8 @@
                 rest = jnp.where(lane == 4 * t + 3, jnp.broadcast_to(eight, rest.shape), rest)
             sums_here[...] = rest
 
-        combine(corr, panel, spread, product, with_level)
+        multiply(corr, panel, spread, product, SLOTS)
+        lay_out(product, with_level)
 
         def far_tile(t, c):
             wait_all(send_2.at[it, t, every], came_2.at[it, t, every], s2.at[it, t], r2.at[it, t]).wait()
@@ -747,6 +762,8 @@
             pltpu.VMEM((ROWS, 48, 2 * BOX), F32),
             pltpu.VMEM((3, 24, 256), BF16),
             pltpu.VMEM((3, 16, 24, 256), BF16),
+            pltpu.VMEM((24, 128), BF16),
+            pltpu.VMEM((16, 24, 128), BF16),
             pltpu.VMEM(natural, F32),
             pltpu.VMEM((3, *natural), F32),
             pltpu.VMEM((2, *natural), F32),
@@ -754,7 +771,7 @@
             pltpu.VMEM((8, 2 * BOX), F32),
             pltpu.VMEM((16, 8, 2 * BOX), F32),
             dma((4,)), dma((12,)), dma((4, 4)), dma((2,)), dma((3,)), dma((3,)),
-            dma((2, 3)), dma((2, 3)), dma((2, 3)), dma((2, 3)), dma((3,)), dma((3,)), dma((2,)),
+            dma((2, 3)), dma((2, 3)), dma((2, 3)), dma((2, 3)), dma((4,)), dma((4,)), dma((2,)),
         ],
         compiler_params=pltpu.CompilerParams(
             vmem_limit_bytes=VMEM_LIMIT, collective_id=0, has_side_effects=True

time: 122 us -> 120 us (0.984)
  Pallas kernels: 121 us -> 119 us
    pallas_call x1, Pallas kernels: 117 us -> 114 us  [run(): pl.pallas_call(kernel, out_shape=(shape(natural), shape(natural)), in_spe...]
where the time goes in v5:
time: 120 us; the launch traced here: 119 us
  Pallas kernels  119 us (99%)
    pallas_call x1, Pallas kernels, run(): pl.pallas_call(kernel, out_shape=(shape(natural), shape(natural)), in_spe...  114 us
    pallas_call x1, Pallas kernels, place(): pl.pallas_call(place_body, grid=(NPERT,), out_shape=(out, out), in_specs=...  4.23 us

profile of v5, /device:TPU:0, one launch (start us, length us, event | category | flops | bytes accessed | tf_op | source)
XLA Modules:
  0.0 119.3 jit_solution(2869031171098745127)
XLA Ops:
  0.6 114.5 %shard_map.113 = (f32[43,48,128]{2,1,0:T(8,128)}, f32[43,48,128]{2,1,0:T(8,128)}) custom-call(bf16[64,4,64,128]{3,2,1,0:T(8,128)(2,1)} %psi.1, s32[4,4096]{1,0:T(4,128)} %g_mask.1, f32[64,256]{1,0:T(8,128)} %v_local.1, f32[3,64,256]{2,1,0:T(8,128)} %dv.1, f32[4]{0:T(128)} %energies.1, f32[3]{0:T(128)} %k_point.1, bf16[256,256]{1,0:T(8,128)(2,1)} %constant.16.fwd_hi, ...), custom_call_target="tpu_custom_call" | custom-call | tf_op jit(solution)/shard_map/pallas_call | solution.py:742
  115.1 4.2 %shard_map.114 = (f32[4,3,4,64,128]{4,3,2,1,0:T(8,128)}, f32[4,3,4,64,128]{4,3,2,1,0:T(8,128)}) custom-call(f32[43,48,128]{2,1,0:T(8,128)} %get-tuple-element.4.response, f32[43,48,128]{2,1,0:T(8,128)} %get-tuple-element.5.residual), custom_call_target="tpu_custom_call" | custom-call | tf_op jit(solution)/shard_map/pallas_call | solution.py:796

commit v6 on v5

--- a/solution.py
+++ b/solution.py
@@ -169,8 +169,9 @@
     forward = np.block([[c, z, s, z], [-s, z, c, z], [z, c, z, s], [z, -s, z, c]])
     s = -s
     back = np.block([[c, s, z, z], [z, z, c, s], [-s, c, z, z], [z, z, -s, c]])
+    grid = np.block([[c, z, -s, z], [z, c, z, -s], [s, z, c, z], [z, s, z, c]])
     out = []
-    for w in (forward, back):
+    for w in (forward, back, grid, grid.T):
         w = jnp.asarray(w, F32)
         high = w.astype(BF16)
         out += [high, (w - high.astype(F32)).astype(BF16)]
@@ -205,6 +206,55 @@
 
     dft64(pair(near), KEPT_SET, tmp, store, -1)
     return lanes_back(near, high, low)
+
+
+def squeeze(src, dst):
+    front = front_lanes((16, 2 * BOX))
+    for g in range(16):
+        first, second, third, guest = (src[4 * g + c] for c in range(4))
+        ahead = pltpu.roll(jnp.where(front, guest, 0.0), GCUT + 1, 1)
+        behind = pltpu.roll(jnp.where(front, 0.0, guest), 2 * BOX - GCUT, 1)
+        dst[3 * g] = (first + ahead).astype(BF16)
+        dst[3 * g + 1] = (second + behind).astype(BF16)
+        dst[3 * g + 2] = third.astype(BF16)
+
+
+def turn_squeezed(src, dst, valid=None):
+    front = front_lanes((16, 2 * BOX))
+    for g in range(16):
+        tiles = [src[3 * g + c].astype(F32) for c in range(3)]
+        ahead = pltpu.roll(tiles[0], 2 * BOX - GCUT - 1, 1)
+        tiles.append(jnp.where(front, ahead, pltpu.roll(tiles[1], GCUT, 1)))
+        if valid is not None:
+            tiles = [t * valid for t in tiles]
+        re = corner_turn([t[0:8] for t in tiles])
+        im = corner_turn([t[8:16] for t in tiles])
+        for c in range(4):
+            dst[4 * g + c, 0:8] = re[c]
+            dst[4 * g + c, 8:16] = im[c]
+
+
+def natural_to_pair(src, first_row, dst):
+    front = lax.broadcasted_iota(jnp.int32, (8, 2 * BOX), 1) < BOX
+    for n in range(KEPT):
+        a, b = src[n, pl.ds(first_row, 8), :], src[n, pl.ds(first_row + 8, 8), :]
+        dst[n, 0:8] = jnp.where(front, a, pltpu.roll(b, BOX, 1))
+        dst[n, 8:16] = jnp.where(front, pltpu.roll(a, BOX, 1), b)
+
+
+def pair_to_natural(src, n):
+    front = lax.broadcasted_iota(jnp.int32, (8, 2 * BOX), 1) < BOX
+    re, im = src[n, 0:8], src[n, 8:16]
+    return jnp.where(front, re, pltpu.roll(im, BOX, 1)), jnp.where(front, pltpu.roll(re, BOX, 1), im)
+
+
+def grid_lanes(ref, high, low, valid=None):
+    x = [ref[:, h : h + 8, :].reshape(BOX * 8, 2 * BOX) for h in (0, 8)]
+    x = jnp.concatenate(x, axis=1).astype(BF16)
+    out = jnp.dot(x, high, preferred_element_type=F32) + jnp.dot(x, low, preferred_element_type=F32)
+    for h, lanes in ((0, slice(0, 2 * BOX)), (8, slice(2 * BOX, 4 * BOX))):
+        part = out[:, lanes].reshape(BOX, 8, 2 * BOX)
+        ref[:, h : h + 8, :] = part if valid is None else part * valid[0:8]
 
 
 def front_lanes(shape):
@@ -376,7 +426,8 @@
 
 
 def kernel(
-    psi, g_mask, v_local, dv, energies, k_point, fwd_hi, fwd_lo, back_hi, back_lo, fold, spread,
+    psi, g_mask, v_local, dv, energies, k_point, fwd_hi, fwd_lo, back_hi, back_lo, up_hi, up_lo, down_hi, down_lo,
+    fold, spread,
     response, residual,
     raw, mask_rows, mask, level, solved, changes, potential, solved_rows, weights, wide_rows, panel, near, tmp, space, send_a, came_a, send_b, came_b, send_1, send_2,
     came_1, came_2, packed, product, share, shares, far_share, far_shares, source, vec, image, sums, sums_here, all_sums,
@@ -596,19 +647,23 @@
     lay_out(product, first_row)
 
     lane = lax.broadcasted_iota(jnp.int32, (8, 2 * BOX), 1)
+    mine3, most = pl.ds(3 * me, 3), pl.ds(0, 45)
+    third = lax.broadcasted_iota(jnp.int32, (16, 2 * BOX), 1) % BOX
+    third = jnp.where(third < BOX // 2, third, third - BOX)
+    side = jnp.minimum(jnp.maximum(4.0 * k_point[2], -1.0), 1.0)
+    edge = jnp.where(third == GCUT, 0.5 - 0.5 * side, jnp.where(third == -GCUT, 0.5 + 0.5 * side, 0.0))
+    valid = jnp.where(jnp.abs(third) < GCUT, 1.0, edge)
 
     def apply(it, carry):
         def near_tile(t, c):
-            start = pl.multiple_of(16 * t, 16)
-            forward_tile(
-                vec.at[it], start, fwd_hi[...], fwd_lo[...], near, tmp,
-                put_pair(send_1.at[it, t], slice(0, 16), BF16),
-            )
+            natural_to_pair(vec.at[it], pl.multiple_of(16 * t, 16), near)
+            dft64(load_kept(near), ALL_SET, tmp, put_pair(space, slice(0, 16), F32), 1)
+            squeeze(space, send_1.at[it, t])
             to_peers(
-                me, lambda g: send_1.at[it, t, pl.ds(4 * g, 4)], came_1.at[it, t, mine],
+                me, lambda g: send_1.at[it, t, pl.ds(3 * g, 3)], came_1.at[it, t, mine3],
                 s1.at[it, t], r1.at[it, t],
             )
-            came_1[it, t, mine] = send_1[it, t, mine]
+            came_1[it, t, mine3] = send_1[it, t, mine3]
             return c
 
         lax.fori_loop(0, 3, near_tile, 0)
@@ -620,8 +675,9 @@
         send_share(n, share.at[n])
 
         def space_tile(t, c):
-            wait_all(send_1.at[it, t, every], came_1.at[it, t, every], s1.at[it, t], r1.at[it, t]).wait()
-            turn_in(came_1.at[it, t], near)
+            wait_all(send_1.at[it, t, most], came_1.at[it, t, most], s1.at[it, t], r1.at[it, t]).wait()
+            turn_squeezed(came_1.at[it, t], near, valid)
+            grid_lanes(near, up_hi[...], up_lo[...])
 
             weight = [jnp.zeros((8, 2 * BOX), F32)]
 
@@ -634,12 +690,14 @@
 
             dft64(pair(near), ALL_SET, tmp, with_potential, 1)
             weights[t] = weight[0]
-            dft64(pair(near), ALL_SET, tmp, put_pair(send_2.at[it, t], slice(0, 16), BF16), -1)
+            dft64(pair(near), ALL_SET, tmp, put_pair(near, slice(0, 16), F32), -1)
+            grid_lanes(near, down_hi[...], down_lo[...], valid)
+            squeeze(near, send_2.at[it, t])
             to_peers(
-                me, lambda g: send_2.at[it, t, pl.ds(4 * g, 4)], came_2.at[it, t, mine],
+                me, lambda g: send_2.at[it, t, pl.ds(3 * g, 3)], came_2.at[it, t, mine3],
                 s2.at[it, t], r2.at[it, t],
             )
-            came_2[it, t, mine] = send_2[it, t, mine]
+            came_2[it, t, mine3] = send_2[it, t, mine3]
             return c
 
         lax.fori_loop(0, 3, space_tile, 0)
@@ -688,14 +746,21 @@
         lay_out(product, with_level)
 
         def far_tile(t, c):
-            wait_all(send_2.at[it, t, every], came_2.at[it, t, every], s2.at[it, t], r2.at[it, t]).wait()
+            wait_all(send_2.at[it, t, most], came_2.at[it, t, most], s2.at[it, t], r2.at[it, t]).wait()
             start = pl.multiple_of(16 * t, 16)
-            a, b = back_tile(came_2.at[it, t], back_hi[...], back_lo[...], near, tmp)
-            for half, value in ((0, a), (8, b)):
-                rows = pl.ds(start + half, 8)
-                total = image[it, :, rows, :] + value * mask[:, half : half + 8, :]
-                image[it, :, rows, :] = total
-                vec[it + 1, :, rows, :] = total - SHIFT * vec[it, :, rows, :]
+            turn_squeezed(came_2.at[it, t], near)
+
+            def to_near(n, value):
+                near[kept_place(n), 0:8] = value[0]
+                near[kept_place(n), 8:16] = value[1]
+
+            dft64(pair(near), KEPT_SET, tmp, to_near, -1)
+            for n in range(KEPT):
+                for half, value in zip((0, 8), pair_to_natural(near, n)):
+                    rows = pl.ds(start + half, 8)
+                    total = image[it, n, rows, :] + value * mask[n, half : half + 8]
+                    image[it, n, rows, :] = total
+                    vec[it + 1, n, rows, :] = total - SHIFT * vec[it, n, rows, :]
             return c
 
         lax.fori_loop(0, 3, far_tile, 0)
@@ -736,13 +801,13 @@
 def run(*args):
     grid_f = pltpu.VMEM((BOX, 16, 2 * BOX), F32)
     three_f = pltpu.VMEM((3, BOX, 16, 2 * BOX), F32)
-    six_b = pltpu.VMEM((2, 3, BOX, 16, 2 * BOX), BF16)
+    six_b = pltpu.VMEM((2, 3, 48, 16, 2 * BOX), BF16)
     natural = (KEPT, 48, 2 * BOX)
     dma = pltpu.SemaphoreType.DMA
     return pl.pallas_call(
         kernel,
         out_shape=(shape(natural), shape(natural)),
-        in_specs=[pl.BlockSpec(memory_space=pl.ANY)] + [vmem] * 3 + [smem] * 2 + [vmem] * 6,
+        in_specs=[pl.BlockSpec(memory_space=pl.ANY)] + [vmem] * 3 + [smem] * 2 + [vmem] * 10,
         out_specs=(vmem, vmem),
         scratch_shapes=[
             pltpu.VMEM((4, 64, BOX, 2 * BOX), BF16),

time: 120 us -> 112 us (0.933)
  Pallas kernels: 119 us -> 111 us
    pallas_call x1, Pallas kernels: 114 us -> 107 us  [run(): pl.pallas_call(kernel, out_shape=(shape(natural), shape(natural)), in_spe...]
where the time goes in v6:
time: 112 us
  Pallas kernels  111 us (99%)
    pallas_call x1, Pallas kernels, run(): pl.pallas_call(kernel, out_shape=(shape(natural), shape(natural)), in_spe...  107 us
    pallas_call x1, Pallas kernels, place(): pl.pallas_call(place_body, grid=(NPERT,), out_shape=(out, out), in_specs=...  4.23 us

profile of v6, /device:TPU:0, one launch (start us, length us, event | category | flops | bytes accessed | tf_op | source)
XLA Modules:
  0.0 111.9 jit_solution(1728186372494814743)
XLA Ops:
  0.6 107.1 %shard_map.131 = (f32[43,48,128]{2,1,0:T(8,128)}, f32[43,48,128]{2,1,0:T(8,128)}) custom-call(bf16[64,4,64,128]{3,2,1,0:T(8,128)(2,1)} %psi.1, s32[4,4096]{1,0:T(4,128)} %g_mask.1, f32[64,256]{1,0:T(8,128)} %v_local.1, f32[3,64,256]{2,1,0:T(8,128)} %dv.1, f32[4]{0:T(128)} %energies.1, f32[3]{0:T(128)} %k_point.1, bf16[256,256]{1,0:T(8,128)(2,1)} %constant.22.fwd_hi, ...), custom_call_target="tpu_custom_call" | custom-call | tf_op jit(solution)/shard_map/pallas_call | solution.py:807
  107.7 4.2 %shard_map.132 = (f32[4,3,4,64,128]{4,3,2,1,0:T(8,128)}, f32[4,3,4,64,128]{4,3,2,1,0:T(8,128)}) custom-call(f32[43,48,128]{2,1,0:T(8,128)} %get-tuple-element.4.response, f32[43,48,128]{2,1,0:T(8,128)} %get-tuple-element.5.residual), custom_call_target="tpu_custom_call" | custom-call | tf_op jit(solution)/shard_map/pallas_call | solution.py:861

commit v7 on v6

--- a/solution.py
+++ b/solution.py
@@ -210,28 +210,39 @@
 
 def squeeze(src, dst):
     front = front_lanes((16, 2 * BOX))
+    zero = jnp.zeros((16, 2 * BOX), BF16)
     for g in range(16):
-        first, second, third, guest = (src[4 * g + c] for c in range(4))
-        ahead = pltpu.roll(jnp.where(front, guest, 0.0), GCUT + 1, 1)
-        behind = pltpu.roll(jnp.where(front, 0.0, guest), 2 * BOX - GCUT, 1)
-        dst[3 * g] = (first + ahead).astype(BF16)
-        dst[3 * g + 1] = (second + behind).astype(BF16)
-        dst[3 * g + 2] = third.astype(BF16)
+        first, second, third, guest = (src[4 * g + c].astype(BF16) for c in range(4))
+        dst[3 * g] = first + pltpu.roll(jnp.where(front, guest, zero), GCUT + 1, 1)
+        dst[3 * g + 1] = second + pltpu.roll(jnp.where(front, zero, guest), 2 * BOX - GCUT, 1)
+        dst[3 * g + 2] = third
 
 
 def turn_squeezed(src, dst, valid=None):
     front = front_lanes((16, 2 * BOX))
+    left = lax.broadcasted_iota(jnp.int32, (16, 2 * BOX), 1) < BOX
+    top = lax.broadcasted_iota(jnp.int32, (8, 2 * BOX), 0) < 4
     for g in range(16):
-        tiles = [src[3 * g + c].astype(F32) for c in range(3)]
+        tiles = [src[3 * g + c] for c in range(3)]
         ahead = pltpu.roll(tiles[0], 2 * BOX - GCUT - 1, 1)
         tiles.append(jnp.where(front, ahead, pltpu.roll(tiles[1], GCUT, 1)))
-        if valid is not None:
-            tiles = [t * valid for t in tiles]
-        re = corner_turn([t[0:8] for t in tiles])
-        im = corner_turn([t[8:16] for t in tiles])
-        for c in range(4):
-            dst[4 * g + c, 0:8] = re[c]
-            dst[4 * g + c, 8:16] = im[c]
+        half = []
+        for h in range(2):
+            a, b = tiles[2 * h], tiles[2 * h + 1]
+            half.append(
+                (
+                    jnp.where(left, a, pltpu.roll(b, BOX, 1)).astype(F32),
+                    jnp.where(left, pltpu.roll(a, BOX, 1), b).astype(F32),
+                )
+            )
+        for i in range(2):
+            a, b = half[0][i], half[1][i]
+            if valid is not None:
+                a, b = a * valid, b * valid
+            for rows in (slice(0, 8), slice(8, 16)):
+                x, y = a[rows], b[rows]
+                dst[4 * g + i, rows] = jnp.where(top, x, pltpu.roll(y, 4, 0))
+                dst[4 * g + 2 + i, rows] = jnp.where(top, pltpu.roll(x, 4, 0), y)
 
 
 def natural_to_pair(src, first_row, dst):
@@ -324,7 +335,7 @@
     sign = lane_sign((48, 2 * BOX))
     for r in range(ROWS):
         straight = pack_row(lambda f: values[place_of[f]], r)
-        turned = pack_row(lambda f: pltpu.roll(values[place_of[f]], BOX, 1) * sign, r)
+        turned = pltpu.roll(straight, BOX, 1) * sign
         packed[r] = jnp.concatenate([straight, turned], axis=0).astype(BF16)
 
 
@@ -394,6 +405,7 @@
 MESH = pl.DeviceIdType.MESH
 vmem = pl.BlockSpec(memory_space=pltpu.VMEM)
 smem = pl.BlockSpec(memory_space=pltpu.SMEM)
+far = pl.BlockSpec(memory_space=pltpu.HBM)
 STEP = 72
 SLOTS = (0, 1, 3, 2)
 
@@ -426,12 +438,11 @@
 
 
 def kernel(
-    psi, g_mask, v_local, dv, energies, k_point, fwd_hi, fwd_lo, back_hi, back_lo, up_hi, up_lo, down_hi, down_lo,
-    fold, spread,
+    psi, g_mask, fold, spread, energies, k_point, far_v, far_dv, far_tables,
     response, residual,
-    raw, mask_rows, mask, level, solved, changes, potential, solved_rows, weights, wide_rows, panel, near, tmp, space, send_a, came_a, send_b, came_b, send_1, send_2,
+    v_local, dv, tables, raw, mask_rows, mask, level, solved, changes, potential, solved_rows, weights, wide_rows, panel, near, tmp, space, send_a, came_a, send_b, came_b, send_1, send_2,
     came_1, came_2, packed, product, share, shares, far_share, far_shares, source, vec, image, sums, sums_here, all_sums,
-    raw_sem, ring_send, ring_recv, a_sem, b_send, b_recv, s1, r1, s2, r2, c_send, c_recv, m_sem,
+    in_sem, raw_sem, ring_send, ring_recv, a_sem, b_send, b_recv, s1, r1, s2, r2, c_send, c_recv, m_sem,
 ):
     me = lax.axis_index("ga")
     z = lax.axis_index("band")
@@ -447,8 +458,15 @@
     def raw_copy(p):
         return pltpu.make_async_copy(psi.at[:, p], raw.at[p], raw_sem.at[p])
 
-    for p in range(4):
+    def late_copy(n):
+        src, dst = ((far_tables, tables), (far_v, v_local), (far_dv, dv))[n]
+        return pltpu.make_async_copy(src, dst, in_sem.at[n])
+
+    for p in (0, 2, 1, 3):
         raw_copy(p).start()
+    for n in range(3):
+        late_copy(n).start()
+    fwd_hi, fwd_lo, back_hi, back_lo, up_hi, up_lo, down_hi, down_lo = (tables.at[n] for n in range(8))
 
     front = lax.broadcasted_iota(jnp.int32, (4, 2 * BOX), 1) < BOX
     top = lax.broadcasted_iota(jnp.int32, (8, 2 * BOX), 0) < 4
@@ -515,6 +533,8 @@
             rows = mask_rows[i, n : n + 1], mask_rows[2 + i, n : n + 1]
             mask[place_of[f], 8 * i : 8 * i + 8] = spread_rows(*rows)
         solved[place_of[f]] = solved_rows[pl.ds(n, 16, stride=STEP), :] * mask[place_of[f]]
+    for n in range(3):
+        late_copy(n).wait()
     forward_tile(solved, 0, fwd_hi[...], fwd_lo[...], near, tmp, put_pair(send_a, slice(0, 16), F32))
 
     mine = pl.ds(4 * me, 4)
@@ -807,9 +827,12 @@
     return pl.pallas_call(
         kernel,
         out_shape=(shape(natural), shape(natural)),
-        in_specs=[pl.BlockSpec(memory_space=pl.ANY)] + [vmem] * 3 + [smem] * 2 + [vmem] * 10,
+        in_specs=[far] + [vmem] * 3 + [smem] * 2 + [far] * 3,
         out_specs=(vmem, vmem),
         scratch_shapes=[
+            pltpu.VMEM((BOX, 4 * BOX), F32),
+            pltpu.VMEM((NPERT, BOX, 4 * BOX), F32),
+            pltpu.VMEM((8, 4 * BOX, 4 * BOX), BF16),
             pltpu.VMEM((4, 64, BOX, 2 * BOX), BF16),
             pltpu.VMEM((4, BOX, 2 * BOX), F32),
             pltpu.VMEM((KEPT, 16, 2 * BOX), F32),
@@ -835,7 +858,7 @@
             pltpu.VMEM((8, 2 * BOX), F32),
             pltpu.VMEM((8, 2 * BOX), F32),
             pltpu.VMEM((16, 8, 2 * BOX), F32),
-            dma((4,)), dma((12,)), dma((4, 4)), dma((2,)), dma((3,)), dma((3,)),
+            dma((3,)), dma((4,)), dma((12,)), dma((4, 4)), dma((2,)), dma((3,)), dma((3,)),
             dma((2, 3)), dma((2, 3)), dma((2, 3)), dma((2, 3)), dma((4,)), dma((4,)), dma((2,)),
         ],
         compiler_params=pltpu.CompilerParams(
@@ -844,33 +867,50 @@
     )(*args)
 
 
-def place_body(response, residual, *outs):
-    for src, out in zip((response, residual), outs):
-        flat = src.reshape(KEPT * 16, 2 * BOX)
-        for i in range(2):
-            for k in range(2):
-                for q in range(4):
-                    line = flat[pl.ds(8 * i + 4 * k + q, KEPT, stride=16), :]
-                    out[q, 0, 2 * k + i, 0 : GCUT + 1] = line[: GCUT + 1]
-                    out[q, 0, 2 * k + i, GCUT + 1 : BOX - GCUT] = jnp.zeros((BOX - KEPT, 2 * BOX), F32)
-                    out[q, 0, 2 * k + i, BOX - GCUT :] = line[GCUT + 1 :]
+def place_body(response, residual, first, second, buffer, sem):
+    pairs = ((0, response, first), (1, residual, second))
+
+    def leave(w, out, t, q):
+        part = pl.ds(12 * q + 4 * t, 4)
+        return pltpu.make_async_copy(buffer.at[w, part], out.at[part], sem.at[w, t, q])
+
+    for t in range(NPERT):
+        for w, src, out in pairs:
+            flat = src.reshape(KEPT * 48, 2 * BOX)
+            for q in range(4):
+                for p in range(4):
+                    row = 16 * t + 8 * (p % 2) + 4 * (p // 2) + q
+                    to = 12 * q + 4 * t + p
+                    buffer[w, to, 0 : GCUT + 1] = flat[pl.ds(row, GCUT + 1, stride=48), :]
+                    buffer[w, to, GCUT + 1 : BOX - GCUT] = jnp.zeros((BOX - KEPT, 2 * BOX), F32)
+                    buffer[w, to, BOX - GCUT :] = flat[pl.ds(row + 48 * (GCUT + 1), GCUT, stride=48), :]
+                leave(w, out, t, q).start()
+    for t in range(NPERT):
+        for w, _, out in pairs:
+            for q in range(4):
+                leave(w, out, t, q).wait()
 
 
 def place(*values):
-    out = shape((4, NPERT, 4, BOX, 2 * BOX))
-    return pl.pallas_call(
+    out = shape((48, BOX, 2 * BOX))
+    outs = pl.pallas_call(
         place_body,
-        grid=(NPERT,),
         out_shape=(out, out),
-        in_specs=[pl.BlockSpec((KEPT, 16, 2 * BOX), lambda t: (0, t, 0))] * 2,
-        out_specs=(pl.BlockSpec((4, 1, 4, BOX, 2 * BOX), lambda t: (0, t, 0, 0, 0)),) * 2,
+        in_specs=[vmem] * 2,
+        out_specs=(pl.BlockSpec(memory_space=pl.ANY),) * 2,
+        scratch_shapes=[
+            pltpu.VMEM((2, 48, BOX, 2 * BOX), F32),
+            pltpu.SemaphoreType.DMA((2, NPERT, 4)),
+        ],
+        compiler_params=pltpu.CompilerParams(vmem_limit_bytes=16 * 1024 * 1024),
     )(*values)
+    return tuple(v.reshape(4, NPERT, 4, BOX, 2 * BOX) for v in outs)
 
 
 def on_device(psi_occ, energies, k_point, g_mask, v_local, dv):
     response, residual = run(
-        psi_occ, g_mask, v_local, dv, energies, k_point, *lane_tables(),
-        jnp.asarray(fold_table(), BF16), jnp.asarray(spread_table(), BF16),
+        psi_occ, g_mask, jnp.asarray(fold_table(), BF16), jnp.asarray(spread_table(), BF16),
+        energies, k_point, v_local, dv, jnp.stack(lane_tables()),
     )
 
     return place(response, residual)

time: 112 us -> 112 us (level)
  Pallas kernels: 111 us -> 108 us
  local copies, waits for them, and re-layouts: 0 us -> 2.45 us
    unnamed x0 -> x4, local copies, waits for them, and re-layouts: none -> 2.45 us
    pallas_call x1, Pallas kernels: 4.23 us -> 1.88 us  [place(): pl.pallas_call(place_body, out_shape=(out, out), in_specs=[vmem] * 2, out...]
where the time goes in v7:
time: 112 us; the launch traced here: 111 us
  Pallas kernels  108 us (96%)
  local copies, waits for them, and re-layouts  2.45 us (2%)
    pallas_call x1, Pallas kernels, run(): pl.pallas_call(kernel, out_shape=(shape(natural), shape(natural)), in_spe...  106 us
    unnamed x4, local copies, waits for them, and re-layouts  2.45 us

profile of v7, /device:TPU:0, one launch (start us, length us, event | category | flops | bytes accessed | tf_op | source)
XLA Modules:
  0.0 111.3 jit_solution(788131489390819224)
XLA Ops:
  0.6 106.4 %shard_map.131 = (f32[43,48,128]{2,1,0:T(8,128)}, f32[43,48,128]{2,1,0:T(8,128)}) custom-call(bf16[64,4,64,128]{3,2,1,0:T(8,128)(2,1)} %psi.1, s32[4,4096]{1,0:T(4,128)} %g_mask.1, bf16[24,96]{1,0:T(8,128)(2,1)} %constant.12.clone.fold, bf16[384,24]{1,0:T(8,128)(2,1)} %constant.13.clone.spread, f32[4]{0:T(128)} %energies.1, f32[3]{0:T(128)} %k_point.1, ...), custom_call_target="tpu_custom_call" | custom-call | tf_op jit(solution)/shard_map/pallas_call | solution.py:827
  107.0 0.0 copy-start
  107.0 1.2 %copy-done = f32[43,48,128]{2,1,0:T(8,128)S(1)} copy-done((f32[43,48,128]{2,1,0:T(8,128)S(1)}, f32[43,48,128]{2,1,0:T(8,128)}, u32[]{:S(2)}) %copy-start) | copy-done | bytes 1056792
  108.2 0.0 copy-start.1
  108.2 1.2 %copy-done.1 = f32[43,48,128]{2,1,0:T(8,128)S(1)} copy-done((f32[43,48,128]{2,1,0:T(8,128)S(1)}, f32[43,48,128]{2,1,0:T(8,128)}, u32[]{:S(2)}) %copy-start.1) | copy-done | bytes 1056792
  109.5 1.9 %shard_map.132 = (f32[48,64,128]{2,1,0:T(8,128)}, f32[48,64,128]{2,1,0:T(8,128)}) custom-call(f32[43,48,128]{2,1,0:T(8,128)S(1)} %copy-done, f32[43,48,128]{2,1,0:T(8,128)S(1)} %copy-done.1), custom_call_target="tpu_custom_call" | custom-call | tf_op jit(solution)/shard_map/pallas_call | solution.py:896
Async XLA Ops:
  107.0 1.2 %copy-start = (f32[43,48,128]{2,1,0:T(8,128)S(1)}, f32[43,48,128]{2,1,0:T(8,128)}, u32[]{:S(2)}) copy-start(f32[43,48,128]{2,1,0:T(8,128)} %get-tuple-element.6.response) | copy-start | bytes 3170308
  108.2 1.2 %copy-start.1 = (f32[43,48,128]{2,1,0:T(8,128)S(1)}, f32[43,48,128]{2,1,0:T(8,128)}, u32[]{:S(2)}) copy-start(f32[43,48,128]{2,1,0:T(8,128)} %get-tuple-element.7.residual) | copy-start | bytes 3170308

commit v8 on v7

--- a/solution.py
+++ b/solution.py
@@ -867,23 +867,32 @@
     )(*args)
 
 
-def place_body(response, residual, first, second, buffer, sem):
+def place_body(response, residual, first, second, stage, buffer, in_sem, sem):
     pairs = ((0, response, first), (1, residual, second))
+
+    def come(w, src, t):
+        return pltpu.make_async_copy(
+            src.at[:, pl.ds(16 * t, 16)], stage.at[w, t, :, pl.ds(0, 16)], in_sem.at[w, t]
+        )
 
     def leave(w, out, t, q):
         part = pl.ds(12 * q + 4 * t, 4)
         return pltpu.make_async_copy(buffer.at[w, part], out.at[part], sem.at[w, t, q])
 
     for t in range(NPERT):
+        for w, src, _ in pairs:
+            come(w, src, t).start()
+    for t in range(NPERT):
         for w, src, out in pairs:
-            flat = src.reshape(KEPT * 48, 2 * BOX)
+            come(w, src, t).wait()
+            flat = stage.at[w, t].reshape(KEPT * 24, 2 * BOX)
             for q in range(4):
                 for p in range(4):
-                    row = 16 * t + 8 * (p % 2) + 4 * (p // 2) + q
+                    row = 8 * (p % 2) + 4 * (p // 2) + q
                     to = 12 * q + 4 * t + p
-                    buffer[w, to, 0 : GCUT + 1] = flat[pl.ds(row, GCUT + 1, stride=48), :]
+                    buffer[w, to, 0 : GCUT + 1] = flat[pl.ds(row, GCUT + 1, stride=24), :]
                     buffer[w, to, GCUT + 1 : BOX - GCUT] = jnp.zeros((BOX - KEPT, 2 * BOX), F32)
-                    buffer[w, to, BOX - GCUT :] = flat[pl.ds(row + 48 * (GCUT + 1), GCUT, stride=48), :]
+                    buffer[w, to, BOX - GCUT :] = flat[pl.ds(row + 24 * (GCUT + 1), GCUT, stride=24), :]
                 leave(w, out, t, q).start()
     for t in range(NPERT):
         for w, _, out in pairs:
@@ -896,13 +905,15 @@
     outs = pl.pallas_call(
         place_body,
         out_shape=(out, out),
-        in_specs=[vmem] * 2,
+        in_specs=[pl.BlockSpec(memory_space=pl.ANY)] * 2,
         out_specs=(pl.BlockSpec(memory_space=pl.ANY),) * 2,
         scratch_shapes=[
+            pltpu.VMEM((2, NPERT, KEPT, 24, 2 * BOX), F32),
             pltpu.VMEM((2, 48, BOX, 2 * BOX), F32),
+            pltpu.SemaphoreType.DMA((2, NPERT)),
             pltpu.SemaphoreType.DMA((2, NPERT, 4)),
         ],
-        compiler_params=pltpu.CompilerParams(vmem_limit_bytes=16 * 1024 * 1024),
+        compiler_params=pltpu.CompilerParams(vmem_limit_bytes=VMEM_LIMIT),
     )(*values)
     return tuple(v.reshape(4, NPERT, 4, BOX, 2 * BOX) for v in outs)
 

time: 112 us -> 110 us (0.982)
  local copies, waits for them, and re-layouts: 2.45 us -> 0 us
    unnamed x4 -> x0, local copies, waits for them, and re-layouts: 2.45 us -> none
where the time goes in v8:
time: 110 us
  Pallas kernels  109 us (99%)
    pallas_call x1, Pallas kernels, run(): pl.pallas_call(kernel, out_shape=(shape(natural), shape(natural)), in_spe...  106 us
    pallas_call x1, Pallas kernels, place(): pl.pallas_call(place_body, out_shape=(out, out), in_specs=[pl.BlockSpec(m...  2.91 us

profile of v8, /device:TPU:0, one launch (start us, length us, event | category | flops | bytes accessed | tf_op | source)
XLA Modules:
  0.0 109.9 jit_solution(8256405984474709852)
XLA Ops:
  0.6 106.4 %shard_map.131 = (f32[43,48,128]{2,1,0:T(8,128)}, f32[43,48,128]{2,1,0:T(8,128)}) custom-call(bf16[64,4,64,128]{3,2,1,0:T(8,128)(2,1)} %psi.1, s32[4,4096]{1,0:T(4,128)} %g_mask.1, bf16[24,96]{1,0:T(8,128)(2,1)} %constant.12.clone.fold, bf16[384,24]{1,0:T(8,128)(2,1)} %constant.13.clone.spread, f32[4]{0:T(128)} %energies.1, f32[3]{0:T(128)} %k_point.1, ...), custom_call_target="tpu_custom_call" | custom-call | tf_op jit(solution)/shard_map/pallas_call | solution.py:827
  107.0 2.9 %shard_map.132 = (f32[48,64,128]{2,1,0:T(8,128)}, f32[48,64,128]{2,1,0:T(8,128)}) custom-call(f32[43,48,128]{2,1,0:T(8,128)} %get-tuple-element.6.response, f32[43,48,128]{2,1,0:T(8,128)} %get-tuple-element.7.residual), custom_call_target="tpu_custom_call" | custom-call | tf_op jit(solution)/shard_map/pallas_call | solution.py:905

commit v9 on v8

--- a/solution.py
+++ b/solution.py
@@ -262,7 +262,8 @@
 def grid_lanes(ref, high, low, valid=None):
     x = [ref[:, h : h + 8, :].reshape(BOX * 8, 2 * BOX) for h in (0, 8)]
     x = jnp.concatenate(x, axis=1).astype(BF16)
-    out = jnp.dot(x, high, preferred_element_type=F32) + jnp.dot(x, low, preferred_element_type=F32)
+    both = jnp.concatenate([high, low], axis=0)
+    out = jnp.dot(jnp.concatenate([x, x], axis=1), both, preferred_element_type=F32)
     for h, lanes in ((0, slice(0, 2 * BOX)), (8, slice(2 * BOX, 4 * BOX))):
         part = out[:, lanes].reshape(BOX, 8, 2 * BOX)
         ref[:, h : h + 8, :] = part if valid is None else part * valid[0:8]
@@ -382,14 +383,11 @@
 
 def multiply(corr, panel, spread, product, slots, more=False):
     rows = jnp.dot(spread[...], corr, preferred_element_type=F32).astype(BF16)
+    rows = jnp.concatenate([rows[96 * p : 96 * p + 96] for p in range(4)], axis=1)
     sign = -lane_sign((48, 2 * BOX))
     for r in range(0, ROWS, 2):
-        total = None
-        for p in range(4):
-            part = jnp.dot(
-                rows[96 * p : 96 * p + 96], panel_rows(panel, slots, r, p), preferred_element_type=F32
-            )
-            total = part if total is None else total + part
+        bands = jnp.concatenate([panel_rows(panel, slots, r, p) for p in range(4)], axis=0)
+        total = jnp.dot(rows, bands, preferred_element_type=F32)
         for c in range(2):
             lanes = slice(2 * BOX * c, 2 * BOX * (c + 1))
             value = total[:48, lanes] + pltpu.roll(total[48:, lanes], BOX, 1) * sign
@@ -872,7 +870,7 @@
 
     def come(w, src, t):
         return pltpu.make_async_copy(
-            src.at[:, pl.ds(16 * t, 16)], stage.at[w, t, :, pl.ds(0, 16)], in_sem.at[w, t]
+            src.at[:, pl.ds(16 * t, 16)], stage.at[w, t, pl.ds(0, KEPT), pl.ds(0, 16)], in_sem.at[w, t]
         )
 
     def leave(w, out, t, q):
@@ -885,7 +883,7 @@
     for t in range(NPERT):
         for w, src, out in pairs:
             come(w, src, t).wait()
-            flat = stage.at[w, t].reshape(KEPT * 24, 2 * BOX)
+            flat = stage.at[w, t].reshape(48 * 24, 2 * BOX)
             for q in range(4):
                 for p in range(4):
                     row = 8 * (p % 2) + 4 * (p // 2) + q
@@ -908,7 +906,7 @@
         in_specs=[pl.BlockSpec(memory_space=pl.ANY)] * 2,
         out_specs=(pl.BlockSpec(memory_space=pl.ANY),) * 2,
         scratch_shapes=[
-            pltpu.VMEM((2, NPERT, KEPT, 24, 2 * BOX), F32),
+            pltpu.VMEM((2, NPERT, 48, 24, 2 * BOX), F32),
             pltpu.VMEM((2, 48, BOX, 2 * BOX), F32),
             pltpu.SemaphoreType.DMA((2, NPERT)),
             pltpu.SemaphoreType.DMA((2, NPERT, 4)),

time: 110 us -> 110 us (level)
  no operation moved by 1% of the time
where the time goes in v9:
time: 110 us
  Pallas kernels  109 us (99%)
    pallas_call x1, Pallas kernels, run(): pl.pallas_call(kernel, out_shape=(shape(natural), shape(natural)), in_spe...  106 us
    pallas_call x1, Pallas kernels, place(): pl.pallas_call(place_body, out_shape=(out, out), in_specs=[pl.BlockSpec(m...  2.91 us

profile of v9, /device:TPU:0, one launch (start us, length us, event | category | flops | bytes accessed | tf_op | source)
XLA Modules:
  0.0 109.5 jit_solution(7053621542656025108)
XLA Ops:
  0.6 106.0 %shard_map.131 = (f32[43,48,128]{2,1,0:T(8,128)}, f32[43,48,128]{2,1,0:T(8,128)}) custom-call(bf16[64,4,64,128]{3,2,1,0:T(8,128)(2,1)} %psi.1, s32[4,4096]{1,0:T(4,128)} %g_mask.1, bf16[24,96]{1,0:T(8,128)(2,1)} %constant.12.clone.fold, bf16[384,24]{1,0:T(8,128)(2,1)} %constant.13.clone.spread, f32[4]{0:T(128)} %energies.1, f32[3]{0:T(128)} %k_point.1, ...), custom_call_target="tpu_custom_call" | custom-call | tf_op jit(solution)/shard_map/pallas_call | solution.py:825
  106.6 2.9 %shard_map.132 = (f32[48,64,128]{2,1,0:T(8,128)}, f32[48,64,128]{2,1,0:T(8,128)}) custom-call(f32[43,48,128]{2,1,0:T(8,128)} %get-tuple-element.6.response, f32[43,48,128]{2,1,0:T(8,128)} %get-tuple-element.7.residual), custom_call_target="tpu_custom_call" | custom-call | tf_op jit(solution)/shard_map/pallas_call | solution.py:903
